TPU v7x, 128 devices: a whole 4x4x4 slice. The times are simulated.
128 devices in a mesh: freq: 8 (over x, z_hi), space: 16 (over z_lo, y, core).
Axes of the slice: x: 4, y: 4, z: 4 (z_hi: 2, z_lo: 2; z = z_hi * 2 + z_lo), core: 2. Of those that a mesh axis runs over, the one named last changes fastest.
Arguments:
- spectra: bfloat16 [128, 49152, 256], P('freq', 'space'), may hold values from -48 to 48, as said below
- weight: float32 [49152], P('space'), may hold values from 0.25 to 4
- partner: int32 [128], P('freq'), may hold values from 0 to 15
- counts: int32 [128], P('freq'), may hold values from 1 to 8
Outputs:
- modes: bfloat16 [128, 16, 49152], P('freq', None, 'space')
- energy: float32 [128, 8], P('freq')
- coherence: float32 [128, 2, 8, 8], P('freq')
Inputs may be any that keep to these rules, and one draw needn't show every extreme that they name: spectra are finite Fourier coefficients.
All inputs are finite; a program needn't handle non-finite values.
Results may differ from a plain program's by a relative error of at most 0.0045.
Values may be sent and summed in bfloat16 or wider, within the bound.
No kernel may reach another device: no remote copies, remote signals or barrier semaphores. Data moves between devices by JAX's collectives and lax.ppermute only.
A program may use at most 128 MiB of HBM per device.

v0:
```python
import jax
import jax.numpy as jnp
from jax import lax
from jax.sharding import PartitionSpec as P

KMAX = 8
ITERS = 4


def cut_along(array, dim, size):
    shape = array.shape
    parts = array.reshape(*shape[:dim], size, shape[dim] // size, *shape[dim + 1 :])
    return jnp.moveaxis(parts, dim, 0)


def edges_of(length, count):
    unit = 8 if length >= 8 * count else 1
    return [length // unit * k // count * unit for k in range(1, count)]


def laid_out(parts, dim):
    shape = list(parts.shape[1:])
    shape[dim] *= parts.shape[0]
    return jnp.moveaxis(parts, 0, dim).reshape(shape)


def cut_exchange(array, axis, pieces, split_dim, concat_dim):
    parts = cut_along(array, split_dim, lax.axis_size(axis))
    split_at = max(range(1, max(2, parts.ndim - 1)), key=lambda d: parts.shape[d])
    outs = []
    for share in jnp.split(parts, edges_of(parts.shape[split_at], pieces), axis=split_at):
        if share.size:
            outs.append(lax.all_to_all(share, axis, split_axis=0, concat_axis=0, tiled=True))
    return laid_out(jnp.concatenate(outs, axis=split_at), concat_dim)


def copy_for_each(array, axis):
    size = lax.axis_size(axis)
    return lax.all_to_all(
        jnp.broadcast_to(array[None], (size, *array.shape)), axis, 0, 0, tiled=True
    )


def gathered_copies(array, axis, dim):
    return laid_out(copy_for_each(array, axis), dim)


def summed_on_arrival(array, axis, dim):
    size = lax.axis_size(axis)
    parts = lax.all_to_all(cut_along(array, dim, size), axis, 0, 0, tiled=True)
    return jnp.sum(parts.astype(jnp.float32), axis=0)


def taken_together(array, axis):
    return copy_for_each(array, axis).sum(axis=0)


def embed(gram_re, gram_im):
    top = jnp.concatenate([gram_re, -gram_im], axis=2)
    bottom = jnp.concatenate([gram_im, gram_re], axis=2)
    return jnp.concatenate([top, bottom], axis=1)


def apply_operator(operator, basis):
    return jnp.einsum("fkc,fdc->fkd", basis, operator, precision=lax.Precision.HIGHEST)


def orthonormal(vectors, half):
    done = []
    for index in range(vectors.shape[1]):
        vector = vectors[:, index, :]
        for earlier in done:
            early_re, early_im = (earlier[:, :half], earlier[:, half:])
            vec_re, vec_im = (vector[:, :half], vector[:, half:])
            proj_re = jnp.sum(early_re * vec_re + early_im * vec_im, axis=1, keepdims=True)
            proj_im = jnp.sum(early_re * vec_im - early_im * vec_re, axis=1, keepdims=True)
            new_re = vec_re - proj_re * early_re + proj_im * early_im
            new_im = vec_im - proj_re * early_im - proj_im * early_re
            vector = jnp.concatenate([new_re, new_im], axis=1)
        length = jnp.sqrt(jnp.sum(vector * vector, axis=1, keepdims=True) + 1e-06)
        done.append(vector / length)
    return jnp.stack(done, axis=1)


def solve(gram_re, gram_im):
    half = gram_re.shape[1]
    operator = embed(gram_re, gram_im)
    basis = jnp.broadcast_to(
        jnp.eye(KMAX, 2 * half, dtype=jnp.float32), (gram_re.shape[0], KMAX, 2 * half)
    )
    for sweep in range(ITERS):
        basis = orthonormal(apply_operator(operator, basis), half)
    image = apply_operator(operator, basis)
    energy = jnp.sum(basis * image, axis=2)
    return (basis, energy)


def combine(moments, half, total):
    gram_re = (moments[:, :half, :half] + moments[:, half:, half:]) / total
    gram_im = (moments[:, :half, half:] - moments[:, half:, :half]) / total
    return (gram_re, gram_im)


def coefficients(basis, energy, counts):
    half = basis.shape[2] // 2
    ranks = jnp.arange(KMAX, dtype=jnp.int32)[None, :]
    scale = jnp.where(ranks < counts[:, None], 1.0 / jnp.sqrt(energy + 1e-06), 0.0)[:, :, None]
    part_re, part_im = (basis[:, :, :half], basis[:, :, half:])
    upper = jnp.concatenate([part_re, -part_im], axis=2) * scale
    lower = jnp.concatenate([part_im, part_re], axis=2) * scale
    return jnp.concatenate([upper, lower], axis=1).astype(jnp.bfloat16)


def cross_terms(own_modes, other_modes, point_weight, total):
    phi = own_modes.astype(jnp.float32)
    psi = other_modes.astype(jnp.float32)
    wphi = phi * point_weight[None, None, :]
    highest = lax.Precision.HIGHEST

    def inner(left, right):
        return jnp.einsum("fkp,flp->fkl", left, right, precision=highest)

    real_part = inner(wphi[:, :KMAX], psi[:, :KMAX]) + inner(wphi[:, KMAX:], psi[:, KMAX:])
    imag_part = inner(wphi[:, :KMAX], psi[:, KMAX:]) - inner(wphi[:, KMAX:], psi[:, :KMAX])
    return jnp.stack([real_part, imag_part], axis=1) / total


def on_device(spectra, weight, partner, counts):
    groups = spectra.shape[0]
    half = spectra.shape[2] // 2
    total = spectra.shape[1] * lax.axis_size("space")
    weighted = (weight[None, :, None] * spectra).astype(jnp.bfloat16)
    moments = lax.dot_general(
        spectra, weighted, (((1,), (1,)), ((0,), (0,))), preferred_element_type=jnp.float32
    )
    local_re, local_im = combine(moments, half, total)
    gram_re, gram_im = lax.psum((local_re, local_im), "space")
    basis, energy = solve(gram_re, gram_im)
    coefficient = coefficients(basis, energy, counts)
    modes = jnp.einsum(
        "fkc,fpc->fkp", coefficient, spectra, preferred_element_type=jnp.float32
    ).astype(jnp.bfloat16)
    spread = cut_exchange(modes, "freq", 2, 2, 0)
    table = gathered_copies(partner, "freq", 0)
    width = spread.shape[2]
    offset = lax.axis_index("freq") * width
    slice_weight = lax.dynamic_slice_in_dim(weight, offset, width, 0)
    freqs = jnp.arange(spread.shape[0], dtype=jnp.int32)
    source = (lax.axis_size("freq") - 1 - freqs // groups) * groups + table
    chosen = jnp.take(spread, source, axis=0)
    partial_value = cross_terms(spread, chosen, slice_weight, total)
    local = summed_on_arrival(partial_value.astype(jnp.bfloat16), "freq", 0)
    coherence = taken_together(local, "space")
    return (modes, energy, coherence)


def solution(mesh):
    in_specs = (P("freq", "space", None), P("space"), P("freq"), P("freq"))
    out_specs = (P("freq", None, "space"), P("freq", None), P("freq", None, None, None))
    return jax.shard_map(
        on_device, mesh=mesh, in_specs=in_specs, out_specs=out_specs, check_vma=False
    )
```

profile of v0, /device:TPU:1, one launch (start us, length us, event | category | flops | bytes accessed | tf_op | source)
XLA Modules:
  0.0 294.8 jit_solution(10261040301872561448)
XLA Ops:
  7.2 20.6 %fusion.2 = f32[16,256,256]{1,2,0:T(8,128)} fusion(bf16[16,3072,256]{2,1,0:T(8,128)(2,1)} %param.4, f32[3072]{0:T(1024)} %param.5), kind=kOutput, calls=%fused_computation.7 | convolution fusion | flops 6480199680 | bytes 29372416 | tf_op jit(solution)/shard_map/dot_general | solution.py:133
  27.8 4.0 %fusion.17 = (f32[16,128,128]{1,2,0:T(8,128)}, f32[16,128,128]{1,2,0:T(8,128)}) fusion(f32[16,256,256]{1,2,0:T(8,128)} %fusion.2), kind=kLoop, calls=%fused_computation.22 | loop fusion | flops 1048576 | bytes 6291456 | tf_op jit(solution)/shard_map/div | solution.py:100
  31.9 0.6 broadcast_in_dim.18
  32.4 8.2 %all-to-all-start.2 = ((s32[8,1,16]{2,1,0:T(1,128)}), s32[8,1,16]{2,1,0:T(1,128)S(1)}, u32[]{:S(2)}, u32[]{:S(2)}) async-start(s32[8,1,16]{2,1,0:T(1,128)} %broadcast_in_dim.18), calls=%async_computation.2 | async-start | bytes 8192 | tf_op jit(solution)/shard_map/all_to_all | solution.py:39
  40.6 118.2 %all-reduce.3.cloned.1.call-done = (f32[16,128,128]{1,2,0:T(8,128)}, f32[16,128,128]{1,2,0:T(8,128)}) async-done(((f32[16,128,128]{1,2,0:T(8,128)}, f32[16,128,128]{1,2,0:T(8,128)}), (f32[16,128,128]{1,2,0:T(8,128)}, f32[16,128,128]{1,2,0:T(8,128)})) %all-reduce.3.cloned.1.call-update) | async-done | bytes 2097168 | tf_op jit(solution)/shard_map/psum | solution.py:137
  158.8 1.3 neg.6
  160.2 4.1 %fusion.36 = f32[16,8,256]{2,1,0:T(8,128)S(1)} fusion(f32[8,256]{1,0:T(8,128)S(1)} %fusion.70, f32[16,128,128]{1,2,0:T(8,128)} %get-tuple-element.347, f32[16,128,128]{1,2,0:T(8,128)} %get-tuple-element.348, f32[16,128,128]{1,2,0:T(8,128)S(1)} %neg.6), kind=kOutput, calls=%fused_computation.80 | convolution fusion | flops 103809024 | bytes 3284992 | tf_op jit(solution)/shard_map/fkc,fdc->fkd/dot_general | solution.py:65
  165.1 0.3 add_reduce_fusion.96
  165.4 0.3 add_reduce_fusion.95
  165.9 0.3 add_reduce_fusion.89
  166.7 0.3 add_reduce_fusion.88
  167.5 0.3 add_reduce_fusion.87
  167.8 0.3 add_reduce_fusion.86
  168.3 0.2 add_reduce_fusion.85
  169.8 1.9 fusion.34
  172.6 0.3 add_reduce_fusion.68
  172.9 0.3 add_reduce_fusion.67
  173.5 0.3 add_reduce_fusion.61
  174.2 0.3 add_reduce_fusion.60
  175.0 0.3 add_reduce_fusion.59
  175.3 0.3 add_reduce_fusion.58
  175.8 0.2 add_reduce_fusion.57
  177.3 2.0 fusion.32
  180.1 0.3 add_reduce_fusion.40
  180.4 0.3 add_reduce_fusion.39
  181.0 0.3 add_reduce_fusion.33
  181.8 0.3 add_reduce_fusion.32
  182.5 0.3 add_reduce_fusion.31
  182.8 0.3 add_reduce_fusion.30
  183.4 0.2 add_reduce_fusion.29
  184.8 2.2 fusion.30
  187.8 0.3 add_reduce_fusion.12
  188.1 0.3 add_reduce_fusion.11
  188.7 0.3 add_reduce_fusion.5
  189.5 0.3 add_reduce_fusion.4
  190.3 0.3 add_reduce_fusion.3
  190.5 0.3 add_reduce_fusion.2
  192.6 2.0 fusion.28
  194.8 11.5 %convolution_convert_fusion = bf16[16,16,3072]{2,1,0:T(8,128)(2,1)S(1)} fusion(bf16[16,3072,256]{2,1,0:T(8,128)(2,1)} %param.4, bf16[16,16,256]{2,0,1:T(8,128)(2,1)S(1)} %pad_maximum_fusion.1), kind=kOutput, calls=%fused_computation.5 | convolution fusion | flops 403439616 | bytes 26869760 | tf_op jit(solution)/shard_map/fkc,fpc->fkp/dot_general | solution.py:140
  206.6 1.2 fusion.78
  207.8 18.6 %all_to_all.26 = bf16[8,8,16,384]{3,2,1,0:T(8,128)(2,1)S(1)} all-to-all(bf16[8,8,16,384]{3,2,1,0:T(8,128)(2,1)S(1)} %get-tuple-element.519), channel_id=1, replica_groups=mesh['freq'=8,'space'=16] {'freq'}, dimensions={0} | all-to-all | bytes 1572864 | tf_op jit(solution)/shard_map/all_to_all | solution.py:33
  226.4 3.8 %all-to-all-start.1 = ((bf16[8,8,16,384]{3,2,1,0:T(8,128)(2,1)}), bf16[8,8,16,384]{3,2,1,0:T(8,128)(2,1)S(1)}, u32[]{:S(2)}, u32[]{:S(2)}) async-start(bf16[8,8,16,384]{3,2,1,0:T(8,128)(2,1)} %get-tuple-element.520), calls=%async_computation.1 | async-start | bytes 1572864 | tf_op jit(solution)/shard_map/all_to_all | solution.py:33
  230.2 0.8 dynamic_slice.3
  231.1 0.5 broadcast.1034
  231.6 0.7 reduce.5
  232.4 7.7 %all-to-all-done.1 = bf16[8,8,16,384]{3,2,1,0:T(8,128)(2,1)S(1)} async-done(((bf16[8,8,16,384]{3,2,1,0:T(8,128)(2,1)}), bf16[8,8,16,384]{3,2,1,0:T(8,128)(2,1)S(1)}, u32[]{:S(2)}, u32[]{:S(2)}) %all-to-all-start.1) | async-done | bytes 786464 | tf_op jit(solution)/shard_map/all_to_all | solution.py:33
  240.2 1.1 copy-done
  241.4 0.4 convert_multiply_fusion
  241.8 3.3 %gather_fusion = bf16[128,16,384]{2,1,0:T(8,128)(2,1)} fusion(bf16[128,16,384]{2,1,0:T(8,128)(2,1)} %bitcast.180, s32[1024]{0:T(1024)S(1)} %pad_clamp_fusion), kind=kCustom, calls=%fused_computation | custom fusion | bytes 3146240 | tf_op jit(solution)/shard_map/jit(_take)/gather | solution.py:150
  245.1 1.7 broadcast_select_fusion
  246.8 1.6 fusion.5
  248.4 2.8 fusion.3
  251.2 2.4 fusion.11
  253.6 1.2 copy.89
  254.8 4.0 %fusion.14 = f32[128,8,8]{2,1,0:T(8,128)} fusion(f32[128,8,8]{2,1,0:T(8,128)} %fusion.3, f32[128,16,384]{2,1,0:T(8,128)S(1)} %convert_multiply_fusion, bf16[128,16,384]{2,1,0:T(8,128)(2,1)} %copy-done.1), kind=kOutput, calls=%fused_computation.20 | convolution fusion | flops 37756928 | bytes 2916352 | tf_op jit(solution)/shard_map/fkp,flp->fkl/dot_general | solution.py:121
  258.9 1.2 copy.90
  260.2 0.3 reshape.1905
  260.5 12.8 %all_to_all.27 = bf16[8,2,1024]{2,1,0:T(2,128)(2,1)S(1)} all-to-all(bf16[8,2,1024]{2,1,0:T(2,128)(2,1)S(1)} %reshape.1905), channel_id=1, replica_groups=mesh['freq'=8,'space'=16] {'freq'}, dimensions={0} | all-to-all | bytes 65536 | tf_op jit(solution)/shard_map/all_to_all | solution.py:50
  273.7 0.4 reshape.1907
  274.1 11.4 %all_to_all.28 = f32[16,1,2048]{2,1,0:T(1,128)S(1)} all-to-all(f32[16,1,2048]{2,1,0:T(1,128)S(1)} %reshape.1907), channel_id=1, replica_groups=mesh['freq'=8,'space'=16] {'space'}, dimensions={0} | all-to-all | bytes 262144 | tf_op jit(solution)/shard_map/all_to_all | solution.py:39
  285.4 0.5 broadcast.1035
  286.0 0.9 reduce.6
  286.9 0.4 reshape.1908
  287.3 0.7 bitcast_reduce_fusion
  (233 shorter events, 15.7 us)
Async XLA Ops:
  7.2 151.7 %all-reduce.3.cloned.1.call-start = ((), (), s32[]{:S(2)}) async-start(), calls=%async_computation.5 | async-start | bytes 4194304 | tf_op jit(solution)/shard_map/psum | solution.py:137
  27.8 4.0 %copy-start.5 = (s32[16]{0:T(128)S(1)}, s32[16]{0:T(128)}, u32[]{:S(2)}) copy-start(s32[16]{0:T(128)} %param.6) | copy-start | bytes 196
  32.4 175.3 %all-to-all-start.2 = ((s32[8,1,16]{2,1,0:T(1,128)}), s32[8,1,16]{2,1,0:T(1,128)S(1)}, u32[]{:S(2)}, u32[]{:S(2)}) async-start(s32[8,1,16]{2,1,0:T(1,128)} %broadcast_in_dim.18), calls=%async_computation.2 | async-start | bytes 8192 | tf_op jit(solution)/shard_map/all_to_all | solution.py:39
  160.1 9.6 %copy-start.3 = (f32[16,128,128]{1,2,0:T(8,128)S(1)}, f32[16,128,128]{1,2,0:T(8,128)}, u32[]{:S(2)}) copy-start(f32[16,128,128]{1,2,0:T(8,128)} %get-tuple-element.348) | copy-start | bytes 3145732
  160.2 9.7 %copy-start.7 = (f32[16,128,128]{1,2,0:T(8,128)S(1)}, f32[16,128,128]{1,2,0:T(8,128)}, u32[]{:S(2)}) copy-start(f32[16,128,128]{1,2,0:T(8,128)} %get-tuple-element.347) | copy-start | bytes 3145732
  190.8 3.9 %copy-start.6 = (s32[16]{0:T(128)S(1)}, s32[16]{0:T(128)}, u32[]{:S(2)}) copy-start(s32[16]{0:T(128)} %param.7) | copy-start | bytes 196
  194.7 11.7 %copy-start.4 = (f32[16,8]{0,1:T(8,128)}, f32[16,8]{0,1:T(8,128)S(1)}, u32[]{:S(2)}) copy-start(f32[16,8]{0,1:T(8,128)S(1)} %fusion.27) | copy-start | bytes 1540
  206.4 20.0 %copy-start.2 = (bf16[16,16,3072]{2,1,0:T(8,128)(2,1)}, bf16[16,16,3072]{2,1,0:T(8,128)(2,1)S(1)}, u32[]{:S(2)}) copy-start(bf16[16,16,3072]{2,1,0:T(8,128)(2,1)S(1)} %convolution_convert_fusion) | copy-start | bytes 4718596
  226.4 13.7 %all-to-all-start.1 = ((bf16[8,8,16,384]{3,2,1,0:T(8,128)(2,1)}), bf16[8,8,16,384]{3,2,1,0:T(8,128)(2,1)S(1)}, u32[]{:S(2)}, u32[]{:S(2)}) async-start(bf16[8,8,16,384]{3,2,1,0:T(8,128)(2,1)} %get-tuple-element.520), calls=%async_computation.1 | async-start | bytes 1572864 | tf_op jit(solution)/shard_map/all_to_all | solution.py:33
  240.2 1.2 copy-start
  246.8 6.8 %copy-start.1 = (bf16[128,16,384]{2,1,0:T(8,128)(2,1)}, bf16[128,16,384]{2,1,0:T(8,128)(2,1)S(1)}, u32[]{:S(2)}) copy-start(bf16[128,16,384]{2,1,0:T(8,128)(2,1)S(1)} %broadcast_select_fusion) | copy-start | bytes 4718596
Sparse Core Ops, SparseCore 0:
  32.0 126.8 all-reduce.2
where the time goes:
time: 295 us
  waiting for transfers between devices  126 us (43%)
  matrix products  55.1 us (19%)
  blocking collectives  42.8 us (15%)
  other arithmetic  31.6 us (11%)
  between operations  14.7 us (5%)
  local copies, waits for them, and re-layouts  12.8 us (4%)
  starting transfers between devices  12 us (4%)
    psum x1, waiting for transfers between devices, on_device(): gram_re, gram_im = lax.psum((local_re, local_im), 'space')  118 us
    dot_general x1, matrix products, on_device(): lax.dot_general(spectra, weighted, (((1,), (1,)), ((0,), (0,))), preferre...  20.6 us
    all_to_all x1, blocking collectives, cut_exchange(): lax.all_to_all(share, axis, split_axis=0, concat_axis=0, tiled=True)  18.6 us
    all_to_all x1, blocking collectives, summed_on_arrival(): parts = lax.all_to_all(cut_along(array, dim, size), axis, 0, 0, tiled=True)  12.8 us
    dot_general x5, matrix products, apply_operator(): jnp.einsum('fkc,fdc->fkd', basis, operator, precision=lax.Precision.HIGHEST)  12.1 us
    dot_general x1, matrix products, on_device(): jnp.einsum('fkc,fpc->fkp', coefficient, spectra, preferred_element_type=j...  11.5 us
    all_to_all x1, blocking collectives, copy_for_each(): lax.all_to_all(jnp.broadcast_to(array[None], (size, *array.shape)), axis,...  11.4 us
    dot_general x4, matrix products, inner(): return jnp.einsum('fkp,flp->fkl', left, right, precision=highest)  10.8 us
  transfers between devices with their start and end apart: 3, of which 2 were waited for; matrix products, arithmetic and copies ran while one was open for 17% of the time, Pallas kernels for 0%

commit v1 on v0

v1 whole, which is shorter than its diff:
```python
import functools

import jax
import jax.numpy as jnp
from jax import lax
from jax.experimental import pallas as pl
from jax.experimental.pallas import tpu as pltpu
from jax.sharding import PartitionSpec as P

KMAX = 8
ITERS = 4
EPS = 1e-06
F32 = jnp.float32
BF16 = jnp.bfloat16
VMEM = pl.BlockSpec(memory_space=pltpu.VMEM)
SMEM = pl.BlockSpec(memory_space=pltpu.SMEM)
ANY = pl.BlockSpec(memory_space=pl.ANY)


def kernel_params(**more):
    return pltpu.CompilerParams(vmem_limit_bytes=48 * 1024 * 1024, **more)


def cost(flops, moved):
    return pl.CostEstimate(flops=flops, bytes_accessed=moved, transcendentals=0)


def iotas(shape):
    return (
        lax.broadcasted_iota(jnp.int32, shape, 0),
        lax.broadcasted_iota(jnp.int32, shape, 1),
    )


def gram_kernel(slots, per_step, spectra, weight, packed, held, sems):
    groups, points, width = spectra.shape
    half = width // 2
    steps = groups // per_step
    rows, cols = iotas((half, half))

    def fetch(step, slot):
        return pltpu.make_async_copy(
            spectra.at[pl.ds(step * per_step, per_step)], held.at[slot], sems.at[slot]
        )

    for slot in range(slots):
        fetch(slot, slot).start()

    def body(step, carry):
        slot = lax.rem(step, slots)
        fetch(step, slot).wait()
        for index in range(per_step):
            block = held[slot, index]
            weighted = (block.T.astype(F32) * weight[...]).astype(BF16)
            moment = jnp.dot(weighted, block, preferred_element_type=F32)
            real = moment[:half, :half] + moment[half:, half:]
            imag = moment[:half, half:] - moment[half:, :half]
            packed[step * per_step + index] = jnp.where(cols >= rows, real, imag).astype(BF16)

        @pl.when(step + slots < steps)
        def _():
            fetch(step + slots, slot).start()

        return carry

    lax.fori_loop(0, steps, body, 0)


def gram(spectra, weight):
    groups, points, width = spectra.shape
    half = width // 2
    slots, per_step = (4, 2)
    return pl.pallas_call(
        functools.partial(gram_kernel, slots, per_step),
        in_specs=[ANY, VMEM],
        out_specs=VMEM,
        out_shape=jax.ShapeDtypeStruct((groups, half, half), BF16),
        scratch_shapes=[
            pltpu.VMEM((slots, per_step, points, width), BF16),
            pltpu.SemaphoreType.DMA((slots,)),
        ],
        compiler_params=kernel_params(),
        cost_estimate=cost(2 * groups * points * width * width, groups * points * width * 2),
        name="gram",
    )(spectra, weight)


def orthonormal(re, im):
    rows, _ = iotas(re.shape)
    for k in range(KMAX):
        ure = jnp.broadcast_to(re[k : k + 1], re.shape)
        uim = jnp.broadcast_to(im[k : k + 1], im.shape)
        square = jnp.sum(ure * ure + uim * uim, axis=1, keepdims=True) + EPS
        pre = jnp.sum(ure * re + uim * im, axis=1, keepdims=True)
        pim = jnp.sum(ure * im - uim * re, axis=1, keepdims=True)
        inverse = 1.0 / square
        pre = pre * inverse
        pim = pim * inverse
        unit = 1.0 / jnp.sqrt(square)
        re, im = (
            jnp.where(rows > k, re - pre * ure + pim * uim, jnp.where(rows == k, ure * unit, re)),
            jnp.where(rows > k, im - pre * uim - pim * ure, jnp.where(rows == k, uim * unit, im)),
        )
    return (re, im)


def solve_kernel(total, parts, counts, out):
    count, half, _ = parts.shape
    summed = parts[0].astype(F32)
    for index in range(1, count):
        summed = summed + parts[index].astype(F32)
    summed = summed / total
    flipped = summed.T
    rows, cols = iotas((half, half))
    gram_re = jnp.where(cols >= rows, summed, flipped)
    gram_im = jnp.where(cols < rows, summed, jnp.where(cols > rows, -flipped, 0.0))
    operator = jnp.concatenate(
        [
            jnp.concatenate([gram_re, -gram_im], axis=1),
            jnp.concatenate([gram_im, gram_re], axis=1),
        ],
        axis=0,
    )
    high = operator.astype(BF16)
    low = (operator - high.astype(F32)).astype(BF16)

    def apply(re, im):
        vectors = jnp.concatenate([re, im], axis=1)
        vhigh = vectors.astype(BF16)
        vlow = (vectors - vhigh.astype(F32)).astype(BF16)
        both = jnp.concatenate([vhigh, vlow], axis=0)
        first = jnp.dot(both, high, preferred_element_type=F32)
        second = jnp.dot(both, low, preferred_element_type=F32)
        image = first[:KMAX] + first[KMAX:] + second[:KMAX]
        return (image[:, :half], image[:, half:])

    re, im = orthonormal(gram_re[:KMAX], -gram_im[:KMAX])
    for _ in range(ITERS - 1):
        re, im = orthonormal(*apply(re, im))
    image_re, image_im = apply(re, im)
    energy = jnp.sum(re * image_re + im * image_im, axis=1, keepdims=True)
    kept = counts[lax.axis_index("space")]
    ranks, lanes = iotas((KMAX, half))
    scale = jnp.where(ranks[:, :1] < kept, 1.0 / jnp.sqrt(energy + EPS), 0.0)
    first = energy.astype(BF16)
    rest = energy - first.astype(F32)
    second = rest.astype(BF16)
    third = (rest - second.astype(F32)).astype(BF16)
    tail = jnp.where(
        lanes == 0,
        first.astype(F32),
        jnp.where(lanes == 1, second.astype(F32), jnp.where(lanes == 2, third.astype(F32), 0.0)),
    )
    message = jnp.concatenate([re * scale, im * scale, tail], axis=1).astype(BF16)
    for index in range(out.shape[0]):
        out[index] = message


def solve(parts, counts, total):
    count, half, _ = parts.shape
    return pl.pallas_call(
        functools.partial(solve_kernel, total),
        in_specs=[VMEM, SMEM],
        out_specs=VMEM,
        out_shape=jax.ShapeDtypeStruct((count, KMAX, 3 * half), BF16),
        compiler_params=kernel_params(),
        cost_estimate=cost(8_000_000_000, parts.size * 2),
        name="solve",
    )(parts, counts)


def coefficient_rows(message, half):
    part_re = message[:, :half]
    part_im = message[:, half : 2 * half]
    return jnp.concatenate(
        [
            jnp.concatenate([part_re, -part_im], axis=1),
            jnp.concatenate([part_im, part_re], axis=1),
        ],
        axis=0,
    )


def project(rows, block):
    return lax.dot_general(
        rows, block, (((1,), (1,)), ((), ())), preferred_element_type=F32
    ).astype(BF16)


def part_kernel(begin, size, half_index, messages, spectra, out, held, sems):
    groups, points, width = spectra.shape
    start = pl.multiple_of(half_index[0] * (points // 2) + begin, 128)
    copies = [
        pltpu.make_async_copy(
            spectra.at[index, pl.ds(start, size)], held.at[index], sems.at[index]
        )
        for index in range(groups)
    ]
    for copy in copies:
        copy.start()
    for index in range(groups):
        copies[index].wait()
        out[index] = project(coefficient_rows(messages[index], width // 2), held[index])


def modes_part(half_index, messages, spectra, begin, size):
    groups, points, width = spectra.shape
    return pl.pallas_call(
        functools.partial(part_kernel, begin, size),
        in_specs=[SMEM, VMEM, ANY],
        out_specs=VMEM,
        out_shape=jax.ShapeDtypeStruct((groups, 2 * KMAX, size), BF16),
        scratch_shapes=[
            pltpu.VMEM((groups, size, width), BF16),
            pltpu.SemaphoreType.DMA((groups,)),
        ],
        compiler_params=kernel_params(),
        cost_estimate=cost(2_000_000_000, groups * size * width * 2),
        name="modes_part",
    )(half_index, messages, spectra)


def modes_kernel(slots, keep, messages, weight, spectra, out, high, low, held, made, sems, put):
    groups, points, width = spectra.shape
    part = points // 2
    start = pl.multiple_of(keep[0] * part, 128)

    def fetch(step, slot):
        return pltpu.make_async_copy(spectra.at[step], held.at[slot], sems.at[slot])

    def store(step, slot):
        return pltpu.make_async_copy(made.at[slot], out.at[step], put.at[slot])

    for slot in range(slots):
        fetch(slot, slot).start()

    def body(step, carry):
        slot = lax.rem(step, slots)

        @pl.when(step >= slots)
        def _():
            store(step - slots, slot).wait()

        fetch(step, slot).wait()
        made[slot] = project(coefficient_rows(messages[step], width // 2), held[slot])
        store(step, slot).start()
        own = made[slot, :, pl.ds(start, part)].astype(F32) * weight[:, pl.ds(start, part)]
        top = own.astype(BF16)
        high[step] = top
        low[step] = (own - top.astype(F32)).astype(BF16)

        @pl.when(step + slots < groups)
        def _():
            fetch(step + slots, slot).start()

        return carry

    lax.fori_loop(0, groups, body, 0)
    for slot in range(slots):
        store(groups - slots + slot, slot).wait()


def modes_all(keep, messages, weight, spectra):
    groups, points, width = spectra.shape
    slots = 4
    weighted = jax.ShapeDtypeStruct((groups, 2 * KMAX, points // 2), BF16)
    return pl.pallas_call(
        functools.partial(modes_kernel, slots),
        in_specs=[SMEM, VMEM, VMEM, ANY],
        out_specs=(ANY, VMEM, VMEM),
        out_shape=(
            jax.ShapeDtypeStruct((groups, 2 * KMAX, points), BF16),
            weighted,
            weighted,
        ),
        scratch_shapes=[
            pltpu.VMEM((slots, points, width), BF16),
            pltpu.VMEM((slots, 2 * KMAX, points), BF16),
            pltpu.SemaphoreType.DMA((slots,)),
            pltpu.SemaphoreType.DMA((slots,)),
        ],
        compiler_params=kernel_params(),
        cost_estimate=cost(10_000_000_000, groups * points * width * 2),
        name="modes_all",
    )(keep, messages, weight, spectra)


def chosen(cross, lane_partner, groups):
    rank = 2 * KMAX
    top = jnp.zeros((KMAX, groups * rank), F32)
    bottom = jnp.zeros((KMAX, groups * rank), F32)
    for index in range(groups):
        taken = lane_partner == index
        top = jnp.where(taken, cross[index * rank : index * rank + KMAX], top)
        bottom = jnp.where(taken, cross[index * rank + KMAX : (index + 1) * rank], bottom)
    _, lanes = iotas(top.shape)
    width = groups * rank
    return jnp.where(
        lanes % rank < KMAX,
        top + pltpu.roll(bottom, width - KMAX, 1),
        pltpu.roll(bottom, KMAX, 1) - top,
    )


def cross_kernel(first_mine, own_partner, other_partner, high, low, *rest):
    arrived, out = (rest[:-1], rest[-1])
    groups, rank, part = high.shape
    rows = groups * rank
    cross = jnp.zeros((rows, rows), F32)
    begin = 0
    for share in arrived:
        size = share.shape[2]
        other = share[...].reshape(rows, size)
        for own in (high, low):
            mine = own[:, :, begin : begin + size].reshape(rows, size)
            cross = cross + lax.dot_general(
                mine, other, (((1,), (1,)), ((), ())), preferred_element_type=F32
            )
        begin += size
    own_value = chosen(cross.T, own_partner[...], groups).astype(BF16)
    other_value = chosen(cross, other_partner[...], groups).astype(BF16)
    mine_first = first_mine[0] == 1
    half = out.shape[0] // 2
    lower = jnp.where(mine_first, own_value, other_value)
    upper = jnp.where(mine_first, other_value, own_value)
    for index in range(half):
        out[index] = lower
        out[half + index] = upper


def cross_sums(first_mine, own_partner, other_partner, high, low, arrived, members):
    groups, rank, part = high.shape
    return pl.pallas_call(
        cross_kernel,
        in_specs=[SMEM] + [VMEM] * (4 + len(arrived)),
        out_specs=VMEM,
        out_shape=jax.ShapeDtypeStruct((members, KMAX, groups * rank), BF16),
        compiler_params=kernel_params(),
        cost_estimate=cost(2_000_000_000, 4 * high.size),
        name="cross_sums",
    )(first_mine, own_partner, other_partner, high, low, *arrived)


def finish_kernel(total, parts, out):
    summed = parts[0].astype(F32)
    for index in range(1, parts.shape[0]):
        summed = summed + parts[index].astype(F32)
    out[...] = (summed / total).T


def finish(parts, total):
    _, kmax, width = parts.shape
    return pl.pallas_call(
        functools.partial(finish_kernel, total),
        in_specs=[VMEM],
        out_specs=VMEM,
        out_shape=jax.ShapeDtypeStruct((width, kmax), F32),
        compiler_params=kernel_params(),
        cost_estimate=cost(1_000_000, parts.size * 2),
        name="finish",
    )(parts)


def on_device(spectra, weight, partner, counts):
    groups, points, width = spectra.shape
    n_freq, n_space = (lax.axis_size("freq"), lax.axis_size("space"))
    total = points * n_space
    place = lax.axis_index("freq")
    lower_group = place < n_freq // 2
    keep = jnp.where(lower_group, 0, 1).astype(jnp.int32).reshape(1)
    give = 1 - keep
    weight_row = weight[None, :]
    lane_partner = jnp.repeat(partner, 2 * KMAX)[None, :]
    mirror = [(index, n_freq - 1 - index) for index in range(n_freq)]

    packed = gram(spectra, weight_row)
    parts = lax.all_to_all(packed, "space", 0, 0, tiled=True)
    message = solve(parts, counts, total)
    messages = lax.all_to_all(message, "space", 0, 0, tiled=True)

    pieces = 2
    size = points // 2 // pieces
    shares = [
        modes_part(give, messages, spectra, index * size, size) for index in range(pieces)
    ]
    arrived = [lax.ppermute(share, "freq", mirror) for share in shares]
    other_partner = lax.ppermute(lane_partner, "freq", mirror)
    modes, high, low = modes_all(keep, messages, weight_row, spectra)
    energy = jnp.sum(messages[:, :, width : width + 3].astype(F32), axis=2)

    pairs = [
        [group * n_space + index for group in (low_group, n_freq - 1 - low_group) for index in range(n_space)]
        for low_group in range(n_freq // 2)
    ]
    sums = cross_sums(
        give, lane_partner, other_partner, high, low, arrived, 2 * n_space
    )
    gathered = lax.all_to_all(
        sums, ("freq", "space"), 0, 0, tiled=True, axis_index_groups=pairs
    )
    coherence = finish(gathered, total).reshape(groups, 2, KMAX, KMAX)
    return (modes, energy, coherence)


def solution(mesh):
    in_specs = (P("freq", "space", None), P("space"), P("freq"), P("freq"))
    out_specs = (P("freq", None, "space"), P("freq", None), P("freq", None, None, None))
    return jax.shard_map(
        on_device, mesh=mesh, in_specs=in_specs, out_specs=out_specs, check_vma=False
    )
```

time: 295 us -> 92.9 us (0.31)
  waiting for transfers between devices: 126 us -> 11.7 us
  matrix products: 55.1 us -> 0 us
  Pallas kernels: 0 us -> 37.9 us
  other arithmetic: 31.6 us -> 0.09 us
  blocking collectives: 42.8 us -> 16.6 us
  between operations: 14.7 us -> 0.73 us
  starting transfers between devices: 12 us -> 23.2 us
  local copies, waits for them, and re-layouts: 12.8 us -> 2.28 us
    psum x1 -> x0, waiting for transfers between devices: 118 us -> none  [on_device(): gram_re, gram_im = lax.psum((local_re, local_im), 'space')]
    dot_general x11 -> x0, matrix products: 55.1 us -> none  [the longest x1 20.6 us: on_device(): lax.dot_general(spectra, weighted, (((1,), (1,)), ((0,), (0,))), preferre...]
    pallas_call x0 -> x7, Pallas kernels: none -> 37.9 us  [the longest x1 10.9 us: modes_all(): pl.pallas_call(functools.partial(modes_kernel, slots), in_specs=[SMEM, VM...]
    all_to_all x3 -> x1, blocking collectives: 42.8 us -> 16.6 us  [on_device(): parts = lax.all_to_all(packed, 'space', 0, 0, tiled=True)]
    reduce_sum x79 -> x1, other arithmetic: 15.2 us -> 0.09 us  [on_device(): energy = jnp.sum(messages[:, :, width:width + 3].astype(F32), axis=2)]
    ppermute x0 -> x3, starting transfers between devices: none -> 11.2 us  [the longest x2 5.67 us: on_device(): arrived = [lax.ppermute(share, 'freq', mirror) for share in shares]]
    div x29 -> x0, other arithmetic: 6.17 us -> none  [the longest x1 3.99 us: combine(): gram_im = (moments[:, :half, half:] - moments[:, half:, :half]) / total]
    gather x1 -> x0, local copies, waits for them, and re-layouts: 3.34 us -> none  [on_device(): chosen = jnp.take(spread, source, axis=0)]
  transfers between devices with their start and end apart: 3 -> 5, of which waited for: 2 -> 3; matrix products, arithmetic and copies ran while one was open for 17% -> 1% of each run, Pallas kernels for 0% -> 23%
where the time goes in v1:
time: 92.9 us; the launch traced here: 92.6 us
  Pallas kernels  37.9 us (41%)
  starting transfers between devices  23.2 us (25%)
  blocking collectives  16.6 us (18%)
  waiting for transfers between devices  11.7 us (13%)
  local copies, waits for them, and re-layouts  2.28 us (2%)
    all_to_all x1, blocking collectives, on_device(): parts = lax.all_to_all(packed, 'space', 0, 0, tiled=True)  16.6 us
    pallas_call x1, Pallas kernels, modes_all(): pl.pallas_call(functools.partial(modes_kernel, slots), in_specs=[SMEM, VM...  10.9 us
    pallas_call x2, Pallas kernels, modes_part(): pl.pallas_call(functools.partial(part_kernel, begin, size), in_specs=[SME...  10.4 us
    pallas_call x1, Pallas kernels, gram(): pl.pallas_call(functools.partial(gram_kernel, slots, per_step), in_specs=...  10.2 us
    all_to_all x1, waiting for transfers between devices, on_device(): lax.all_to_all(sums, ('freq', 'space'), 0, 0, tiled=True, axis_index_grou...  8.98 us
    all_to_all x1, starting transfers between devices, on_device(): lax.all_to_all(sums, ('freq', 'space'), 0, 0, tiled=True, axis_index_grou...  7.29 us
    ppermute x2, starting transfers between devices, on_device(): arrived = [lax.ppermute(share, 'freq', mirror) for share in shares]  5.67 us
    ppermute x1, starting transfers between devices, on_device(): other_partner = lax.ppermute(lane_partner, 'freq', mirror)  5.51 us
  transfers between devices with their start and end apart: 5, of which 3 were waited for; matrix products, arithmetic and copies ran while one was open for 1% of the time, Pallas kernels for 23%

profile of v1, /device:TPU:1, one launch (start us, length us, event | category | flops | bytes accessed | tf_op | source)
XLA Modules:
  0.0 92.6 jit_solution(7781445728497097151)
XLA Ops:
  0.6 0.0 copy-start.2
  0.6 0.0 copy-start
  0.7 0.7 copy-done
  1.4 0.0 copy-start.3
  1.4 10.2 %gram.1 = bf16[16,128,128]{2,1,0:T(8,128)(2,1)S(1)} custom-call(bf16[16,3072,256]{2,1,0:T(8,128)(2,1)} %spectra.7, f32[1,3072]{1,0:T(1,128)S(1)} %bitcast.4), custom_call_target="tpu_custom_call" | custom-call | flops 6442450944 | bytes 25165824 | tf_op jit(solution)/shard_map/gram/pallas_call | solution.py:73
  11.5 16.6 %all_to_all.15.parts = bf16[16,128,128]{2,1,0:T(8,128)(2,1)S(1)} all-to-all(bf16[16,128,128]{2,1,0:T(8,128)(2,1)S(1)} %gram.1), channel_id=1, replica_groups=mesh['freq'=8,'space'=16] {'space'}, dimensions={0} | all-to-all | bytes 1048576 | tf_op jit(solution)/shard_map/all_to_all | solution.py:377
  28.1 0.0 copy-done.2
  28.1 4.9 %solve.1 = bf16[16,8,384]{2,1,0:T(8,128)(2,1)} custom-call(bf16[16,128,128]{2,1,0:T(8,128)(2,1)S(1)} %all_to_all.15.parts, s32[16]{0:T(128)S(1)} %copy-done.2), custom_call_target="tpu_custom_call" | custom-call | flops 8000000000 | bytes 524288 | tf_op jit(solution)/shard_map/solve/pallas_call | solution.py:161
  33.1 4.7 %all-to-all-start.1 = ((bf16[16,8,384]{2,1,0:T(8,128)(2,1)}), bf16[16,8,384]{2,1,0:T(8,128)(2,1)S(1)}, u32[]{:S(2)}, u32[]{:S(2)}) async-start(bf16[16,8,384]{2,1,0:T(8,128)(2,1)} %solve.1), calls=%async_computation.1 | async-start | bytes 196608 | tf_op jit(solution)/shard_map/all_to_all | solution.py:379
  37.8 0.0 copy-done.3
  37.8 0.1 broadcast_in_dim.7
  37.9 0.1 broadcast_in_dim_reshape.3.own_partner
  37.9 5.5 %collective-permute-start = (s32[1,256]{1,0:T(1,128)S(1)}, s32[1,256]{1,0:T(1,128)S(1)}, u32[]{:S(2)}, u32[]{:S(2)}) collective-permute-start(s32[1,256]{1,0:T(1,128)S(1)} %broadcast_in_dim_reshape.3.own_partner), channel_id=1, source_target_pairs={{0,112},{16,96},{32,80},{48,64},{64,48},{80,32},{96,16},{112,0},{1... | collective-permute-start | bytes 3080 | tf_op jit(solution)/shard_map/ppermute | solution.py:387
  43.5 0.0 copy-start.1
  43.5 0.2 all-to-all-done.1.messages
  43.7 5.2 %modes_part.2 = bf16[16,16,768]{2,1,0:T(8,128)(2,1)S(1)} custom-call(s32[1]{0:T(128)S(6)} %sub.3.half_index.first_mine, bf16[16,8,384]{2,1,0:T(8,128)(2,1)S(1)} %all-to-all-done.1.messages, bf16[16,3072,256]{2,1,0:T(8,128)(2,1)} %spectra.7), custom_call_target="tpu_custom_call" | custom-call | flops 2000000000 | bytes 6291456 | tf_op jit(solution)/shard_map/modes_part/pallas_call | solution.py:208
  48.9 5.6 %collective-permute-start.1 = (bf16[16,16,768]{2,1,0:T(8,128)(2,1)S(1)}, bf16[16,16,768]{2,1,0:T(8,128)(2,1)S(1)}, u32[]{:S(2)}, u32[]{:S(2)}) collective-permute-start(bf16[16,16,768]{2,1,0:T(8,128)(2,1)S(1)} %modes_part.2), channel_id=1, source_target_pairs={{0,112},{16,96},{32,80},{48,64},{64,48},{80,32},{96,16},{112,0},{1... | collective-permute-start | bytes 1179656 | tf_op jit(solution)/shard_map/ppermute | solution.py:386
  54.5 5.2 %modes_part.3 = bf16[16,16,768]{2,1,0:T(8,128)(2,1)S(1)} custom-call(s32[1]{0:T(128)S(6)} %sub.3.half_index.first_mine, bf16[16,8,384]{2,1,0:T(8,128)(2,1)S(1)} %all-to-all-done.1.messages, bf16[16,3072,256]{2,1,0:T(8,128)(2,1)} %spectra.7), custom_call_target="tpu_custom_call" | custom-call | flops 2000000000 | bytes 6291456 | tf_op jit(solution)/shard_map/modes_part/pallas_call | solution.py:208
  59.7 0.1 collective-permute-start.2
  59.8 0.0 copy-done.1
  59.8 10.9 %modes_all.1 = (bf16[16,16,3072]{2,1,0:T(8,128)(2,1)}, bf16[16,16,1536]{2,1,0:T(8,128)(2,1)S(1)}, bf16[16,16,1536]{2,1,0:T(8,128)(2,1)S(1)}) custom-call(s32[1]{0:T(128)} %bitcast.keep, bf16[16,8,384]{2,1,0:T(8,128)(2,1)S(1)} %all-to-all-done.1.messages, f32[1,3072]{1,0:T(1,128)S(1)} %bitcast.5, bf16[16,3072,256]{2,1,0:T(8,128)(2,1)} %spectra.7), custom_call_target="tpu_custom_call" | custom-call | flops 10000000000 | bytes 25165824 | tf_op jit(solution)/shard_map/modes_all/pallas_call | solution.py:267
  70.6 0.0 collective-permute-done.other_partner
  70.7 0.0 collective-permute-done.1.rest_0_
  70.7 2.5 %collective-permute-done.2.rest_1_ = bf16[16,16,768]{2,1,0:T(8,128)(2,1)S(1)} collective-permute-done((bf16[16,16,768]{2,1,0:T(8,128)(2,1)S(1)}, bf16[16,16,768]{2,1,0:T(8,128)(2,1)S(1)}, u32[]{:S(2)}, u32[]{:S(2)}) %collective-permute-start.2) | collective-permute-done | bytes 393248 | tf_op jit(solution)/shard_map/ppermute | solution.py:386
  73.2 1.5 %cross_sums.1 = bf16[32,8,256]{2,1,0:T(8,128)(2,1)} custom-call(s32[1]{0:T(128)S(6)} %sub.3.half_index.first_mine, s32[1,256]{1,0:T(1,128)S(1)} %broadcast_in_dim_reshape.3.own_partner, s32[1,256]{1,0:T(1,128)S(1)} %collective-permute-done.other_partner, bf16[16,16,1536]{2,1,0:T(8,128)(2,1)S(1)} %get-tuple-element.7.high, ...), custom_call_target="tpu_custom_call" | custom-call | flops 2000000000 | bytes 1572864 | tf_op jit(solution)/shard_map/cross_sums/pallas_call | solution.py:333
  74.6 7.3 %all-to-all-start.2 = ((bf16[32,8,256]{2,1,0:T(8,128)(2,1)}), bf16[32,8,256]{2,1,0:T(8,128)(2,1)S(1)}, u32[]{:S(2)}, u32[]{:S(2)}) async-start(bf16[32,8,256]{2,1,0:T(8,128)(2,1)} %cross_sums.1), calls=%async_computation.2 | async-start | bytes 262144 | tf_op jit(solution)/shard_map/all_to_all | solution.py:398
  81.9 0.1 convert_reduce_fusion
  82.0 0.7 copy.8
  82.7 9.0 %all-to-all-done.2.parts = bf16[32,8,256]{2,1,0:T(8,128)(2,1)S(1)} async-done(((bf16[32,8,256]{2,1,0:T(8,128)(2,1)}), bf16[32,8,256]{2,1,0:T(8,128)(2,1)S(1)}, u32[]{:S(2)}, u32[]{:S(2)}) %all-to-all-start.2) | async-done | bytes 131104 | tf_op jit(solution)/shard_map/all_to_all | solution.py:398
  91.7 0.2 finish.1
  91.8 0.8 copy.9
Async XLA Ops:
  0.6 27.5 %copy-start.2 = (s32[16]{0:T(128)S(1)}, s32[16]{0:T(128)}, u32[]{:S(2)}) copy-start(s32[16]{0:T(128)} %counts.1) | copy-start | bytes 196
  0.6 0.7 copy-start
  1.4 36.4 %copy-start.3 = (s32[16]{0:T(128)S(1)}, s32[16]{0:T(128)}, u32[]{:S(2)}) copy-start(s32[16]{0:T(128)} %param.6) | copy-start | bytes 196
  33.1 10.6 %all-to-all-start.1 = ((bf16[16,8,384]{2,1,0:T(8,128)(2,1)}), bf16[16,8,384]{2,1,0:T(8,128)(2,1)S(1)}, u32[]{:S(2)}, u32[]{:S(2)}) async-start(bf16[16,8,384]{2,1,0:T(8,128)(2,1)} %solve.1), calls=%async_computation.1 | async-start | bytes 196608 | tf_op jit(solution)/shard_map/all_to_all | solution.py:379
  37.9 32.7 %collective-permute-start = (s32[1,256]{1,0:T(1,128)S(1)}, s32[1,256]{1,0:T(1,128)S(1)}, u32[]{:S(2)}, u32[]{:S(2)}) collective-permute-start(s32[1,256]{1,0:T(1,128)S(1)} %broadcast_in_dim_reshape.3.own_partner), channel_id=1, source_target_pairs={{0,112},{16,96},{32,80},{48,64},{64,48},{80,32},{96,16},{112,0},{1... | collective-permute-start | bytes 3080 | tf_op jit(solution)/shard_map/ppermute | solution.py:387
  43.5 16.3 %copy-start.1 = (f32[3072]{0:T(1024)S(1)}, f32[3072]{0:T(1024)}, u32[]{:S(2)}) copy-start(f32[3072]{0:T(1024)} %param.5) | copy-start | bytes 36868
  48.9 21.8 %collective-permute-start.1 = (bf16[16,16,768]{2,1,0:T(8,128)(2,1)S(1)}, bf16[16,16,768]{2,1,0:T(8,128)(2,1)S(1)}, u32[]{:S(2)}, u32[]{:S(2)}) collective-permute-start(bf16[16,16,768]{2,1,0:T(8,128)(2,1)S(1)} %modes_part.2), channel_id=1, source_target_pairs={{0,112},{16,96},{32,80},{48,64},{64,48},{80,32},{96,16},{112,0},{1... | collective-permute-start | bytes 1179656 | tf_op jit(solution)/shard_map/ppermute | solution.py:386
  59.7 13.5 %collective-permute-start.2 = (bf16[16,16,768]{2,1,0:T(8,128)(2,1)S(1)}, bf16[16,16,768]{2,1,0:T(8,128)(2,1)S(1)}, u32[]{:S(2)}, u32[]{:S(2)}) collective-permute-start(bf16[16,16,768]{2,1,0:T(8,128)(2,1)S(1)} %modes_part.3), channel_id=1, source_target_pairs={{0,112},{16,96},{32,80},{48,64},{64,48},{80,32},{96,16},{112,0},{1... | collective-permute-start | bytes 1179656 | tf_op jit(solution)/shard_map/ppermute | solution.py:386
  74.6 17.0 %all-to-all-start.2 = ((bf16[32,8,256]{2,1,0:T(8,128)(2,1)}), bf16[32,8,256]{2,1,0:T(8,128)(2,1)S(1)}, u32[]{:S(2)}, u32[]{:S(2)}) async-start(bf16[32,8,256]{2,1,0:T(8,128)(2,1)} %cross_sums.1), calls=%async_computation.2 | async-start | bytes 262144 | tf_op jit(solution)/shard_map/all_to_all | solution.py:398

commit v2 on v1

--- a/solution.py
+++ b/solution.py
@@ -15,14 +15,19 @@
 VMEM = pl.BlockSpec(memory_space=pltpu.VMEM)
 SMEM = pl.BlockSpec(memory_space=pltpu.SMEM)
 ANY = pl.BlockSpec(memory_space=pl.ANY)
-
-
-def kernel_params(**more):
-    return pltpu.CompilerParams(vmem_limit_bytes=48 * 1024 * 1024, **more)
+HBM = pl.BlockSpec(memory_space=pltpu.HBM)
+
+
+def kernel_params(mebibytes):
+    return pltpu.CompilerParams(vmem_limit_bytes=mebibytes * 1024 * 1024)
 
 
 def cost(flops, moved):
     return pl.CostEstimate(flops=flops, bytes_accessed=moved, transcendentals=0)
+
+
+def kept_half():
+    return jnp.where(lax.axis_index("freq") < lax.axis_size("freq") // 2, 0, 1)
 
 
 def iotas(shape):
@@ -32,35 +37,40 @@
     )
 
 
-def gram_kernel(slots, per_step, spectra, weight, packed, held, sems):
+def gram_kernel(depth, spectra, weight, packed, held, scale, sems, scale_sem):
     groups, points, width = spectra.shape
     half = width // 2
+    slots, per_step = held.shape[:2]
     steps = groups // per_step
     rows, cols = iotas((half, half))
 
-    def fetch(step, slot):
+    def fetch(step):
+        slot = lax.rem(step, slots)
         return pltpu.make_async_copy(
             spectra.at[pl.ds(step * per_step, per_step)], held.at[slot], sems.at[slot]
         )
 
-    for slot in range(slots):
-        fetch(slot, slot).start()
+    fetch(0).start()
+    scale_copy = pltpu.make_async_copy(weight, scale, scale_sem)
+    scale_copy.start()
+    for step in range(1, depth):
+        fetch(step).start()
+    scale_copy.wait()
 
     def body(step, carry):
-        slot = lax.rem(step, slots)
-        fetch(step, slot).wait()
+        fetch(step).wait()
+
+        @pl.when(step + depth < steps)
+        def _():
+            fetch(step + depth).start()
+
         for index in range(per_step):
-            block = held[slot, index]
-            weighted = (block.T.astype(F32) * weight[...]).astype(BF16)
+            block = held[lax.rem(step, slots), index]
+            weighted = (block.T.astype(F32) * scale[...]).astype(BF16)
             moment = jnp.dot(weighted, block, preferred_element_type=F32)
             real = moment[:half, :half] + moment[half:, half:]
             imag = moment[:half, half:] - moment[half:, :half]
             packed[step * per_step + index] = jnp.where(cols >= rows, real, imag).astype(BF16)
-
-        @pl.when(step + slots < steps)
-        def _():
-            fetch(step + slots, slot).start()
-
         return carry
 
     lax.fori_loop(0, steps, body, 0)
@@ -69,17 +79,19 @@
 def gram(spectra, weight):
     groups, points, width = spectra.shape
     half = width // 2
-    slots, per_step = (4, 2)
-    return pl.pallas_call(
-        functools.partial(gram_kernel, slots, per_step),
-        in_specs=[ANY, VMEM],
+    depth, slots, per_step = (2, 3, 2)
+    return pl.pallas_call(
+        functools.partial(gram_kernel, depth),
+        in_specs=[HBM, ANY],
         out_specs=VMEM,
         out_shape=jax.ShapeDtypeStruct((groups, half, half), BF16),
         scratch_shapes=[
             pltpu.VMEM((slots, per_step, points, width), BF16),
+            pltpu.VMEM((1, points), F32),
             pltpu.SemaphoreType.DMA((slots,)),
+            pltpu.SemaphoreType.DMA,
         ],
-        compiler_params=kernel_params(),
+        compiler_params=kernel_params(24),
         cost_estimate=cost(2 * groups * points * width * width, groups * points * width * 2),
         name="gram",
     )(spectra, weight)
@@ -104,8 +116,18 @@
     return (re, im)
 
 
-def solve_kernel(total, parts, counts, out):
+def solve_kernel(total, parts, counts, spectra, out, staged, sems):
     count, half, _ = parts.shape
+    groups, part, _ = staged.shape
+    start = pl.multiple_of((1 - kept_half()) * part, 128)
+    copies = [
+        pltpu.make_async_copy(
+            spectra.at[index, pl.ds(start, part)], staged.at[index], sems.at[index]
+        )
+        for index in range(groups)
+    ]
+    for copy in copies:
+        copy.start()
     summed = parts[0].astype(F32)
     for index in range(1, count):
         summed = summed + parts[index].astype(F32)
@@ -154,19 +176,26 @@
     message = jnp.concatenate([re * scale, im * scale, tail], axis=1).astype(BF16)
     for index in range(out.shape[0]):
         out[index] = message
-
-
-def solve(parts, counts, total):
+    for copy in copies:
+        copy.wait()
+
+
+def solve(parts, counts, spectra, total):
     count, half, _ = parts.shape
+    groups, points, width = spectra.shape
     return pl.pallas_call(
         functools.partial(solve_kernel, total),
-        in_specs=[VMEM, SMEM],
-        out_specs=VMEM,
-        out_shape=jax.ShapeDtypeStruct((count, KMAX, 3 * half), BF16),
-        compiler_params=kernel_params(),
-        cost_estimate=cost(8_000_000_000, parts.size * 2),
+        in_specs=[VMEM, SMEM, HBM],
+        out_specs=(VMEM, VMEM),
+        out_shape=(
+            jax.ShapeDtypeStruct((count, KMAX, 3 * half), BF16),
+            pltpu.VMEM((groups, points // 2, width), BF16),
+        ),
+        scratch_shapes=[pltpu.SemaphoreType.DMA((groups,))],
+        compiler_params=kernel_params(16),
+        cost_estimate=cost(8_000_000_000, groups * points * width),
         name="solve",
-    )(parts, counts)
+    )(parts, counts, spectra)
 
 
 def coefficient_rows(message, half):
@@ -187,43 +216,31 @@
     ).astype(BF16)
 
 
-def part_kernel(begin, size, half_index, messages, spectra, out, held, sems):
-    groups, points, width = spectra.shape
-    start = pl.multiple_of(half_index[0] * (points // 2) + begin, 128)
-    copies = [
-        pltpu.make_async_copy(
-            spectra.at[index, pl.ds(start, size)], held.at[index], sems.at[index]
-        )
-        for index in range(groups)
-    ]
-    for copy in copies:
-        copy.start()
+def part_kernel(begin, size, messages, staged, *rest):
+    out = rest[-1]
+    groups, _, width = staged.shape
     for index in range(groups):
-        copies[index].wait()
-        out[index] = project(coefficient_rows(messages[index], width // 2), held[index])
-
-
-def modes_part(half_index, messages, spectra, begin, size):
-    groups, points, width = spectra.shape
+        rows = coefficient_rows(messages[index], width // 2)
+        out[index] = project(rows, staged[index, begin : begin + size])
+
+
+def modes_part(messages, staged, begin, size, *after):
+    groups, _, width = staged.shape
     return pl.pallas_call(
         functools.partial(part_kernel, begin, size),
-        in_specs=[SMEM, VMEM, ANY],
+        in_specs=[VMEM, VMEM] + [ANY] * len(after),
         out_specs=VMEM,
         out_shape=jax.ShapeDtypeStruct((groups, 2 * KMAX, size), BF16),
-        scratch_shapes=[
-            pltpu.VMEM((groups, size, width), BF16),
-            pltpu.SemaphoreType.DMA((groups,)),
-        ],
-        compiler_params=kernel_params(),
+        compiler_params=kernel_params(8),
         cost_estimate=cost(2_000_000_000, groups * size * width * 2),
         name="modes_part",
-    )(half_index, messages, spectra)
-
-
-def modes_kernel(slots, keep, messages, weight, spectra, out, high, low, held, made, sems, put):
+    )(messages, staged, *after)
+
+
+def modes_kernel(slots, messages, weight, spectra, out, energy, high, low, held, made, sems, put):
     groups, points, width = spectra.shape
     part = points // 2
-    start = pl.multiple_of(keep[0] * part, 128)
+    start = pl.multiple_of(kept_half() * part, 128)
 
     def fetch(step, slot):
         return pltpu.make_async_copy(spectra.at[step], held.at[slot], sems.at[slot])
@@ -233,6 +250,12 @@
 
     for slot in range(slots):
         fetch(slot, slot).start()
+    _, lanes = iotas(energy.shape)
+    value = jnp.zeros(energy.shape, F32)
+    for index in range(groups):
+        column = jnp.sum(messages[index, :, width:].astype(F32), axis=1, keepdims=True)
+        value = jnp.where(lanes == index, column, value)
+    energy[...] = value
 
     def body(step, carry):
         slot = lax.rem(step, slots)
@@ -260,16 +283,17 @@
         store(groups - slots + slot, slot).wait()
 
 
-def modes_all(keep, messages, weight, spectra):
+def modes_all(messages, weight, spectra):
     groups, points, width = spectra.shape
     slots = 4
     weighted = jax.ShapeDtypeStruct((groups, 2 * KMAX, points // 2), BF16)
     return pl.pallas_call(
         functools.partial(modes_kernel, slots),
-        in_specs=[SMEM, VMEM, VMEM, ANY],
-        out_specs=(ANY, VMEM, VMEM),
+        in_specs=[VMEM, VMEM, HBM],
+        out_specs=(HBM, VMEM, VMEM, VMEM),
         out_shape=(
             jax.ShapeDtypeStruct((groups, 2 * KMAX, points), BF16),
+            jax.ShapeDtypeStruct((KMAX, groups), F32),
             weighted,
             weighted,
         ),
@@ -279,10 +303,19 @@
             pltpu.SemaphoreType.DMA((slots,)),
             pltpu.SemaphoreType.DMA((slots,)),
         ],
-        compiler_params=kernel_params(),
+        compiler_params=kernel_params(24),
         cost_estimate=cost(10_000_000_000, groups * points * width * 2),
         name="modes_all",
-    )(keep, messages, weight, spectra)
+    )(messages, weight, spectra)
+
+
+def lane_table(partner, rank):
+    groups = partner.shape[0]
+    _, lanes = iotas((KMAX, groups * rank))
+    table = jnp.zeros((KMAX, groups * rank), jnp.int32)
+    for index in range(groups):
+        table = jnp.where(lanes // rank == index, partner[index], table)
+    return table
 
 
 def chosen(cross, lane_partner, groups):
@@ -302,7 +335,7 @@
     )
 
 
-def cross_kernel(first_mine, own_partner, other_partner, high, low, *rest):
+def cross_kernel(own_partner, other_partner, high, low, *rest):
     arrived, out = (rest[:-1], rest[-1])
     groups, rank, part = high.shape
     rows = groups * rank
@@ -317,35 +350,61 @@
                 mine, other, (((1,), (1,)), ((), ())), preferred_element_type=F32
             )
         begin += size
-    own_value = chosen(cross.T, own_partner[...], groups).astype(BF16)
-    other_value = chosen(cross, other_partner[...], groups).astype(BF16)
-    mine_first = first_mine[0] == 1
+    out[:KMAX] = chosen(cross.T, lane_table(own_partner, rank), groups)
+    out[KMAX:] = chosen(cross, lane_table(other_partner, rank), groups)
+
+
+def cross_sums(own_partner, other_partner, high, low, arrived):
+    groups, rank, part = high.shape
+    return pl.pallas_call(
+        cross_kernel,
+        in_specs=[SMEM, SMEM] + [VMEM] * (2 + len(arrived)),
+        out_specs=VMEM,
+        out_shape=jax.ShapeDtypeStruct((2 * KMAX, groups * rank), F32),
+        compiler_params=kernel_params(16),
+        cost_estimate=cost(2_000_000_000, 4 * high.size),
+        name="cross_sums",
+    )(own_partner, other_partner, high, low, *arrived)
+
+
+def spread_kernel(mine, other, out):
+    summed = (mine[...] + other[...]).astype(BF16)
+    width = summed.shape[1]
+    rank = 2 * KMAX
+    rows, cols = iotas((width, width))
+    moved = cols == (rows % rank) * (width // rank) + rows // rank
+    ordered = jnp.dot(summed, moved.astype(F32).astype(BF16), preferred_element_type=F32)
+    first = kept_half() == 0
+    lower = jnp.where(first, ordered[:KMAX], ordered[KMAX:]).astype(BF16)
+    upper = jnp.where(first, ordered[KMAX:], ordered[:KMAX]).astype(BF16)
     half = out.shape[0] // 2
-    lower = jnp.where(mine_first, own_value, other_value)
-    upper = jnp.where(mine_first, other_value, own_value)
     for index in range(half):
         out[index] = lower
         out[half + index] = upper
 
 
-def cross_sums(first_mine, own_partner, other_partner, high, low, arrived, members):
-    groups, rank, part = high.shape
-    return pl.pallas_call(
-        cross_kernel,
-        in_specs=[SMEM] + [VMEM] * (4 + len(arrived)),
+def spread(mine, other, members):
+    return pl.pallas_call(
+        spread_kernel,
+        in_specs=[VMEM, VMEM],
         out_specs=VMEM,
-        out_shape=jax.ShapeDtypeStruct((members, KMAX, groups * rank), BF16),
-        compiler_params=kernel_params(),
-        cost_estimate=cost(2_000_000_000, 4 * high.size),
-        name="cross_sums",
-    )(first_mine, own_partner, other_partner, high, low, *arrived)
+        out_shape=jax.ShapeDtypeStruct((members, KMAX, mine.shape[1]), BF16),
+        compiler_params=kernel_params(8),
+        cost_estimate=cost(10_000_000, 4 * mine.size),
+        name="spread",
+    )(mine, other)
 
 
 def finish_kernel(total, parts, out):
     summed = parts[0].astype(F32)
     for index in range(1, parts.shape[0]):
         summed = summed + parts[index].astype(F32)
-    out[...] = (summed / total).T
+    summed = summed / total
+    groups = out.shape[3]
+    for side in range(2):
+        for k in range(KMAX):
+            begin = (side * KMAX + k) * groups
+            out[side, k] = summed[:, begin : begin + groups]
 
 
 def finish(parts, total):
@@ -354,8 +413,8 @@
         functools.partial(finish_kernel, total),
         in_specs=[VMEM],
         out_specs=VMEM,
-        out_shape=jax.ShapeDtypeStruct((width, kmax), F32),
-        compiler_params=kernel_params(),
+        out_shape=jax.ShapeDtypeStruct((2, kmax, kmax, width // (2 * kmax)), F32),
+        compiler_params=kernel_params(8),
         cost_estimate=cost(1_000_000, parts.size * 2),
         name="finish",
     )(parts)
@@ -365,41 +424,42 @@
     groups, points, width = spectra.shape
     n_freq, n_space = (lax.axis_size("freq"), lax.axis_size("space"))
     total = points * n_space
-    place = lax.axis_index("freq")
-    lower_group = place < n_freq // 2
-    keep = jnp.where(lower_group, 0, 1).astype(jnp.int32).reshape(1)
-    give = 1 - keep
+    spectra = pltpu.with_memory_space_constraint(spectra, pltpu.HBM)
     weight_row = weight[None, :]
-    lane_partner = jnp.repeat(partner, 2 * KMAX)[None, :]
     mirror = [(index, n_freq - 1 - index) for index in range(n_freq)]
 
-    packed = gram(spectra, weight_row)
+    packed = gram(spectra, pltpu.with_memory_space_constraint(weight_row, pltpu.HBM))
     parts = lax.all_to_all(packed, "space", 0, 0, tiled=True)
-    message = solve(parts, counts, total)
+    message, staged = solve(parts, counts, spectra, total)
     messages = lax.all_to_all(message, "space", 0, 0, tiled=True)
 
-    pieces = 2
-    size = points // 2 // pieces
-    shares = [
-        modes_part(give, messages, spectra, index * size, size) for index in range(pieces)
+    staged = pltpu.with_memory_space_constraint(staged, pltpu.VMEM)
+    part = points // 2
+    cut = part // 4
+    first_share = modes_part(messages, staged, 0, cut)
+    shares = [first_share, modes_part(messages, staged, cut, part - cut, first_share)]
+    arrived = [lax.ppermute(share, "freq", mirror) for share in shares]
+    later_partner, _ = lax.optimization_barrier((partner, shares[-1]))
+    other_partner = lax.ppermute(later_partner, "freq", mirror)
+    modes, energy, high, low = modes_all(messages, weight_row, spectra)
+
+    sums = cross_sums(partner, other_partner, high, low, arrived)
+    paired = lax.ppermute(sums, "space", [(index, index ^ 1) for index in range(n_space)])
+    members = [
+        [group * n_space + index for group in (low_group, n_freq - 1 - low_group) for index in range(core, n_space, 2)]
+        for low_group in range(n_freq // 2)
+        for core in range(2)
     ]
-    arrived = [lax.ppermute(share, "freq", mirror) for share in shares]
-    other_partner = lax.ppermute(lane_partner, "freq", mirror)
-    modes, high, low = modes_all(keep, messages, weight_row, spectra)
-    energy = jnp.sum(messages[:, :, width : width + 3].astype(F32), axis=2)
-
-    pairs = [
-        [group * n_space + index for group in (low_group, n_freq - 1 - low_group) for index in range(n_space)]
-        for low_group in range(n_freq // 2)
-    ]
-    sums = cross_sums(
-        give, lane_partner, other_partner, high, low, arrived, 2 * n_space
-    )
     gathered = lax.all_to_all(
-        sums, ("freq", "space"), 0, 0, tiled=True, axis_index_groups=pairs
-    )
-    coherence = finish(gathered, total).reshape(groups, 2, KMAX, KMAX)
-    return (modes, energy, coherence)
+        spread(sums, paired, n_space),
+        ("freq", "space"),
+        0,
+        0,
+        tiled=True,
+        axis_index_groups=members,
+    )
+    coherence = jnp.transpose(finish(gathered, total), (3, 0, 1, 2))
+    return (modes, jnp.transpose(energy), coherence)
 
 
 def solution(mesh):

time: 92.9 us -> 87.2 us (0.939)
  blocking collectives: 16.6 us -> 38.5 us
  starting transfers between devices: 23.2 us -> 12.4 us
  waiting for transfers between devices: 11.7 us -> 1.96 us
  Pallas kernels: 37.9 us -> 33 us
  local copies, waits for them, and re-layouts: 2.28 us -> 0.01 us
    all_to_all x0 -> x2, blocking collectives: none -> 21.9 us  [the longest x1 12.2 us: on_device(): lax.all_to_all(spread(sums, paired, n_space), ('freq', 'space'), 0, 0, ti...]
    all_to_all x2 -> x0, starting transfers between devices: 12 us -> none  [the longest x1 7.29 us: on_device(): lax.all_to_all(sums, ('freq', 'space'), 0, 0, tiled=True, axis_index_grou...]
    all_to_all x2 -> x0, waiting for transfers between devices: 9.22 us -> none  [the longest x1 8.98 us: on_device(): lax.all_to_all(sums, ('freq', 'space'), 0, 0, tiled=True, axis_index_grou...]
    pallas_call x5 -> x6, Pallas kernels: 32.8 us -> 26.8 us  [the longest x1 11.5 us: modes_all(): pl.pallas_call(functools.partial(modes_kernel, slots), in_specs=[VMEM, VM...]
    ppermute x2, waiting for transfers between devices: 2.51 us -> 0.01 us  [on_device(): arrived = [lax.ppermute(share, 'freq', mirror) for share in shares]]
    unnamed x10 -> x6, local copies, waits for them, and re-layouts: 2.13 us -> 0.01 us
    ppermute x1 -> x2, waiting for transfers between devices: 0.01 us -> 1.95 us  [the longest x1 1.11 us: on_device(): other_partner = lax.ppermute(later_partner, 'freq', mirror)]
    ppermute x1 -> x2, starting transfers between devices: 5.51 us -> 6.88 us  [the longest x1 5.06 us: on_device(): other_partner = lax.ppermute(later_partner, 'freq', mirror)]
  transfers between devices with their start and end apart: 5 -> 4, of which waited for: 3 -> 2; matrix products, arithmetic and copies ran while one was open for 1% -> 0% of each run, Pallas kernels for 23% -> 16%
where the time goes in v2:
time: 87.2 us; the launch traced here: 86.6 us
  blocking collectives  38.5 us (44%)
  Pallas kernels  33 us (38%)
  starting transfers between devices  12.4 us (14%)
  waiting for transfers between devices  1.96 us (2%)
    all_to_all x1, blocking collectives, on_device(): parts = lax.all_to_all(packed, 'space', 0, 0, tiled=True)  16.6 us
    all_to_all x1, blocking collectives, on_device(): lax.all_to_all(spread(sums, paired, n_space), ('freq', 'space'), 0, 0, ti...  12.2 us
    pallas_call x1, Pallas kernels, modes_all(): pl.pallas_call(functools.partial(modes_kernel, slots), in_specs=[VMEM, VM...  11.5 us
    pallas_call x1, Pallas kernels, gram(): pl.pallas_call(functools.partial(gram_kernel, depth), in_specs=[HBM, ANY]...  10.3 us
    all_to_all x1, blocking collectives, on_device(): messages = lax.all_to_all(message, 'space', 0, 0, tiled=True)  9.75 us
    pallas_call x1, Pallas kernels, solve(): pl.pallas_call(functools.partial(solve_kernel, total), in_specs=[VMEM, SM...  5.53 us
    ppermute x2, starting transfers between devices, on_device(): arrived = [lax.ppermute(share, 'freq', mirror) for share in shares]  5.52 us
    ppermute x1, starting transfers between devices, on_device(): other_partner = lax.ppermute(later_partner, 'freq', mirror)  5.06 us
  transfers between devices with their start and end apart: 4, of which 2 were waited for; matrix products, arithmetic and copies ran while one was open for 0% of the time, Pallas kernels for 16%

profile of v2, /device:TPU:1, one launch (start us, length us, event | category | flops | bytes accessed | tf_op | source)
XLA Modules:
  0.0 86.6 jit_solution(2574506155856602577)
XLA Ops:
  0.6 0.0 copy-start.1
  0.6 10.3 %gram.1 = bf16[16,128,128]{2,1,0:T(8,128)(2,1)S(1)} custom-call(bf16[16,3072,256]{2,1,0:T(8,128)(2,1)} %spectra.5, f32[1,3072]{1,0:T(1,128)} %bitcast.3), custom_call_target="tpu_custom_call" | custom-call | flops 6442450944 | bytes 25165824 | tf_op jit(solution)/shard_map/gram/pallas_call | solution.py:83
  11.0 16.6 %all_to_all.15.parts = bf16[16,128,128]{2,1,0:T(8,128)(2,1)S(1)} all-to-all(bf16[16,128,128]{2,1,0:T(8,128)(2,1)S(1)} %gram.1), channel_id=1, replica_groups=mesh['freq'=8,'space'=16] {'space'}, dimensions={0} | all-to-all | bytes 1048576 | tf_op jit(solution)/shard_map/all_to_all | solution.py:432
  27.6 0.0 copy-done.1
  27.6 5.5 %solve.1 = (bf16[16,8,384]{2,1,0:T(8,128)(2,1)S(1)}, bf16[16,1536,256]{2,1,0:T(8,128)(2,1)S(1)}) custom-call(bf16[16,128,128]{2,1,0:T(8,128)(2,1)S(1)} %all_to_all.15.parts, s32[16]{0:T(128)S(1)} %copy-done.1, bf16[16,3072,256]{2,1,0:T(8,128)(2,1)} %spectra.5), custom_call_target="tpu_custom_call" | custom-call | flops 8000000000 | bytes 12582912 | tf_op jit(solution)/shard_map/solve/pallas_call | solution.py:186
  33.1 9.8 %all_to_all.16.messages = bf16[16,8,384]{2,1,0:T(8,128)(2,1)S(1)} all-to-all(bf16[16,8,384]{2,1,0:T(8,128)(2,1)S(1)} %get-tuple-element.10), channel_id=1, replica_groups=mesh['freq'=8,'space'=16] {'space'}, dimensions={0} | all-to-all | bytes 196608 | tf_op jit(solution)/shard_map/all_to_all | solution.py:434
  42.9 0.0 copy-start.2
  42.9 0.0 copy-start
  42.9 0.9 %modes_part.2.rest_0_ = bf16[16,16,384]{2,1,0:T(8,128)(2,1)S(1)} custom-call(bf16[16,8,384]{2,1,0:T(8,128)(2,1)S(1)} %all_to_all.16.messages, bf16[16,1536,256]{2,1,0:T(8,128)(2,1)S(1)} %get-tuple-element.13.staged), custom_call_target="tpu_custom_call" | custom-call | flops 2000000000 | bytes 3145728 | tf_op jit(solution)/shard_map/modes_part/pallas_call | solution.py:229
  43.8 5.5 %collective-permute-start.1 = (bf16[16,16,384]{2,1,0:T(8,128)(2,1)S(1)}, bf16[16,16,384]{2,1,0:T(8,128)(2,1)S(1)}, u32[]{:S(2)}, u32[]{:S(2)}) collective-permute-start(bf16[16,16,384]{2,1,0:T(8,128)(2,1)S(1)} %modes_part.2.rest_0_), channel_id=1, source_target_pairs={{0,112},{16,96},{32,80},{48,64},{64,48},{80,32},{96,16},{112,0},{1... | collective-permute-start | bytes 589832 | tf_op jit(solution)/shard_map/ppermute | solution.py:441
  49.3 2.5 %modes_part.3 = bf16[16,16,1152]{2,1,0:T(8,128)(2,1)S(1)} custom-call(bf16[16,8,384]{2,1,0:T(8,128)(2,1)S(1)} %all_to_all.16.messages, bf16[16,1536,256]{2,1,0:T(8,128)(2,1)S(1)} %get-tuple-element.13.staged, bf16[16,16,384]{2,1,0:T(8,128)(2,1)S(1)} %modes_part.2.rest_0_), custom_call_target="tpu_custom_call" | custom-call | flops 2000000000 | bytes 9437184 | tf_op jit(solution)/shard_map/modes_part/pallas_call | solution.py:229
  51.8 0.1 collective-permute-start.2
  51.9 0.0 copy-done.2
  51.9 5.1 %collective-permute-start = (s32[16]{0:T(128)S(1)}, s32[16]{0:T(128)S(1)}, u32[]{:S(2)}, u32[]{:S(2)}) collective-permute-start(s32[16]{0:T(128)S(1)} %copy-done.2), channel_id=1, source_target_pairs={{0,112},{16,96},{32,80},{48,64},{64,48},{80,32},{96,16},{112,0},{1... | collective-permute-start | bytes 200 | tf_op jit(solution)/shard_map/ppermute | solution.py:443
  56.9 0.0 copy-done
  56.9 11.5 %modes_all.1 = (bf16[16,16,3072]{2,1,0:T(8,128)(2,1)}, f32[8,16]{1,0:T(8,128)}, bf16[16,16,1536]{2,1,0:T(8,128)(2,1)S(1)}, bf16[16,16,1536]{2,1,0:T(8,128)(2,1)S(1)}) custom-call(bf16[16,8,384]{2,1,0:T(8,128)(2,1)S(1)} %all_to_all.16.messages, f32[1,3072]{1,0:T(1,128)S(1)} %bitcast.4, bf16[16,3072,256]{2,1,0:T(8,128)(2,1)} %spectra.5), custom_call_target="tpu_custom_call" | custom-call | flops 10000000000 | bytes 25165824 | tf_op jit(solution)/shard_map/modes_all/pallas_call | solution.py:290
  68.4 1.1 %collective-permute-done.other_partner = s32[16]{0:T(128)S(1)} collective-permute-done((s32[16]{0:T(128)S(1)}, s32[16]{0:T(128)S(1)}, u32[]{:S(2)}, u32[]{:S(2)}) %collective-permute-start) | collective-permute-done | bytes 96 | tf_op jit(solution)/shard_map/ppermute | solution.py:443
  69.5 0.0 collective-permute-done.1.rest_0_
  69.5 0.0 collective-permute-done.2.rest_1_
  69.5 1.4 %cross_sums.1.mine = f32[16,256]{1,0:T(8,128)S(1)} custom-call(s32[16]{0:T(128)S(1)} %copy-done.2, s32[16]{0:T(128)S(1)} %collective-permute-done.other_partner, bf16[16,16,1536]{2,1,0:T(8,128)(2,1)S(1)} %get-tuple-element.15.high, bf16[16,16,1536]{2,1,0:T(8,128)(2,1)S(1)} %get-tuple-element.16.low, bf16[16,16,384]{2,1,0:T(8,128)(2,1)S(1)} %collective-permute-done.1.rest_0_, ...), custom_call_target="tpu_custom_call" | custom-call | flops 2000000000 | bytes 1572864 | tf_op jit(solution)/shard_map/cross_sums/pallas_call | solution.py:359
  70.9 1.8 %collective-permute-start.3 = (f32[16,256]{1,0:T(8,128)S(1)}, f32[16,256]{1,0:T(8,128)S(1)}, u32[]{:S(2)}, u32[]{:S(2)}) collective-permute-start(f32[16,256]{1,0:T(8,128)S(1)} %cross_sums.1.mine), channel_id=1, source_target_pairs={{0,1},{1,0},{2,3},{3,2},{4,5},{5,4},{6,7},{7,6},{8,9},{9,8},{10,11... | collective-permute-start | bytes 49160 | tf_op jit(solution)/shard_map/ppermute | solution.py:447
  72.7 0.8 collective-permute-done.3.other
  73.5 0.2 spread.1
  73.7 12.2 %all_to_all.17.parts = bf16[16,8,256]{2,1,0:T(8,128)(2,1)S(1)} all-to-all(bf16[16,8,256]{2,1,0:T(8,128)(2,1)S(1)} %spread.1), channel_id=1, replica_groups={{0,2,4,6,8,10,12,14,112,114,116,118,120,122,124,126},{1,3,5,7,9,11,13,1..., dimensions={0} | all-to-all | bytes 131072 | tf_op jit(solution)/shard_map/all_to_all | solution.py:453
  85.9 0.7 finish.1
Async XLA Ops:
  0.6 27.0 %copy-start.1 = (s32[16]{0:T(128)S(1)}, s32[16]{0:T(128)}, u32[]{:S(2)}) copy-start(s32[16]{0:T(128)} %counts.1) | copy-start | bytes 196
  42.9 9.0 %copy-start.2 = (s32[16]{0:T(128)S(1)}, s32[16]{0:T(128)}, u32[]{:S(2)}) copy-start(s32[16]{0:T(128)} %own_partner.1) | copy-start | bytes 196
  42.9 14.1 %copy-start = (f32[3072]{0:T(1024)S(1)}, f32[3072]{0:T(1024)}, u32[]{:S(2)}) copy-start(f32[3072]{0:T(1024)} %param.5) | copy-start | bytes 36868
  43.8 25.7 %collective-permute-start.1 = (bf16[16,16,384]{2,1,0:T(8,128)(2,1)S(1)}, bf16[16,16,384]{2,1,0:T(8,128)(2,1)S(1)}, u32[]{:S(2)}, u32[]{:S(2)}) collective-permute-start(bf16[16,16,384]{2,1,0:T(8,128)(2,1)S(1)} %modes_part.2.rest_0_), channel_id=1, source_target_pairs={{0,112},{16,96},{32,80},{48,64},{64,48},{80,32},{96,16},{112,0},{1... | collective-permute-start | bytes 589832 | tf_op jit(solution)/shard_map/ppermute | solution.py:441
  51.8 17.7 %collective-permute-start.2 = (bf16[16,16,1152]{2,1,0:T(8,128)(2,1)S(1)}, bf16[16,16,1152]{2,1,0:T(8,128)(2,1)S(1)}, u32[]{:S(2)}, u32[]{:S(2)}) collective-permute-start(bf16[16,16,1152]{2,1,0:T(8,128)(2,1)S(1)} %modes_part.3), channel_id=1, source_target_pairs={{0,112},{16,96},{32,80},{48,64},{64,48},{80,32},{96,16},{112,0},{1... | collective-permute-start | bytes 1769480 | tf_op jit(solution)/shard_map/ppermute | solution.py:441
  51.9 17.7 %collective-permute-start = (s32[16]{0:T(128)S(1)}, s32[16]{0:T(128)S(1)}, u32[]{:S(2)}, u32[]{:S(2)}) collective-permute-start(s32[16]{0:T(128)S(1)} %copy-done.2), channel_id=1, source_target_pairs={{0,112},{16,96},{32,80},{48,64},{64,48},{80,32},{96,16},{112,0},{1... | collective-permute-start | bytes 200 | tf_op jit(solution)/shard_map/ppermute | solution.py:443
  70.9 2.7 %collective-permute-start.3 = (f32[16,256]{1,0:T(8,128)S(1)}, f32[16,256]{1,0:T(8,128)S(1)}, u32[]{:S(2)}, u32[]{:S(2)}) collective-permute-start(f32[16,256]{1,0:T(8,128)S(1)} %cross_sums.1.mine), channel_id=1, source_target_pairs={{0,1},{1,0},{2,3},{3,2},{4,5},{5,4},{6,7},{7,6},{8,9},{9,8},{10,11... | collective-permute-start | bytes 49160 | tf_op jit(solution)/shard_map/ppermute | solution.py:447

commit v3 on v2

--- a/solution.py
+++ b/solution.py
@@ -37,18 +37,16 @@
     )
 
 
-def gram_kernel(depth, spectra, weight, packed, held, scale, sems, scale_sem):
+def gram_kernel(depth, per_step, spectra, weight, mine, other, resident, scale, sems, scale_sem):
     groups, points, width = spectra.shape
     half = width // 2
-    slots, per_step = held.shape[:2]
     steps = groups // per_step
     rows, cols = iotas((half, half))
+    south = lax.rem(lax.axis_index("space"), 2) == 0
 
     def fetch(step):
-        slot = lax.rem(step, slots)
-        return pltpu.make_async_copy(
-            spectra.at[pl.ds(step * per_step, per_step)], held.at[slot], sems.at[slot]
-        )
+        part = pl.ds(step * per_step, per_step)
+        return pltpu.make_async_copy(spectra.at[part], resident.at[part], sems.at[step])
 
     fetch(0).start()
     scale_copy = pltpu.make_async_copy(weight, scale, scale_sem)
@@ -57,6 +55,14 @@
         fetch(step).start()
     scale_copy.wait()
 
+    def hermitian(index):
+        block = resident[index]
+        weighted = (block.T.astype(F32) * scale[...]).astype(BF16)
+        moment = jnp.dot(weighted, block, preferred_element_type=F32)
+        real = moment[:half, :half] + moment[half:, half:]
+        imag = moment[:half, half:] - moment[half:, :half]
+        return jnp.where(cols >= rows, real, imag)
+
     def body(step, carry):
         fetch(step).wait()
 
@@ -64,13 +70,12 @@
         def _():
             fetch(step + depth).start()
 
-        for index in range(per_step):
-            block = held[lax.rem(step, slots), index]
-            weighted = (block.T.astype(F32) * scale[...]).astype(BF16)
-            moment = jnp.dot(weighted, block, preferred_element_type=F32)
-            real = moment[:half, :half] + moment[half:, half:]
-            imag = moment[:half, half:] - moment[half:, :half]
-            packed[step * per_step + index] = jnp.where(cols >= rows, real, imag).astype(BF16)
+        for index in range(0, per_step, 2):
+            even = hermitian(step * per_step + index)
+            odd = hermitian(step * per_step + index + 1)
+            place = (step * per_step + index) // 2
+            mine[place] = jnp.where(south, even, odd)
+            other[place] = jnp.where(south, odd, even)
         return carry
 
     lax.fori_loop(0, steps, body, 0)
@@ -79,19 +84,19 @@
 def gram(spectra, weight):
     groups, points, width = spectra.shape
     half = width // 2
-    depth, slots, per_step = (2, 3, 2)
-    return pl.pallas_call(
-        functools.partial(gram_kernel, depth),
-        in_specs=[HBM, ANY],
-        out_specs=VMEM,
-        out_shape=jax.ShapeDtypeStruct((groups, half, half), BF16),
+    depth, per_step = (2, 2)
+    sums = jax.ShapeDtypeStruct((groups // 2, half, half), F32)
+    return pl.pallas_call(
+        functools.partial(gram_kernel, depth, per_step),
+        in_specs=[HBM, HBM],
+        out_specs=(VMEM, VMEM, VMEM),
+        out_shape=(sums, sums, pltpu.VMEM((groups, points, width), BF16)),
         scratch_shapes=[
-            pltpu.VMEM((slots, per_step, points, width), BF16),
             pltpu.VMEM((1, points), F32),
-            pltpu.SemaphoreType.DMA((slots,)),
+            pltpu.SemaphoreType.DMA((groups // per_step,)),
             pltpu.SemaphoreType.DMA,
         ],
-        compiler_params=kernel_params(24),
+        compiler_params=kernel_params(16),
         cost_estimate=cost(2 * groups * points * width * width, groups * points * width * 2),
         name="gram",
     )(spectra, weight)
@@ -116,18 +121,8 @@
     return (re, im)
 
 
-def solve_kernel(total, parts, counts, spectra, out, staged, sems):
+def solve_kernel(total, parts, counts, out):
     count, half, _ = parts.shape
-    groups, part, _ = staged.shape
-    start = pl.multiple_of((1 - kept_half()) * part, 128)
-    copies = [
-        pltpu.make_async_copy(
-            spectra.at[index, pl.ds(start, part)], staged.at[index], sems.at[index]
-        )
-        for index in range(groups)
-    ]
-    for copy in copies:
-        copy.start()
     summed = parts[0].astype(F32)
     for index in range(1, count):
         summed = summed + parts[index].astype(F32)
@@ -176,26 +171,19 @@
     message = jnp.concatenate([re * scale, im * scale, tail], axis=1).astype(BF16)
     for index in range(out.shape[0]):
         out[index] = message
-    for copy in copies:
-        copy.wait()
-
-
-def solve(parts, counts, spectra, total):
-    count, half, _ = parts.shape
-    groups, points, width = spectra.shape
+
+
+def solve(parts, counts, total):
+    _, half, _ = parts.shape
     return pl.pallas_call(
         functools.partial(solve_kernel, total),
-        in_specs=[VMEM, SMEM, HBM],
-        out_specs=(VMEM, VMEM),
-        out_shape=(
-            jax.ShapeDtypeStruct((count, KMAX, 3 * half), BF16),
-            pltpu.VMEM((groups, points // 2, width), BF16),
-        ),
-        scratch_shapes=[pltpu.SemaphoreType.DMA((groups,))],
-        compiler_params=kernel_params(16),
-        cost_estimate=cost(8_000_000_000, groups * points * width),
+        in_specs=[VMEM, SMEM],
+        out_specs=VMEM,
+        out_shape=jax.ShapeDtypeStruct((counts.shape[0], KMAX, 3 * half), BF16),
+        compiler_params=kernel_params(8),
+        cost_estimate=cost(8_000_000_000, parts.size * 2),
         name="solve",
-    )(parts, counts, spectra)
+    )(parts, counts)
 
 
 def coefficient_rows(message, half):
@@ -216,40 +204,43 @@
     ).astype(BF16)
 
 
-def part_kernel(begin, size, messages, staged, *rest):
+def part_kernel(begin, size, messages, partner, resident, *rest):
     out = rest[-1]
-    groups, _, width = staged.shape
+    groups, points, width = resident.shape
+    start = pl.multiple_of((1 - kept_half()) * (points // 2) + begin, 128)
     for index in range(groups):
         rows = coefficient_rows(messages[index], width // 2)
-        out[index] = project(rows, staged[index, begin : begin + size])
-
-
-def modes_part(messages, staged, begin, size, *after):
-    groups, _, width = staged.shape
+        out[index] = project(rows, resident[index, pl.ds(start, size)])
+    if out.shape[0] > groups:
+        _, lanes = iotas((2 * KMAX, size))
+        table = jnp.zeros((2 * KMAX, size), jnp.int32)
+        for index in range(groups):
+            table = jnp.where(lanes // (2 * KMAX) == index, partner[index], table)
+        out[groups] = table.astype(F32).astype(BF16)
+
+
+def modes_part(messages, partner, resident, begin, size, *after):
+    groups, _, width = resident.shape
+    planes = groups if after else groups + 1
     return pl.pallas_call(
         functools.partial(part_kernel, begin, size),
-        in_specs=[VMEM, VMEM] + [ANY] * len(after),
+        in_specs=[VMEM, SMEM, VMEM] + [ANY] * len(after),
         out_specs=VMEM,
-        out_shape=jax.ShapeDtypeStruct((groups, 2 * KMAX, size), BF16),
+        out_shape=jax.ShapeDtypeStruct((planes, 2 * KMAX, size), BF16),
         compiler_params=kernel_params(8),
         cost_estimate=cost(2_000_000_000, groups * size * width * 2),
         name="modes_part",
-    )(messages, staged, *after)
-
-
-def modes_kernel(slots, messages, weight, spectra, out, energy, high, low, held, made, sems, put):
-    groups, points, width = spectra.shape
+    )(messages, partner, resident, *after)
+
+
+def modes_kernel(slots, messages, weight, resident, after, out, energy, high, low, made, put):
+    groups, points, width = resident.shape
     part = points // 2
     start = pl.multiple_of(kept_half() * part, 128)
 
-    def fetch(step, slot):
-        return pltpu.make_async_copy(spectra.at[step], held.at[slot], sems.at[slot])
-
     def store(step, slot):
         return pltpu.make_async_copy(made.at[slot], out.at[step], put.at[slot])
 
-    for slot in range(slots):
-        fetch(slot, slot).start()
     _, lanes = iotas(energy.shape)
     value = jnp.zeros(energy.shape, F32)
     for index in range(groups):
@@ -264,18 +255,12 @@
         def _():
             store(step - slots, slot).wait()
 
-        fetch(step, slot).wait()
-        made[slot] = project(coefficient_rows(messages[step], width // 2), held[slot])
+        made[slot] = project(coefficient_rows(messages[step], width // 2), resident[step])
         store(step, slot).start()
         own = made[slot, :, pl.ds(start, part)].astype(F32) * weight[:, pl.ds(start, part)]
         top = own.astype(BF16)
         high[step] = top
         low[step] = (own - top.astype(F32)).astype(BF16)
-
-        @pl.when(step + slots < groups)
-        def _():
-            fetch(step + slots, slot).start()
-
         return carry
 
     lax.fori_loop(0, groups, body, 0)
@@ -283,13 +268,13 @@
         store(groups - slots + slot, slot).wait()
 
 
-def modes_all(messages, weight, spectra):
-    groups, points, width = spectra.shape
+def modes_all(messages, weight, resident, after):
+    groups, points, width = resident.shape
     slots = 4
     weighted = jax.ShapeDtypeStruct((groups, 2 * KMAX, points // 2), BF16)
     return pl.pallas_call(
         functools.partial(modes_kernel, slots),
-        in_specs=[VMEM, VMEM, HBM],
+        in_specs=[VMEM, VMEM, VMEM, ANY],
         out_specs=(HBM, VMEM, VMEM, VMEM),
         out_shape=(
             jax.ShapeDtypeStruct((groups, 2 * KMAX, points), BF16),
@@ -298,15 +283,13 @@
             weighted,
         ),
         scratch_shapes=[
-            pltpu.VMEM((slots, points, width), BF16),
             pltpu.VMEM((slots, 2 * KMAX, points), BF16),
             pltpu.SemaphoreType.DMA((slots,)),
-            pltpu.SemaphoreType.DMA((slots,)),
         ],
-        compiler_params=kernel_params(24),
-        cost_estimate=cost(10_000_000_000, groups * points * width * 2),
+        compiler_params=kernel_params(12),
+        cost_estimate=cost(7_000_000_000, groups * points * width * 2),
         name="modes_all",
-    )(messages, weight, spectra)
+    )(messages, weight, resident, after)
 
 
 def lane_table(partner, rank):
@@ -335,7 +318,7 @@
     )
 
 
-def cross_kernel(own_partner, other_partner, high, low, *rest):
+def cross_kernel(own_partner, high, low, *rest):
     arrived, out = (rest[:-1], rest[-1])
     groups, rank, part = high.shape
     rows = groups * rank
@@ -343,37 +326,20 @@
     begin = 0
     for share in arrived:
         size = share.shape[2]
-        other = share[...].reshape(rows, size)
+        other = share[:groups].reshape(rows, size)
         for own in (high, low):
             mine = own[:, :, begin : begin + size].reshape(rows, size)
             cross = cross + lax.dot_general(
                 mine, other, (((1,), (1,)), ((), ())), preferred_element_type=F32
             )
         begin += size
-    out[:KMAX] = chosen(cross.T, lane_table(own_partner, rank), groups)
-    out[KMAX:] = chosen(cross, lane_table(other_partner, rank), groups)
-
-
-def cross_sums(own_partner, other_partner, high, low, arrived):
-    groups, rank, part = high.shape
-    return pl.pallas_call(
-        cross_kernel,
-        in_specs=[SMEM, SMEM] + [VMEM] * (2 + len(arrived)),
-        out_specs=VMEM,
-        out_shape=jax.ShapeDtypeStruct((2 * KMAX, groups * rank), F32),
-        compiler_params=kernel_params(16),
-        cost_estimate=cost(2_000_000_000, 4 * high.size),
-        name="cross_sums",
-    )(own_partner, other_partner, high, low, *arrived)
-
-
-def spread_kernel(mine, other, out):
-    summed = (mine[...] + other[...]).astype(BF16)
-    width = summed.shape[1]
-    rank = 2 * KMAX
-    rows, cols = iotas((width, width))
-    moved = cols == (rows % rank) * (width // rank) + rows // rank
-    ordered = jnp.dot(summed, moved.astype(F32).astype(BF16), preferred_element_type=F32)
+    other_table = arrived[0][groups, :KMAX, :rows].astype(F32).astype(jnp.int32)
+    own_value = chosen(cross.T, lane_table(own_partner, rank), groups)
+    other_value = chosen(cross, other_table, groups)
+    both = jnp.concatenate([own_value, other_value], axis=0).astype(BF16)
+    source, target = iotas((rows, rows))
+    moved = target == (source % rank) * groups + source // rank
+    ordered = jnp.dot(both, moved.astype(F32).astype(BF16), preferred_element_type=F32)
     first = kept_half() == 0
     lower = jnp.where(first, ordered[:KMAX], ordered[KMAX:]).astype(BF16)
     upper = jnp.where(first, ordered[KMAX:], ordered[:KMAX]).astype(BF16)
@@ -383,16 +349,17 @@
         out[half + index] = upper
 
 
-def spread(mine, other, members):
-    return pl.pallas_call(
-        spread_kernel,
-        in_specs=[VMEM, VMEM],
+def cross_sums(own_partner, high, low, arrived, members):
+    groups, rank, part = high.shape
+    return pl.pallas_call(
+        cross_kernel,
+        in_specs=[SMEM] + [VMEM] * (2 + len(arrived)),
         out_specs=VMEM,
-        out_shape=jax.ShapeDtypeStruct((members, KMAX, mine.shape[1]), BF16),
-        compiler_params=kernel_params(8),
-        cost_estimate=cost(10_000_000, 4 * mine.size),
-        name="spread",
-    )(mine, other)
+        out_shape=jax.ShapeDtypeStruct((members, KMAX, groups * rank), BF16),
+        compiler_params=kernel_params(16),
+        cost_estimate=cost(2_000_000_000, 4 * high.size),
+        name="cross_sums",
+    )(own_partner, high, low, *arrived)
 
 
 def finish_kernel(total, parts, out):
@@ -428,30 +395,34 @@
     weight_row = weight[None, :]
     mirror = [(index, n_freq - 1 - index) for index in range(n_freq)]
 
-    packed = gram(spectra, pltpu.with_memory_space_constraint(weight_row, pltpu.HBM))
-    parts = lax.all_to_all(packed, "space", 0, 0, tiled=True)
-    message, staged = solve(parts, counts, spectra, total)
+    mine, other, resident = gram(
+        spectra, pltpu.with_memory_space_constraint(weight_row, pltpu.HBM)
+    )
+    resident = pltpu.with_memory_space_constraint(resident, pltpu.VMEM)
+    swapped = lax.ppermute(other, "space", [(index, index ^ 1) for index in range(n_space)])
+    chips = [[index for index in range(core, n_space, 2)] for core in range(2)]
+    parts = lax.all_to_all(
+        (mine + swapped).astype(BF16), "space", 0, 0, tiled=True, axis_index_groups=chips
+    )
+    message = solve(parts, counts, total)
     messages = lax.all_to_all(message, "space", 0, 0, tiled=True)
 
-    staged = pltpu.with_memory_space_constraint(staged, pltpu.VMEM)
     part = points // 2
-    cut = part // 4
-    first_share = modes_part(messages, staged, 0, cut)
-    shares = [first_share, modes_part(messages, staged, cut, part - cut, first_share)]
+    cut = part // 3
+    first_share = modes_part(messages, partner, resident, 0, cut)
+    shares = [
+        first_share,
+        modes_part(messages, partner, resident, cut, part - cut, first_share),
+    ]
     arrived = [lax.ppermute(share, "freq", mirror) for share in shares]
-    later_partner, _ = lax.optimization_barrier((partner, shares[-1]))
-    other_partner = lax.ppermute(later_partner, "freq", mirror)
-    modes, energy, high, low = modes_all(messages, weight_row, spectra)
-
-    sums = cross_sums(partner, other_partner, high, low, arrived)
-    paired = lax.ppermute(sums, "space", [(index, index ^ 1) for index in range(n_space)])
+    modes, energy, high, low = modes_all(messages, weight_row, resident, shares[-1])
+
     members = [
-        [group * n_space + index for group in (low_group, n_freq - 1 - low_group) for index in range(core, n_space, 2)]
+        [group * n_space + index for group in (low_group, n_freq - 1 - low_group) for index in range(n_space)]
         for low_group in range(n_freq // 2)
-        for core in range(2)
     ]
     gathered = lax.all_to_all(
-        spread(sums, paired, n_space),
+        cross_sums(partner, high, low, arrived, 2 * n_space),
         ("freq", "space"),
         0,
         0,

time: 87.2 us -> 86 us (0.986)
  waiting for transfers between devices: 1.96 us -> 7.66 us
  starting transfers between devices: 12.4 us -> 7.01 us
  Pallas kernels: 33 us -> 31.5 us
    ppermute x2, waiting for transfers between devices: 0.01 us -> 6.12 us  [on_device(): arrived = [lax.ppermute(share, 'freq', mirror) for share in shares]]
    ppermute x2 -> x1, starting transfers between devices: 6.88 us -> 1.46 us  [on_device(): lax.ppermute(other, 'space', [(index, index ^ 1) for index in range(n_spa...]
    pallas_call x1, Pallas kernels: 11.5 us -> 10.1 us  [modes_all(): pl.pallas_call(functools.partial(modes_kernel, slots), in_specs=[VMEM, VM...]
    pallas_call x1, Pallas kernels: 5.53 us -> 4.24 us  [solve(): pl.pallas_call(functools.partial(solve_kernel, total), in_specs=[VMEM, SM...]
    pallas_call x2, Pallas kernels: 3.46 us -> 4.58 us  [modes_part(): pl.pallas_call(functools.partial(part_kernel, begin, size), in_specs=[VME...]
    ppermute x2 -> x1, waiting for transfers between devices: 1.95 us -> 1.54 us  [on_device(): lax.ppermute(other, 'space', [(index, index ^ 1) for index in range(n_spa...]
    pallas_call x3 -> x2, Pallas kernels: 11.8 us -> 11.8 us  [the longest x1 10.4 us: gram(): pl.pallas_call(functools.partial(gram_kernel, depth, per_step), in_specs=...]
  transfers between devices with their start and end apart: 4 -> 3, of which waited for: 2 -> 2; matrix products, arithmetic and copies ran while one was open for 0% -> 0% of each run, Pallas kernels for 16% -> 15%
where the time goes in v3:
time: 86 us; the launch traced here: 85.8 us
  blocking collectives  38.9 us (45%)
  Pallas kernels  31.5 us (37%)
  waiting for transfers between devices  7.66 us (9%)
  starting transfers between devices  7.01 us (8%)
    all_to_all x1, blocking collectives, on_device(): lax.all_to_all(cross_sums(partner, high, low, arrived, 2 * n_space), ('fr...  16.8 us
    all_to_all x1, blocking collectives, on_device(): lax.all_to_all((mine + swapped).astype(BF16), 'space', 0, 0, tiled=True,...  12.4 us
    pallas_call x1, Pallas kernels, gram(): pl.pallas_call(functools.partial(gram_kernel, depth, per_step), in_specs=...  10.4 us
    pallas_call x1, Pallas kernels, modes_all(): pl.pallas_call(functools.partial(modes_kernel, slots), in_specs=[VMEM, VM...  10.1 us
    all_to_all x1, blocking collectives, on_device(): messages = lax.all_to_all(message, 'space', 0, 0, tiled=True)  9.63 us
    ppermute x2, waiting for transfers between devices, on_device(): arrived = [lax.ppermute(share, 'freq', mirror) for share in shares]  6.12 us
    ppermute x2, starting transfers between devices, on_device(): arrived = [lax.ppermute(share, 'freq', mirror) for share in shares]  5.55 us
    pallas_call x2, Pallas kernels, modes_part(): pl.pallas_call(functools.partial(part_kernel, begin, size), in_specs=[VME...  4.58 us
  transfers between devices with their start and end apart: 3, of which 2 were waited for; matrix products, arithmetic and copies ran while one was open for 0% of the time, Pallas kernels for 15%

profile of v3, /device:TPU:1, one launch (start us, length us, event | category | flops | bytes accessed | tf_op | source)
XLA Modules:
  0.0 85.8 jit_solution(2875641524058329621)
XLA Ops:
  0.6 0.0 copy-start.2
  0.6 0.0 copy-start.1
  0.7 10.4 %gram.1 = (f32[8,128,128]{2,1,0:T(8,128)S(1)}, f32[8,128,128]{2,1,0:T(8,128)S(1)}, bf16[16,3072,256]{2,1,0:T(8,128)(2,1)S(1)}) custom-call(bf16[16,3072,256]{2,1,0:T(8,128)(2,1)} %spectra.1, f32[1,3072]{1,0:T(1,128)} %bitcast.3), custom_call_target="tpu_custom_call" | custom-call | flops 6442450944 | bytes 25165824 | tf_op jit(solution)/shard_map/gram/pallas_call | solution.py:89
  11.0 1.5 %collective-permute-start = (f32[8,128,128]{2,1,0:T(8,128)S(1)}, f32[8,128,128]{2,1,0:T(8,128)S(1)}, u32[]{:S(2)}, u32[]{:S(2)}) collective-permute-start(f32[8,128,128]{2,1,0:T(8,128)S(1)} %get-tuple-element.11), channel_id=1, source_target_pairs={{0,1},{1,0},{2,3},{3,2},{4,5},{5,4},{6,7},{7,6},{8,9},{9,8},{10,11... | collective-permute-start | bytes 1572872 | tf_op jit(solution)/shard_map/ppermute | solution.py:402
  12.5 1.5 %collective-permute-done = f32[8,128,128]{2,1,0:T(8,128)S(1)} collective-permute-done((f32[8,128,128]{2,1,0:T(8,128)S(1)}, f32[8,128,128]{2,1,0:T(8,128)S(1)}, u32[]{:S(2)}, u32[]{:S(2)}) %collective-permute-start) | collective-permute-done | bytes 524320 | tf_op jit(solution)/shard_map/ppermute | solution.py:402
  14.0 0.1 add_convert_fusion
  14.1 12.4 %all_to_all.15.parts = bf16[8,128,128]{2,1,0:T(8,128)(2,1)S(1)} all-to-all(bf16[8,128,128]{2,1,0:T(8,128)(2,1)S(1)} %add_convert_fusion), channel_id=1, replica_groups={{0,2,4,6,8,10,12,14},{1,3,5,7,9,11,13,15},{16,18,20,22,24,26,28,30},{17..., dimensions={0} | all-to-all | bytes 524288 | tf_op jit(solution)/shard_map/all_to_all | solution.py:404
  26.5 0.0 copy-done.2
  26.5 4.2 %solve.1 = bf16[16,8,384]{2,1,0:T(8,128)(2,1)S(1)} custom-call(bf16[8,128,128]{2,1,0:T(8,128)(2,1)S(1)} %all_to_all.15.parts, s32[16]{0:T(128)S(1)} %copy-done.2), custom_call_target="tpu_custom_call" | custom-call | flops 8000000000 | bytes 262144 | tf_op jit(solution)/shard_map/solve/pallas_call | solution.py:178
  30.8 9.6 %all_to_all.16.messages = bf16[16,8,384]{2,1,0:T(8,128)(2,1)S(1)} all-to-all(bf16[16,8,384]{2,1,0:T(8,128)(2,1)S(1)} %solve.1), channel_id=1, replica_groups=mesh['freq'=8,'space'=16] {'space'}, dimensions={0} | all-to-all | bytes 196608 | tf_op jit(solution)/shard_map/all_to_all | solution.py:408
  40.4 0.0 copy-done.1
  40.4 0.0 copy-start
  40.4 1.7 %modes_part.2.rest_0_ = bf16[17,16,512]{2,1,0:T(8,128)(2,1)S(1)} custom-call(bf16[16,8,384]{2,1,0:T(8,128)(2,1)S(1)} %all_to_all.16.messages, s32[16]{0:T(128)S(1)} %copy-done.1, bf16[16,3072,256]{2,1,0:T(8,128)(2,1)S(1)} %get-tuple-element.12.resident), custom_call_target="tpu_custom_call" | custom-call | flops 2000000000 | bytes 4194304 | tf_op jit(solution)/shard_map/modes_part/pallas_call | solution.py:225
  42.2 5.5 %collective-permute-start.1 = (bf16[17,16,512]{2,1,0:T(8,128)(2,1)S(1)}, bf16[17,16,512]{2,1,0:T(8,128)(2,1)S(1)}, u32[]{:S(2)}, u32[]{:S(2)}) collective-permute-start(bf16[17,16,512]{2,1,0:T(8,128)(2,1)S(1)} %modes_part.2.rest_0_), channel_id=1, source_target_pairs={{0,112},{16,96},{32,80},{48,64},{64,48},{80,32},{96,16},{112,0},{1... | collective-permute-start | bytes 835592 | tf_op jit(solution)/shard_map/ppermute | solution.py:417
  47.7 2.8 %modes_part.3.after = bf16[16,16,1024]{2,1,0:T(8,128)(2,1)S(1)} custom-call(bf16[16,8,384]{2,1,0:T(8,128)(2,1)S(1)} %all_to_all.16.messages, s32[16]{0:T(128)S(1)} %copy-done.1, bf16[16,3072,256]{2,1,0:T(8,128)(2,1)S(1)} %get-tuple-element.12.resident, bf16[17,16,512]{2,1,0:T(8,128)(2,1)S(1)} %modes_part.2.rest_0_), custom_call_target="tpu_custom_call" | custom-call | flops 2000000000 | bytes 8388608 | tf_op jit(solution)/shard_map/modes_part/pallas_call | solution.py:225
  50.5 0.0 collective-permute-start.2
  50.5 0.0 copy-done
  50.6 10.1 %modes_all.1 = (bf16[16,16,3072]{2,1,0:T(8,128)(2,1)}, f32[8,16]{1,0:T(8,128)}, bf16[16,16,1536]{2,1,0:T(8,128)(2,1)S(1)}, bf16[16,16,1536]{2,1,0:T(8,128)(2,1)S(1)}) custom-call(bf16[16,8,384]{2,1,0:T(8,128)(2,1)S(1)} %all_to_all.16.messages, f32[1,3072]{1,0:T(1,128)S(1)} %bitcast.4, bf16[16,3072,256]{2,1,0:T(8,128)(2,1)S(1)} %get-tuple-element.12.resident, ...), custom_call_target="tpu_custom_call" | custom-call | flops 7000000000 | bytes 25165824 | tf_op jit(solution)/shard_map/modes_all/pallas_call | solution.py:275
  60.7 0.0 collective-permute-done.1.rest_0_
  60.7 6.1 %collective-permute-done.2.rest_1_ = bf16[16,16,1024]{2,1,0:T(8,128)(2,1)S(1)} collective-permute-done((bf16[16,16,1024]{2,1,0:T(8,128)(2,1)S(1)}, bf16[16,16,1024]{2,1,0:T(8,128)(2,1)S(1)}, u32[]{:S(2)}, u32[]{:S(2)}) %collective-permute-start.2) | collective-permute-done | bytes 524320 | tf_op jit(solution)/shard_map/ppermute | solution.py:417
  66.8 1.5 %cross_sums.1 = bf16[32,8,256]{2,1,0:T(8,128)(2,1)S(1)} custom-call(s32[16]{0:T(128)S(1)} %copy-done.1, bf16[16,16,1536]{2,1,0:T(8,128)(2,1)S(1)} %get-tuple-element.15.high, bf16[16,16,1536]{2,1,0:T(8,128)(2,1)S(1)} %get-tuple-element.16.low, bf16[17,16,512]{2,1,0:T(8,128)(2,1)S(1)} %collective-permute-done.1.rest_0_, ...), custom_call_target="tpu_custom_call" | custom-call | flops 2000000000 | bytes 1572864 | tf_op jit(solution)/shard_map/cross_sums/pallas_call | solution.py:354
  68.3 16.8 %all_to_all.17.parts = bf16[32,8,256]{2,1,0:T(8,128)(2,1)S(1)} all-to-all(bf16[32,8,256]{2,1,0:T(8,128)(2,1)S(1)} %cross_sums.1), channel_id=1, replica_groups={{0,1,2,3,4,5,6,7,8,9,10,11,12,13,14,15,112,113,114,115,116,117,118,119,..., dimensions={0} | all-to-all | bytes 262144 | tf_op jit(solution)/shard_map/all_to_all | solution.py:424
  85.0 0.7 finish.1
Async XLA Ops:
  0.6 25.9 %copy-start.2 = (s32[16]{0:T(128)S(1)}, s32[16]{0:T(128)}, u32[]{:S(2)}) copy-start(s32[16]{0:T(128)} %counts.1) | copy-start | bytes 196
  0.6 39.8 %copy-start.1 = (s32[16]{0:T(128)S(1)}, s32[16]{0:T(128)}, u32[]{:S(2)}) copy-start(s32[16]{0:T(128)} %own_partner.1) | copy-start | bytes 196
  11.0 3.0 %collective-permute-start = (f32[8,128,128]{2,1,0:T(8,128)S(1)}, f32[8,128,128]{2,1,0:T(8,128)S(1)}, u32[]{:S(2)}, u32[]{:S(2)}) collective-permute-start(f32[8,128,128]{2,1,0:T(8,128)S(1)} %get-tuple-element.11), channel_id=1, source_target_pairs={{0,1},{1,0},{2,3},{3,2},{4,5},{5,4},{6,7},{7,6},{8,9},{9,8},{10,11... | collective-permute-start | bytes 1572872 | tf_op jit(solution)/shard_map/ppermute | solution.py:402
  40.4 10.1 %copy-start = (f32[3072]{0:T(1024)S(1)}, f32[3072]{0:T(1024)}, u32[]{:S(2)}) copy-start(f32[3072]{0:T(1024)} %param.5) | copy-start | bytes 36868
  42.2 18.5 %collective-permute-start.1 = (bf16[17,16,512]{2,1,0:T(8,128)(2,1)S(1)}, bf16[17,16,512]{2,1,0:T(8,128)(2,1)S(1)}, u32[]{:S(2)}, u32[]{:S(2)}) collective-permute-start(bf16[17,16,512]{2,1,0:T(8,128)(2,1)S(1)} %modes_part.2.rest_0_), channel_id=1, source_target_pairs={{0,112},{16,96},{32,80},{48,64},{64,48},{80,32},{96,16},{112,0},{1... | collective-permute-start | bytes 835592 | tf_op jit(solution)/shard_map/ppermute | solution.py:417
  50.5 16.3 %collective-permute-start.2 = (bf16[16,16,1024]{2,1,0:T(8,128)(2,1)S(1)}, bf16[16,16,1024]{2,1,0:T(8,128)(2,1)S(1)}, u32[]{:S(2)}, u32[]{:S(2)}) collective-permute-start(bf16[16,16,1024]{2,1,0:T(8,128)(2,1)S(1)} %modes_part.3.after), channel_id=1, source_target_pairs={{0,112},{16,96},{32,80},{48,64},{64,48},{80,32},{96,16},{112,0},{1... | collective-permute-start | bytes 1572872 | tf_op jit(solution)/shard_map/ppermute | solution.py:417

commit v4 on v3

--- a/solution.py
+++ b/solution.py
@@ -110,10 +110,10 @@
         square = jnp.sum(ure * ure + uim * uim, axis=1, keepdims=True) + EPS
         pre = jnp.sum(ure * re + uim * im, axis=1, keepdims=True)
         pim = jnp.sum(ure * im - uim * re, axis=1, keepdims=True)
-        inverse = 1.0 / square
+        unit = lax.rsqrt(square)
+        inverse = unit * unit
         pre = pre * inverse
         pim = pim * inverse
-        unit = 1.0 / jnp.sqrt(square)
         re, im = (
             jnp.where(rows > k, re - pre * ure + pim * uim, jnp.where(rows == k, ure * unit, re)),
             jnp.where(rows > k, im - pre * uim - pim * ure, jnp.where(rows == k, uim * unit, im)),
@@ -121,8 +121,14 @@
     return (re, im)
 
 
-def solve_kernel(total, parts, counts, out):
+def solve_kernel(total, parts, counts, partner, out, table, kept_all, partners, sems):
     count, half, _ = parts.shape
+    small = (
+        pltpu.make_async_copy(counts, kept_all, sems.at[0]),
+        pltpu.make_async_copy(partner, partners, sems.at[1]),
+    )
+    for copy in small:
+        copy.start()
     summed = parts[0].astype(F32)
     for index in range(1, count):
         summed = summed + parts[index].astype(F32)
@@ -156,7 +162,9 @@
         re, im = orthonormal(*apply(re, im))
     image_re, image_im = apply(re, im)
     energy = jnp.sum(re * image_re + im * image_im, axis=1, keepdims=True)
-    kept = counts[lax.axis_index("space")]
+    for copy in small:
+        copy.wait()
+    kept = kept_all[lax.axis_index("space")]
     ranks, lanes = iotas((KMAX, half))
     scale = jnp.where(ranks[:, :1] < kept, 1.0 / jnp.sqrt(energy + EPS), 0.0)
     first = energy.astype(BF16)
@@ -171,19 +179,33 @@
     message = jnp.concatenate([re * scale, im * scale, tail], axis=1).astype(BF16)
     for index in range(out.shape[0]):
         out[index] = message
-
-
-def solve(parts, counts, total):
+    _, lanes = iotas(table.shape)
+    value = jnp.zeros(table.shape, jnp.int32)
+    for index in range(partners.shape[0]):
+        value = jnp.where(lanes // (2 * KMAX) == index, partners[index], value)
+    table[...] = value.astype(F32).astype(BF16)
+
+
+def solve(parts, counts, partner, total, lanes):
     _, half, _ = parts.shape
+    groups = counts.shape[0]
     return pl.pallas_call(
         functools.partial(solve_kernel, total),
-        in_specs=[VMEM, SMEM],
-        out_specs=VMEM,
-        out_shape=jax.ShapeDtypeStruct((counts.shape[0], KMAX, 3 * half), BF16),
+        in_specs=[VMEM, HBM, HBM],
+        out_specs=(VMEM, VMEM),
+        out_shape=(
+            jax.ShapeDtypeStruct((groups, KMAX, 3 * half), BF16),
+            jax.ShapeDtypeStruct((2 * KMAX, lanes), BF16),
+        ),
+        scratch_shapes=[
+            pltpu.SMEM((groups,), jnp.int32),
+            pltpu.SMEM((groups,), jnp.int32),
+            pltpu.SemaphoreType.DMA((2,)),
+        ],
         compiler_params=kernel_params(8),
         cost_estimate=cost(8_000_000_000, parts.size * 2),
         name="solve",
-    )(parts, counts)
+    )(parts, counts, partner)
 
 
 def coefficient_rows(message, half):
@@ -204,7 +226,7 @@
     ).astype(BF16)
 
 
-def part_kernel(begin, size, messages, partner, resident, *rest):
+def part_kernel(begin, size, messages, table, resident, *rest):
     out = rest[-1]
     groups, points, width = resident.shape
     start = pl.multiple_of((1 - kept_half()) * (points // 2) + begin, 128)
@@ -212,31 +234,27 @@
         rows = coefficient_rows(messages[index], width // 2)
         out[index] = project(rows, resident[index, pl.ds(start, size)])
     if out.shape[0] > groups:
-        _, lanes = iotas((2 * KMAX, size))
-        table = jnp.zeros((2 * KMAX, size), jnp.int32)
-        for index in range(groups):
-            table = jnp.where(lanes // (2 * KMAX) == index, partner[index], table)
-        out[groups] = table.astype(F32).astype(BF16)
-
-
-def modes_part(messages, partner, resident, begin, size, *after):
+        out[groups] = table[...]
+
+
+def modes_part(messages, table, resident, begin, size, planes, *after):
     groups, _, width = resident.shape
-    planes = groups if after else groups + 1
     return pl.pallas_call(
         functools.partial(part_kernel, begin, size),
-        in_specs=[VMEM, SMEM, VMEM] + [ANY] * len(after),
+        in_specs=[VMEM, VMEM, VMEM] + [ANY] * len(after),
         out_specs=VMEM,
         out_shape=jax.ShapeDtypeStruct((planes, 2 * KMAX, size), BF16),
         compiler_params=kernel_params(8),
         cost_estimate=cost(2_000_000_000, groups * size * width * 2),
         name="modes_part",
-    )(messages, partner, resident, *after)
-
-
-def modes_kernel(slots, messages, weight, resident, after, out, energy, high, low, made, put):
+    )(messages, table, resident, *after)
+
+
+def modes_kernel(slots, per_turn, messages, weight, resident, after, out, energy, high, low, made, put):
     groups, points, width = resident.shape
     part = points // 2
-    start = pl.multiple_of(kept_half() * part, 128)
+    upper = kept_half() == 1
+    scale = weight[:, pl.ds(pl.multiple_of(kept_half() * part, 128), part)]
 
     def store(step, slot):
         return pltpu.make_async_copy(made.at[slot], out.at[step], put.at[slot])
@@ -248,22 +266,30 @@
         value = jnp.where(lanes == index, column, value)
     energy[...] = value
 
-    def body(step, carry):
-        slot = lax.rem(step, slots)
-
-        @pl.when(step >= slots)
-        def _():
-            store(step - slots, slot).wait()
-
-        made[slot] = project(coefficient_rows(messages[step], width // 2), resident[step])
-        store(step, slot).start()
-        own = made[slot, :, pl.ds(start, part)].astype(F32) * weight[:, pl.ds(start, part)]
-        top = own.astype(BF16)
-        high[step] = top
-        low[step] = (own - top.astype(F32)).astype(BF16)
+    def body(turn, carry):
+        for offset in range(per_turn):
+            step = turn * per_turn + offset
+            slot = lax.rem(step, slots)
+
+            @pl.when(step >= slots)
+            def _():
+                store(step - slots, slot).wait()
+
+        for offset in range(per_turn):
+            step = turn * per_turn + offset
+            slot = lax.rem(step, slots)
+            value = project(coefficient_rows(messages[step], width // 2), resident[step])
+            made[slot] = value
+            own = jnp.where(upper, value[:, part:], value[:, :part]).astype(F32) * scale
+            top = own.astype(BF16)
+            high[step] = top
+            low[step] = (own - top.astype(F32)).astype(BF16)
+        for offset in range(per_turn):
+            step = turn * per_turn + offset
+            store(step, lax.rem(step, slots)).start()
         return carry
 
-    lax.fori_loop(0, groups, body, 0)
+    lax.fori_loop(0, groups // per_turn, body, 0)
     for slot in range(slots):
         store(groups - slots + slot, slot).wait()
 
@@ -273,7 +299,7 @@
     slots = 4
     weighted = jax.ShapeDtypeStruct((groups, 2 * KMAX, points // 2), BF16)
     return pl.pallas_call(
-        functools.partial(modes_kernel, slots),
+        functools.partial(modes_kernel, slots, 2),
         in_specs=[VMEM, VMEM, VMEM, ANY],
         out_specs=(HBM, VMEM, VMEM, VMEM),
         out_shape=(
@@ -292,15 +318,6 @@
     )(messages, weight, resident, after)
 
 
-def lane_table(partner, rank):
-    groups = partner.shape[0]
-    _, lanes = iotas((KMAX, groups * rank))
-    table = jnp.zeros((KMAX, groups * rank), jnp.int32)
-    for index in range(groups):
-        table = jnp.where(lanes // rank == index, partner[index], table)
-    return table
-
-
 def chosen(cross, lane_partner, groups):
     rank = 2 * KMAX
     top = jnp.zeros((KMAX, groups * rank), F32)
@@ -318,23 +335,46 @@
     )
 
 
-def cross_kernel(own_partner, high, low, *rest):
+def products(high, low, share, begin):
+    groups, rank, _ = high.shape
+    rows, size = (groups * rank, share.shape[2])
+    other = share[:groups].reshape(rows, size)
+    total = None
+    for own in (high, low):
+        mine = own[:, :, begin : begin + size].reshape(rows, size)
+        part = lax.dot_general(mine, other, (((1,), (1,)), ((), ())), preferred_element_type=F32)
+        total = part if total is None else total + part
+    return total
+
+
+def early_kernel(begins, high, low, *rest):
     arrived, out = (rest[:-1], rest[-1])
+    value = products(high, low, arrived[0], begins[0])
+    for share, begin in zip(arrived[1:], begins[1:]):
+        value = value + products(high, low, share, begin)
+    out[...] = value
+
+
+def early_products(high, low, arrived, begins):
+    rows = high.shape[0] * high.shape[1]
+    return pl.pallas_call(
+        functools.partial(early_kernel, begins),
+        in_specs=[VMEM] * (2 + len(arrived)),
+        out_specs=VMEM,
+        out_shape=jax.ShapeDtypeStruct((rows, rows), F32),
+        compiler_params=kernel_params(8),
+        cost_estimate=cost(2_000_000_000, 4 * high.size),
+        name="early_products",
+    )(high, low, *arrived)
+
+
+def cross_kernel(begin, early, table, high, low, share, out):
     groups, rank, part = high.shape
     rows = groups * rank
-    cross = jnp.zeros((rows, rows), F32)
-    begin = 0
-    for share in arrived:
-        size = share.shape[2]
-        other = share[:groups].reshape(rows, size)
-        for own in (high, low):
-            mine = own[:, :, begin : begin + size].reshape(rows, size)
-            cross = cross + lax.dot_general(
-                mine, other, (((1,), (1,)), ((), ())), preferred_element_type=F32
-            )
-        begin += size
-    other_table = arrived[0][groups, :KMAX, :rows].astype(F32).astype(jnp.int32)
-    own_value = chosen(cross.T, lane_table(own_partner, rank), groups)
+    cross = early[...] + products(high, low, share, begin)
+    own_table = table[:KMAX, :rows].astype(F32).astype(jnp.int32)
+    other_table = share[groups, :KMAX, :rows].astype(F32).astype(jnp.int32)
+    own_value = chosen(cross.T, own_table, groups)
     other_value = chosen(cross, other_table, groups)
     both = jnp.concatenate([own_value, other_value], axis=0).astype(BF16)
     source, target = iotas((rows, rows))
@@ -349,17 +389,17 @@
         out[half + index] = upper
 
 
-def cross_sums(own_partner, high, low, arrived, members):
+def cross_sums(early, table, high, low, share, begin, members):
     groups, rank, part = high.shape
     return pl.pallas_call(
-        cross_kernel,
-        in_specs=[SMEM] + [VMEM] * (2 + len(arrived)),
+        functools.partial(cross_kernel, begin),
+        in_specs=[VMEM] * 5,
         out_specs=VMEM,
         out_shape=jax.ShapeDtypeStruct((members, KMAX, groups * rank), BF16),
-        compiler_params=kernel_params(16),
+        compiler_params=kernel_params(8),
         cost_estimate=cost(2_000_000_000, 4 * high.size),
         name="cross_sums",
-    )(own_partner, high, low, *arrived)
+    )(early, table, high, low, share)
 
 
 def finish_kernel(total, parts, out):
@@ -404,25 +444,29 @@
     parts = lax.all_to_all(
         (mine + swapped).astype(BF16), "space", 0, 0, tiled=True, axis_index_groups=chips
     )
-    message = solve(parts, counts, total)
+    part = points // 2
+    sizes = (part // 4, part // 2, part // 4)
+    begins = (0, part // 4, 3 * part // 4)
+    in_hbm = [pltpu.with_memory_space_constraint(array, pltpu.HBM) for array in (counts, partner)]
+    message, table = solve(parts, *in_hbm, total, sizes[-1])
     messages = lax.all_to_all(message, "space", 0, 0, tiled=True)
 
-    part = points // 2
-    cut = part // 3
-    first_share = modes_part(messages, partner, resident, 0, cut)
-    shares = [
-        first_share,
-        modes_part(messages, partner, resident, cut, part - cut, first_share),
-    ]
+    shares = []
+    for begin, size in zip(begins, sizes):
+        planes = groups + 1 if size + begin == part else groups
+        shares.append(modes_part(messages, table, resident, begin, size, planes, *shares[-1:]))
     arrived = [lax.ppermute(share, "freq", mirror) for share in shares]
     modes, energy, high, low = modes_all(messages, weight_row, resident, shares[-1])
+    early = early_products(high, low, arrived[:-1], begins[:-1])
 
     members = [
         [group * n_space + index for group in (low_group, n_freq - 1 - low_group) for index in range(n_space)]
         for low_group in range(n_freq // 2)
     ]
     gathered = lax.all_to_all(
-        cross_sums(partner, high, low, arrived, 2 * n_space),
+        cross_sums(
+            early, table, high, low, arrived[-1], begins[-1], 2 * n_space
+        ),
         ("freq", "space"),
         0,
         0,

time: 86 us -> 83.6 us (0.972)
  starting transfers between devices: 7.01 us -> 12.1 us
  waiting for transfers between devices: 7.66 us -> 3.93 us
  Pallas kernels: 31.5 us -> 28.4 us
    ppermute x2 -> x3, starting transfers between devices: 5.55 us -> 10.7 us  [on_device(): arrived = [lax.ppermute(share, 'freq', mirror) for share in shares]]
    ppermute x2 -> x3, waiting for transfers between devices: 6.12 us -> 2.4 us  [on_device(): arrived = [lax.ppermute(share, 'freq', mirror) for share in shares]]
    pallas_call x3 -> x4, Pallas kernels: 15.8 us -> 13.7 us  [the longest x1 8.96 us: modes_all(): pl.pallas_call(functools.partial(modes_kernel, slots, 2), in_specs=[VMEM,...]
    pallas_call x2 -> x3, Pallas kernels: 4.58 us -> 3.57 us  [modes_part(): pl.pallas_call(functools.partial(part_kernel, begin, size), in_specs=[VME...]
  transfers between devices with their start and end apart: 3 -> 4, of which waited for: 2 -> 2; matrix products, arithmetic and copies ran while one was open for 0% -> 0% of each run, Pallas kernels for 15% -> 15%
where the time goes in v4:
time: 83.6 us; the launch traced here: 83.4 us
  blocking collectives  38.2 us (46%)
  Pallas kernels  28.4 us (34%)
  starting transfers between devices  12.1 us (14%)
  waiting for transfers between devices  3.93 us (5%)
    all_to_all x1, blocking collectives, on_device(): lax.all_to_all(cross_sums(early, table, high, low, arrived[-1], begins[-1...  16.1 us
    all_to_all x1, blocking collectives, on_device(): lax.all_to_all((mine + swapped).astype(BF16), 'space', 0, 0, tiled=True,...  12.4 us
    ppermute x3, starting transfers between devices, on_device(): arrived = [lax.ppermute(share, 'freq', mirror) for share in shares]  10.7 us
    pallas_call x1, Pallas kernels, gram(): pl.pallas_call(functools.partial(gram_kernel, depth, per_step), in_specs=...  10.4 us
    all_to_all x1, blocking collectives, on_device(): messages = lax.all_to_all(message, 'space', 0, 0, tiled=True)  9.63 us
    pallas_call x1, Pallas kernels, modes_all(): pl.pallas_call(functools.partial(modes_kernel, slots, 2), in_specs=[VMEM,...  8.96 us
    pallas_call x1, Pallas kernels, solve(): pl.pallas_call(functools.partial(solve_kernel, total), in_specs=[VMEM, HB...  3.59 us
    pallas_call x3, Pallas kernels, modes_part(): pl.pallas_call(functools.partial(part_kernel, begin, size), in_specs=[VME...  3.57 us
  transfers between devices with their start and end apart: 4, of which 2 were waited for; matrix products, arithmetic and copies ran while one was open for 0% of the time, Pallas kernels for 15%

profile of v4, /device:TPU:1, one launch (start us, length us, event | category | flops | bytes accessed | tf_op | source)
XLA Modules:
  0.0 83.4 jit_solution(14821566077193346982)
XLA Ops:
  0.6 10.4 %gram.1 = (f32[8,128,128]{2,1,0:T(8,128)S(1)}, f32[8,128,128]{2,1,0:T(8,128)S(1)}, bf16[16,3072,256]{2,1,0:T(8,128)(2,1)S(1)}) custom-call(bf16[16,3072,256]{2,1,0:T(8,128)(2,1)} %spectra.1, f32[1,3072]{1,0:T(1,128)} %bitcast.3), custom_call_target="tpu_custom_call" | custom-call | flops 6442450944 | bytes 25165824 | tf_op jit(solution)/shard_map/gram/pallas_call | solution.py:89
  11.0 1.5 %collective-permute-start = (f32[8,128,128]{2,1,0:T(8,128)S(1)}, f32[8,128,128]{2,1,0:T(8,128)S(1)}, u32[]{:S(2)}, u32[]{:S(2)}) collective-permute-start(f32[8,128,128]{2,1,0:T(8,128)S(1)} %get-tuple-element.13), channel_id=1, source_target_pairs={{0,1},{1,0},{2,3},{3,2},{4,5},{5,4},{6,7},{7,6},{8,9},{9,8},{10,11... | collective-permute-start | bytes 1572872 | tf_op jit(solution)/shard_map/ppermute | solution.py:442
  12.5 1.5 %collective-permute-done = f32[8,128,128]{2,1,0:T(8,128)S(1)} collective-permute-done((f32[8,128,128]{2,1,0:T(8,128)S(1)}, f32[8,128,128]{2,1,0:T(8,128)S(1)}, u32[]{:S(2)}, u32[]{:S(2)}) %collective-permute-start) | collective-permute-done | bytes 524320 | tf_op jit(solution)/shard_map/ppermute | solution.py:442
  14.0 0.1 add_convert_fusion
  14.1 12.4 %all_to_all.15.parts = bf16[8,128,128]{2,1,0:T(8,128)(2,1)S(1)} all-to-all(bf16[8,128,128]{2,1,0:T(8,128)(2,1)S(1)} %add_convert_fusion), channel_id=1, replica_groups={{0,2,4,6,8,10,12,14},{1,3,5,7,9,11,13,15},{16,18,20,22,24,26,28,30},{17..., dimensions={0} | all-to-all | bytes 524288 | tf_op jit(solution)/shard_map/all_to_all | solution.py:444
  26.5 3.6 %solve.1 = (bf16[16,8,384]{2,1,0:T(8,128)(2,1)S(1)}, bf16[16,384]{1,0:T(8,128)(2,1)S(1)}) custom-call(bf16[8,128,128]{2,1,0:T(8,128)(2,1)S(1)} %all_to_all.15.parts, s32[16]{0:T(128)} %counts.1, s32[16]{0:T(128)} %partner.1), custom_call_target="tpu_custom_call" | custom-call | flops 8000000000 | bytes 262144 | tf_op jit(solution)/shard_map/solve/pallas_call | solution.py:192
  30.1 9.6 %all_to_all.16.messages = bf16[16,8,384]{2,1,0:T(8,128)(2,1)S(1)} all-to-all(bf16[16,8,384]{2,1,0:T(8,128)(2,1)S(1)} %get-tuple-element.14), channel_id=1, replica_groups=mesh['freq'=8,'space'=16] {'space'}, dimensions={0} | all-to-all | bytes 196608 | tf_op jit(solution)/shard_map/all_to_all | solution.py:452
  39.7 0.9 %modes_part.3.rest_0_ = bf16[16,16,384]{2,1,0:T(8,128)(2,1)S(1)} custom-call(bf16[16,8,384]{2,1,0:T(8,128)(2,1)S(1)} %all_to_all.16.messages, bf16[16,384]{1,0:T(8,128)(2,1)S(1)} %get-tuple-element.16.table, bf16[16,3072,256]{2,1,0:T(8,128)(2,1)S(1)} %get-tuple-element.15.resident), custom_call_target="tpu_custom_call" | custom-call | flops 2000000000 | bytes 3145728 | tf_op jit(solution)/shard_map/modes_part/pallas_call | solution.py:242
  40.7 0.0 copy-start
  40.7 5.5 %collective-permute-start.1 = (bf16[16,16,384]{2,1,0:T(8,128)(2,1)S(1)}, bf16[16,16,384]{2,1,0:T(8,128)(2,1)S(1)}, u32[]{:S(2)}, u32[]{:S(2)}) collective-permute-start(bf16[16,16,384]{2,1,0:T(8,128)(2,1)S(1)} %modes_part.3.rest_0_), channel_id=1, source_target_pairs={{0,112},{16,96},{32,80},{48,64},{64,48},{80,32},{96,16},{112,0},{1... | collective-permute-start | bytes 589832 | tf_op jit(solution)/shard_map/ppermute | solution.py:458
  46.2 1.7 %modes_part.4.rest_0_ = bf16[16,16,768]{2,1,0:T(8,128)(2,1)S(1)} custom-call(bf16[16,8,384]{2,1,0:T(8,128)(2,1)S(1)} %all_to_all.16.messages, bf16[16,384]{1,0:T(8,128)(2,1)S(1)} %get-tuple-element.16.table, bf16[16,3072,256]{2,1,0:T(8,128)(2,1)S(1)} %get-tuple-element.15.resident, bf16[16,16,384]{2,1,0:T(8,128)(2,1)S(1)} %modes_part.3.rest_0_), custom_call_target="tpu_custom_call" | custom-call | flops 2000000000 | bytes 6291456 | tf_op jit(solution)/shard_map/modes_part/pallas_call | solution.py:242
  47.9 0.0 collective-permute-start.2
  48.0 0.9 %modes_part.5.after = bf16[17,16,384]{2,1,0:T(8,128)(2,1)S(1)} custom-call(bf16[16,8,384]{2,1,0:T(8,128)(2,1)S(1)} %all_to_all.16.messages, bf16[16,384]{1,0:T(8,128)(2,1)S(1)} %get-tuple-element.16.table, bf16[16,3072,256]{2,1,0:T(8,128)(2,1)S(1)} %get-tuple-element.15.resident, bf16[16,16,768]{2,1,0:T(8,128)(2,1)S(1)} %modes_part.4.rest_0_), custom_call_target="tpu_custom_call" | custom-call | flops 2000000000 | bytes 3145728 | tf_op jit(solution)/shard_map/modes_part/pallas_call | solution.py:242
  48.9 5.1 %collective-permute-start.3 = (bf16[17,16,384]{2,1,0:T(8,128)(2,1)S(1)}, bf16[17,16,384]{2,1,0:T(8,128)(2,1)S(1)}, u32[]{:S(2)}, u32[]{:S(2)}) collective-permute-start(bf16[17,16,384]{2,1,0:T(8,128)(2,1)S(1)} %modes_part.5.after), channel_id=1, source_target_pairs={{0,112},{16,96},{32,80},{48,64},{64,48},{80,32},{96,16},{112,0},{1... | collective-permute-start | bytes 626696 | tf_op jit(solution)/shard_map/ppermute | solution.py:458
  54.0 0.0 copy-done
  54.0 9.0 %modes_all.1 = (bf16[16,16,3072]{2,1,0:T(8,128)(2,1)}, f32[8,16]{1,0:T(8,128)}, bf16[16,16,1536]{2,1,0:T(8,128)(2,1)S(1)}, bf16[16,16,1536]{2,1,0:T(8,128)(2,1)S(1)}) custom-call(bf16[16,8,384]{2,1,0:T(8,128)(2,1)S(1)} %all_to_all.16.messages, f32[1,3072]{1,0:T(1,128)S(1)} %bitcast.4, bf16[16,3072,256]{2,1,0:T(8,128)(2,1)S(1)} %get-tuple-element.15.resident, ...), custom_call_target="tpu_custom_call" | custom-call | flops 7000000000 | bytes 25165824 | tf_op jit(solution)/shard_map/modes_all/pallas_call | solution.py:301
  63.0 0.0 collective-permute-done.1.rest_0_
  63.0 0.0 collective-permute-done.2.rest_1_
  63.0 0.5 early_products.1.early
  63.5 2.4 %collective-permute-done.3.share = bf16[17,16,384]{2,1,0:T(8,128)(2,1)S(1)} collective-permute-done((bf16[17,16,384]{2,1,0:T(8,128)(2,1)S(1)}, bf16[17,16,384]{2,1,0:T(8,128)(2,1)S(1)}, u32[]{:S(2)}, u32[]{:S(2)}) %collective-permute-start.3) | collective-permute-done | bytes 208928 | tf_op jit(solution)/shard_map/ppermute | solution.py:458
  65.9 0.6 cross_sums.1
  66.5 16.1 %all_to_all.17.parts = bf16[32,8,256]{2,1,0:T(8,128)(2,1)S(1)} all-to-all(bf16[32,8,256]{2,1,0:T(8,128)(2,1)S(1)} %cross_sums.1), channel_id=1, replica_groups={{0,1,2,3,4,5,6,7,8,9,10,11,12,13,14,15,112,113,114,115,116,117,118,119,..., dimensions={0} | all-to-all | bytes 262144 | tf_op jit(solution)/shard_map/all_to_all | solution.py:466
  82.7 0.7 finish.1
Async XLA Ops:
  11.0 3.0 %collective-permute-start = (f32[8,128,128]{2,1,0:T(8,128)S(1)}, f32[8,128,128]{2,1,0:T(8,128)S(1)}, u32[]{:S(2)}, u32[]{:S(2)}) collective-permute-start(f32[8,128,128]{2,1,0:T(8,128)S(1)} %get-tuple-element.13), channel_id=1, source_target_pairs={{0,1},{1,0},{2,3},{3,2},{4,5},{5,4},{6,7},{7,6},{8,9},{9,8},{10,11... | collective-permute-start | bytes 1572872 | tf_op jit(solution)/shard_map/ppermute | solution.py:442
  40.7 13.3 %copy-start = (f32[3072]{0:T(1024)S(1)}, f32[3072]{0:T(1024)}, u32[]{:S(2)}) copy-start(f32[3072]{0:T(1024)} %param.5) | copy-start | bytes 36868
  40.7 22.3 %collective-permute-start.1 = (bf16[16,16,384]{2,1,0:T(8,128)(2,1)S(1)}, bf16[16,16,384]{2,1,0:T(8,128)(2,1)S(1)}, u32[]{:S(2)}, u32[]{:S(2)}) collective-permute-start(bf16[16,16,384]{2,1,0:T(8,128)(2,1)S(1)} %modes_part.3.rest_0_), channel_id=1, source_target_pairs={{0,112},{16,96},{32,80},{48,64},{64,48},{80,32},{96,16},{112,0},{1... | collective-permute-start | bytes 589832 | tf_op jit(solution)/shard_map/ppermute | solution.py:458
  47.9 15.0 %collective-permute-start.2 = (bf16[16,16,768]{2,1,0:T(8,128)(2,1)S(1)}, bf16[16,16,768]{2,1,0:T(8,128)(2,1)S(1)}, u32[]{:S(2)}, u32[]{:S(2)}) collective-permute-start(bf16[16,16,768]{2,1,0:T(8,128)(2,1)S(1)} %modes_part.4.rest_0_), channel_id=1, source_target_pairs={{0,112},{16,96},{32,80},{48,64},{64,48},{80,32},{96,16},{112,0},{1... | collective-permute-start | bytes 1179656 | tf_op jit(solution)/shard_map/ppermute | solution.py:458
  48.9 17.0 %collective-permute-start.3 = (bf16[17,16,384]{2,1,0:T(8,128)(2,1)S(1)}, bf16[17,16,384]{2,1,0:T(8,128)(2,1)S(1)}, u32[]{:S(2)}, u32[]{:S(2)}) collective-permute-start(bf16[17,16,384]{2,1,0:T(8,128)(2,1)S(1)} %modes_part.5.after), channel_id=1, source_target_pairs={{0,112},{16,96},{32,80},{48,64},{64,48},{80,32},{96,16},{112,0},{1... | collective-permute-start | bytes 626696 | tf_op jit(solution)/shard_map/ppermute | solution.py:458

commit v5 on v4

--- a/solution.py
+++ b/solution.py
@@ -37,69 +37,108 @@
     )
 
 
-def gram_kernel(depth, per_step, spectra, weight, mine, other, resident, scale, sems, scale_sem):
+def hermitian(block, scale):
+    half = block.shape[1] // 2
+    rows, cols = iotas((half, half))
+    weighted = (block.T.astype(F32) * scale).astype(BF16)
+    moment = jnp.dot(weighted, block, preferred_element_type=F32)
+    real = moment[:half, :half] + moment[half:, half:]
+    imag = moment[:half, half:] - moment[half:, :half]
+    return jnp.where(cols >= rows, real, imag)
+
+
+def on_core():
+    return lax.rem(lax.axis_index("space"), 2)
+
+
+def pair_copy(spectra, held, sems, side, pair, slot):
+    begin = side * (spectra.shape[0] // 2) + 2 * pair
+    return pltpu.make_async_copy(
+        spectra.at[pl.ds(begin, 2)], held.at[pl.ds(2 * slot, 2)], sems.at[slot]
+    )
+
+
+def gram_other_kernel(spectra, weight, sums, theirs, ahead, scale, sems, ahead_sems, scale_sem):
+    pairs = theirs.shape[0] // 2
+    early = ahead.shape[0] // 2
+    copies = [pair_copy(spectra, theirs, sems, 1 - on_core(), p, p) for p in range(pairs)]
+    copies += [pair_copy(spectra, ahead, ahead_sems, on_core(), p, p) for p in range(early)]
+    due = {0: (2, 3), 1: (4,), 2: (5,)}
+    copies[0].start()
+    scale_copy = pltpu.make_async_copy(weight, scale, scale_sem)
+    scale_copy.start()
+    copies[1].start()
+    scale_copy.wait()
+    for pair in range(pairs):
+        copies[pair].wait()
+        for later in due.get(pair, ()):
+            copies[later].start()
+        for index in range(2 * pair, 2 * pair + 2):
+            sums[index] = hermitian(theirs[index], scale[...])
+    for copy in copies[pairs:]:
+        copy.wait()
+
+
+def gram_mine_kernel(ahead, spectra, weight, sums, rest, scale, sems, scale_sem):
+    early, late = (ahead.shape[0] // 2, rest.shape[0] // 2)
+    copies = [pair_copy(spectra, rest, sems, on_core(), early + p, p) for p in range(late)]
+    for copy in copies:
+        copy.start()
+    scale_copy = pltpu.make_async_copy(weight, scale, scale_sem)
+    scale_copy.start()
+    scale_copy.wait()
+    for index in range(2 * early):
+        sums[index] = hermitian(ahead[index], scale[...])
+    for pair in range(late):
+        copies[pair].wait()
+        for index in range(2 * pair, 2 * pair + 2):
+            sums[2 * early + index] = hermitian(rest[index], scale[...])
+
+
+def gram_other(spectra, weight):
     groups, points, width = spectra.shape
     half = width // 2
-    steps = groups // per_step
-    rows, cols = iotas((half, half))
-    south = lax.rem(lax.axis_index("space"), 2) == 0
-
-    def fetch(step):
-        part = pl.ds(step * per_step, per_step)
-        return pltpu.make_async_copy(spectra.at[part], resident.at[part], sems.at[step])
-
-    fetch(0).start()
-    scale_copy = pltpu.make_async_copy(weight, scale, scale_sem)
-    scale_copy.start()
-    for step in range(1, depth):
-        fetch(step).start()
-    scale_copy.wait()
-
-    def hermitian(index):
-        block = resident[index]
-        weighted = (block.T.astype(F32) * scale[...]).astype(BF16)
-        moment = jnp.dot(weighted, block, preferred_element_type=F32)
-        real = moment[:half, :half] + moment[half:, half:]
-        imag = moment[:half, half:] - moment[half:, :half]
-        return jnp.where(cols >= rows, real, imag)
-
-    def body(step, carry):
-        fetch(step).wait()
-
-        @pl.when(step + depth < steps)
-        def _():
-            fetch(step + depth).start()
-
-        for index in range(0, per_step, 2):
-            even = hermitian(step * per_step + index)
-            odd = hermitian(step * per_step + index + 1)
-            place = (step * per_step + index) // 2
-            mine[place] = jnp.where(south, even, odd)
-            other[place] = jnp.where(south, odd, even)
-        return carry
-
-    lax.fori_loop(0, steps, body, 0)
-
-
-def gram(spectra, weight):
-    groups, points, width = spectra.shape
-    half = width // 2
-    depth, per_step = (2, 2)
-    sums = jax.ShapeDtypeStruct((groups // 2, half, half), F32)
-    return pl.pallas_call(
-        functools.partial(gram_kernel, depth, per_step),
+    return pl.pallas_call(
+        gram_other_kernel,
         in_specs=[HBM, HBM],
         out_specs=(VMEM, VMEM, VMEM),
-        out_shape=(sums, sums, pltpu.VMEM((groups, points, width), BF16)),
+        out_shape=(
+            jax.ShapeDtypeStruct((groups // 2, half, half), F32),
+            pltpu.VMEM((groups // 2, points, width), BF16),
+            pltpu.VMEM((groups // 4, points, width), BF16),
+        ),
         scratch_shapes=[
             pltpu.VMEM((1, points), F32),
-            pltpu.SemaphoreType.DMA((groups // per_step,)),
+            pltpu.SemaphoreType.DMA((groups // 4,)),
+            pltpu.SemaphoreType.DMA((groups // 8,)),
             pltpu.SemaphoreType.DMA,
         ],
         compiler_params=kernel_params(16),
-        cost_estimate=cost(2 * groups * points * width * width, groups * points * width * 2),
-        name="gram",
+        cost_estimate=cost(groups * points * width * width, groups * points * width),
+        name="gram_other",
     )(spectra, weight)
+
+
+def gram_mine(ahead, spectra, weight):
+    groups, points, width = spectra.shape
+    half = width // 2
+    return pl.pallas_call(
+        gram_mine_kernel,
+        in_specs=[VMEM, HBM, HBM],
+        out_specs=(VMEM, VMEM),
+        out_shape=(
+            jax.ShapeDtypeStruct((groups // 2, half, half), F32),
+            pltpu.VMEM((groups // 4, points, width), BF16),
+        ),
+        scratch_shapes=[
+            pltpu.VMEM((1, points), F32),
+            pltpu.SemaphoreType.DMA((groups // 8,)),
+            pltpu.SemaphoreType.DMA,
+        ],
+        compiler_params=kernel_params(16),
+        cost_estimate=cost(groups * points * width * width, groups * points * width),
+        name="gram_mine",
+    )(ahead, spectra, weight)
 
 
 def orthonormal(re, im):
@@ -164,7 +203,8 @@
     energy = jnp.sum(re * image_re + im * image_im, axis=1, keepdims=True)
     for copy in small:
         copy.wait()
-    kept = kept_all[lax.axis_index("space")]
+    place = lax.axis_index("space")
+    kept = kept_all[lax.rem(place, 2) * (kept_all.shape[0] // 2) + place // 2]
     ranks, lanes = iotas((KMAX, half))
     scale = jnp.where(ranks[:, :1] < kept, 1.0 / jnp.sqrt(energy + EPS), 0.0)
     first = energy.astype(BF16)
@@ -208,6 +248,15 @@
     )(parts, counts, partner)
 
 
+def place_of(index, groups):
+    return 2 * (index % (groups // 2)) + index // (groups // 2)
+
+
+def held_parts(theirs, ahead, rest):
+    core = on_core()
+    return ((theirs, 1 - core, 0), (ahead, core, 0), (rest, core, ahead.shape[0]))
+
+
 def coefficient_rows(message, half):
     part_re = message[:, :half]
     part_im = message[:, half : 2 * half]
@@ -226,81 +275,91 @@
     ).astype(BF16)
 
 
-def part_kernel(begin, size, messages, table, resident, *rest):
-    out = rest[-1]
-    groups, points, width = resident.shape
+def part_kernel(begin, size, messages, table, theirs, ahead, rest, *more):
+    out = more[-1]
+    groups = messages.shape[0]
+    _, points, width = theirs.shape
     start = pl.multiple_of((1 - kept_half()) * (points // 2) + begin, 128)
-    for index in range(groups):
-        rows = coefficient_rows(messages[index], width // 2)
-        out[index] = project(rows, resident[index, pl.ds(start, size)])
+    for held, side, first in held_parts(theirs, ahead, rest):
+        for index in range(held.shape[0]):
+            rows = coefficient_rows(messages[2 * (first + index) + side], width // 2)
+            target = side * (groups // 2) + first + index
+            out[target] = project(rows, held[index, pl.ds(start, size)])
     if out.shape[0] > groups:
         out[groups] = table[...]
 
 
-def modes_part(messages, table, resident, begin, size, planes, *after):
-    groups, _, width = resident.shape
+def modes_part(messages, table, held, begin, size, planes, *after):
+    groups = messages.shape[0]
+    width = held[0].shape[2]
     return pl.pallas_call(
         functools.partial(part_kernel, begin, size),
-        in_specs=[VMEM, VMEM, VMEM] + [ANY] * len(after),
+        in_specs=[VMEM] * 5 + [ANY] * len(after),
         out_specs=VMEM,
         out_shape=jax.ShapeDtypeStruct((planes, 2 * KMAX, size), BF16),
         compiler_params=kernel_params(8),
         cost_estimate=cost(2_000_000_000, groups * size * width * 2),
         name="modes_part",
-    )(messages, table, resident, *after)
-
-
-def modes_kernel(slots, per_turn, messages, weight, resident, after, out, energy, high, low, made, put):
-    groups, points, width = resident.shape
+    )(messages, table, *held, *after)
+
+
+def modes_kernel(slots, messages, weight, theirs, ahead, rest, after, out, energy, high, low, made, put):
+    groups = messages.shape[0]
+    _, points, width = theirs.shape
     part = points // 2
     upper = kept_half() == 1
     scale = weight[:, pl.ds(pl.multiple_of(kept_half() * part, 128), part)]
-
-    def store(step, slot):
-        return pltpu.make_async_copy(made.at[slot], out.at[step], put.at[slot])
-
     _, lanes = iotas(energy.shape)
     value = jnp.zeros(energy.shape, F32)
     for index in range(groups):
-        column = jnp.sum(messages[index, :, width:].astype(F32), axis=1, keepdims=True)
+        column = jnp.sum(
+            messages[place_of(index, groups), :, width:].astype(F32), axis=1, keepdims=True
+        )
         value = jnp.where(lanes == index, column, value)
     energy[...] = value
 
-    def body(turn, carry):
-        for offset in range(per_turn):
-            step = turn * per_turn + offset
-            slot = lax.rem(step, slots)
-
-            @pl.when(step >= slots)
-            def _():
-                store(step - slots, slot).wait()
-
-        for offset in range(per_turn):
-            step = turn * per_turn + offset
-            slot = lax.rem(step, slots)
-            value = project(coefficient_rows(messages[step], width // 2), resident[step])
-            made[slot] = value
-            own = jnp.where(upper, value[:, part:], value[:, :part]).astype(F32) * scale
-            top = own.astype(BF16)
-            high[step] = top
-            low[step] = (own - top.astype(F32)).astype(BF16)
-        for offset in range(per_turn):
-            step = turn * per_turn + offset
-            store(step, lax.rem(step, slots)).start()
-        return carry
-
-    lax.fori_loop(0, groups // per_turn, body, 0)
+    def store(slot, target):
+        return pltpu.make_async_copy(made.at[slot], out.at[target], put.at[slot])
+
+    done = 0
+    for held, side, first in held_parts(theirs, ahead, rest):
+
+        def body(turn, carry, held=held, side=side, first=first, done=done):
+            local = [2 * turn, 2 * turn + 1]
+            places = [lax.rem(done + index, slots) for index in local]
+            targets = [side * (groups // 2) + first + index for index in local]
+            for index, slot, target in zip(local, places, targets):
+
+                @pl.when(done + index >= slots)
+                def _():
+                    store(slot, target).wait()
+
+            for index, slot, target in zip(local, places, targets):
+                rows = coefficient_rows(messages[2 * (first + index) + side], width // 2)
+                value = project(rows, held[index])
+                made[slot] = value
+                own = jnp.where(upper, value[:, part:], value[:, :part]).astype(F32) * scale
+                top = own.astype(BF16)
+                high[target] = top
+                low[target] = (own - top.astype(F32)).astype(BF16)
+            for slot, target in zip(places, targets):
+                store(slot, target).start()
+            return carry
+
+        lax.fori_loop(0, held.shape[0] // 2, body, 0)
+        done += held.shape[0]
     for slot in range(slots):
-        store(groups - slots + slot, slot).wait()
-
-
-def modes_all(messages, weight, resident, after):
-    groups, points, width = resident.shape
+        store(slot, slot).wait()
+
+
+def modes_all(messages, weight, held, after):
+    groups = messages.shape[0]
+    _, points, width = held[0].shape
     slots = 4
     weighted = jax.ShapeDtypeStruct((groups, 2 * KMAX, points // 2), BF16)
     return pl.pallas_call(
-        functools.partial(modes_kernel, slots, 2),
-        in_specs=[VMEM, VMEM, VMEM, ANY],
+        functools.partial(modes_kernel, slots),
+        in_specs=[VMEM] * 5 + [ANY],
         out_specs=(HBM, VMEM, VMEM, VMEM),
         out_shape=(
             jax.ShapeDtypeStruct((groups, 2 * KMAX, points), BF16),
@@ -315,7 +374,7 @@
         compiler_params=kernel_params(12),
         cost_estimate=cost(7_000_000_000, groups * points * width * 2),
         name="modes_all",
-    )(messages, weight, resident, after)
+    )(messages, weight, *held, after)
 
 
 def chosen(cross, lane_partner, groups):
@@ -435,11 +494,16 @@
     weight_row = weight[None, :]
     mirror = [(index, n_freq - 1 - index) for index in range(n_freq)]
 
-    mine, other, resident = gram(
-        spectra, pltpu.with_memory_space_constraint(weight_row, pltpu.HBM)
-    )
-    resident = pltpu.with_memory_space_constraint(resident, pltpu.VMEM)
+    weight_hbm = pltpu.with_memory_space_constraint(weight_row, pltpu.HBM)
+    other, theirs, ahead = gram_other(spectra, weight_hbm)
     swapped = lax.ppermute(other, "space", [(index, index ^ 1) for index in range(n_space)])
+    ahead = pltpu.with_memory_space_constraint(ahead, pltpu.VMEM)
+    mine, rest = gram_mine(ahead, spectra, weight_hbm)
+    held = [
+        pltpu.with_memory_space_constraint(theirs, pltpu.VMEM),
+        ahead,
+        pltpu.with_memory_space_constraint(rest, pltpu.VMEM),
+    ]
     chips = [[index for index in range(core, n_space, 2)] for core in range(2)]
     parts = lax.all_to_all(
         (mine + swapped).astype(BF16), "space", 0, 0, tiled=True, axis_index_groups=chips
@@ -454,9 +518,9 @@
     shares = []
     for begin, size in zip(begins, sizes):
         planes = groups + 1 if size + begin == part else groups
-        shares.append(modes_part(messages, table, resident, begin, size, planes, *shares[-1:]))
+        shares.append(modes_part(messages, table, held, begin, size, planes, *shares[-1:]))
     arrived = [lax.ppermute(share, "freq", mirror) for share in shares]
-    modes, energy, high, low = modes_all(messages, weight_row, resident, shares[-1])
+    modes, energy, high, low = modes_all(messages, weight_row, held, shares[-1])
     early = early_products(high, low, arrived[:-1], begins[:-1])
 
     members = [

time: 83.6 us -> 83.3 us (level)
  waiting for transfers between devices: 3.93 us -> 2.24 us
  Pallas kernels: 28.4 us -> 29.4 us
    ppermute x1, waiting for transfers between devices: 1.54 us -> 0.01 us  [on_device(): lax.ppermute(other, 'space', [(index, index ^ 1) for index in range(n_spa...]
    pallas_call x2 -> x3, Pallas kernels: 19.3 us -> 20.4 us  [the longest x1 8.95 us: modes_all(): pl.pallas_call(functools.partial(modes_kernel, slots), in_specs=[VMEM] *...]
  transfers between devices with their start and end apart: 4 -> 4, of which waited for: 2 -> 1; matrix products, arithmetic and copies ran while one was open for 0% -> 0% of each run, Pallas kernels for 15% -> 20%
where the time goes in v5:
time: 83.3 us; the launch traced here: 83 us
  blocking collectives  38.2 us (46%)
  Pallas kernels  29.4 us (35%)
  starting transfers between devices  12.3 us (15%)
  waiting for transfers between devices  2.24 us (3%)
    all_to_all x1, blocking collectives, on_device(): lax.all_to_all(cross_sums(early, table, high, low, arrived[-1], begins[-1...  16.1 us
    all_to_all x1, blocking collectives, on_device(): lax.all_to_all((mine + swapped).astype(BF16), 'space', 0, 0, tiled=True,...  12.9 us
    ppermute x3, starting transfers between devices, on_device(): arrived = [lax.ppermute(share, 'freq', mirror) for share in shares]  10.9 us
    all_to_all x1, blocking collectives, on_device(): messages = lax.all_to_all(message, 'space', 0, 0, tiled=True)  9.19 us
    pallas_call x1, Pallas kernels, modes_all(): pl.pallas_call(functools.partial(modes_kernel, slots), in_specs=[VMEM] *...  8.95 us
    pallas_call x1, Pallas kernels, gram_other(): pl.pallas_call(gram_other_kernel, in_specs=[HBM, HBM], out_specs=(VMEM, V...  6.81 us
    pallas_call x1, Pallas kernels, gram_mine(): pl.pallas_call(gram_mine_kernel, in_specs=[VMEM, HBM, HBM], out_specs=(VM...  4.65 us
    pallas_call x1, Pallas kernels, solve(): pl.pallas_call(functools.partial(solve_kernel, total), in_specs=[VMEM, HB...  3.59 us
  transfers between devices with their start and end apart: 4, of which 1 were waited for; matrix products, arithmetic and copies ran while one was open for 0% of the time, Pallas kernels for 20%

profile of v5, /device:TPU:1, one launch (start us, length us, event | category | flops | bytes accessed | tf_op | source)
XLA Modules:
  0.0 83.0 jit_solution(15560555046450657578)
XLA Ops:
  0.6 6.8 %gram_other.1 = (f32[8,128,128]{2,1,0:T(8,128)S(1)}, bf16[8,3072,256]{2,1,0:T(8,128)(2,1)S(1)}, bf16[4,3072,256]{2,1,0:T(8,128)(2,1)S(1)}) custom-call(bf16[16,3072,256]{2,1,0:T(8,128)(2,1)} %spectra.3, f32[1,3072]{1,0:T(1,128)} %bitcast.3), custom_call_target="tpu_custom_call" | custom-call | flops 3221225472 | bytes 12582912 | tf_op jit(solution)/shard_map/gram_other/pallas_call | solution.py:101
  7.4 1.5 %collective-permute-start = (f32[8,128,128]{2,1,0:T(8,128)S(1)}, f32[8,128,128]{2,1,0:T(8,128)S(1)}, u32[]{:S(2)}, u32[]{:S(2)}) collective-permute-start(f32[8,128,128]{2,1,0:T(8,128)S(1)} %get-tuple-element.16), channel_id=1, source_target_pairs={{0,1},{1,0},{2,3},{3,2},{4,5},{5,4},{6,7},{7,6},{8,9},{9,8},{10,11... | collective-permute-start | bytes 1572872 | tf_op jit(solution)/shard_map/ppermute | solution.py:499
  8.9 4.7 %gram_mine.1 = (f32[8,128,128]{2,1,0:T(8,128)S(1)}, bf16[4,3072,256]{2,1,0:T(8,128)(2,1)S(1)}) custom-call(bf16[4,3072,256]{2,1,0:T(8,128)(2,1)S(1)} %get-tuple-element.14.ahead, bf16[16,3072,256]{2,1,0:T(8,128)(2,1)} %spectra.3, f32[1,3072]{1,0:T(1,128)} %bitcast.4), custom_call_target="tpu_custom_call" | custom-call | flops 3221225472 | bytes 12582912 | tf_op jit(solution)/shard_map/gram_mine/pallas_call | solution.py:125
  13.6 0.0 collective-permute-done
  13.6 0.1 add_convert_fusion
  13.6 12.9 %all_to_all.15.parts = bf16[8,128,128]{2,1,0:T(8,128)(2,1)S(1)} all-to-all(bf16[8,128,128]{2,1,0:T(8,128)(2,1)S(1)} %add_convert_fusion), channel_id=1, replica_groups={{0,2,4,6,8,10,12,14},{1,3,5,7,9,11,13,15},{16,18,20,22,24,26,28,30},{17..., dimensions={0} | all-to-all | bytes 524288 | tf_op jit(solution)/shard_map/all_to_all | solution.py:508
  26.5 3.6 %solve.1 = (bf16[16,8,384]{2,1,0:T(8,128)(2,1)S(1)}, bf16[16,384]{1,0:T(8,128)(2,1)S(1)}) custom-call(bf16[8,128,128]{2,1,0:T(8,128)(2,1)S(1)} %all_to_all.15.parts, s32[16]{0:T(128)} %counts.1, s32[16]{0:T(128)} %partner.1), custom_call_target="tpu_custom_call" | custom-call | flops 8000000000 | bytes 262144 | tf_op jit(solution)/shard_map/solve/pallas_call | solution.py:232
  30.1 9.2 %all_to_all.16.messages = bf16[16,8,384]{2,1,0:T(8,128)(2,1)S(1)} all-to-all(bf16[16,8,384]{2,1,0:T(8,128)(2,1)S(1)} %get-tuple-element.17), channel_id=1, replica_groups=mesh['freq'=8,'space'=16] {'space'}, dimensions={0} | all-to-all | bytes 196608 | tf_op jit(solution)/shard_map/all_to_all | solution.py:516
  39.3 0.9 %modes_part.3.more_0_ = bf16[16,16,384]{2,1,0:T(8,128)(2,1)S(1)} custom-call(bf16[16,8,384]{2,1,0:T(8,128)(2,1)S(1)} %all_to_all.16.messages, bf16[16,384]{1,0:T(8,128)(2,1)S(1)} %get-tuple-element.20.table, bf16[8,3072,256]{2,1,0:T(8,128)(2,1)S(1)} %get-tuple-element.18.theirs, bf16[4,3072,256]{2,1,0:T(8,128)(2,1)S(1)} %get-tuple-element.14.ahead, ...), custom_call_target="tpu_custom_call" | custom-call | flops 2000000000 | bytes 3145728 | tf_op jit(solution)/shard_map/modes_part/pallas_call | solution.py:295
  40.2 5.5 %collective-permute-start.1 = (bf16[16,16,384]{2,1,0:T(8,128)(2,1)S(1)}, bf16[16,16,384]{2,1,0:T(8,128)(2,1)S(1)}, u32[]{:S(2)}, u32[]{:S(2)}) collective-permute-start(bf16[16,16,384]{2,1,0:T(8,128)(2,1)S(1)} %modes_part.3.more_0_), channel_id=1, source_target_pairs={{0,112},{16,96},{32,80},{48,64},{64,48},{80,32},{96,16},{112,0},{1... | collective-permute-start | bytes 589832 | tf_op jit(solution)/shard_map/ppermute | solution.py:522
  45.8 1.7 %modes_part.4.more_0_ = bf16[16,16,768]{2,1,0:T(8,128)(2,1)S(1)} custom-call(bf16[16,8,384]{2,1,0:T(8,128)(2,1)S(1)} %all_to_all.16.messages, bf16[16,384]{1,0:T(8,128)(2,1)S(1)} %get-tuple-element.20.table, bf16[8,3072,256]{2,1,0:T(8,128)(2,1)S(1)} %get-tuple-element.18.theirs, bf16[4,3072,256]{2,1,0:T(8,128)(2,1)S(1)} %get-tuple-element.14.ahead, ...), custom_call_target="tpu_custom_call" | custom-call | flops 2000000000 | bytes 6291456 | tf_op jit(solution)/shard_map/modes_part/pallas_call | solution.py:295
  47.5 0.0 copy-start
  47.5 0.1 collective-permute-start.2
  47.6 0.9 %modes_part.5.after = bf16[17,16,384]{2,1,0:T(8,128)(2,1)S(1)} custom-call(bf16[16,8,384]{2,1,0:T(8,128)(2,1)S(1)} %all_to_all.16.messages, bf16[16,384]{1,0:T(8,128)(2,1)S(1)} %get-tuple-element.20.table, bf16[8,3072,256]{2,1,0:T(8,128)(2,1)S(1)} %get-tuple-element.18.theirs, bf16[4,3072,256]{2,1,0:T(8,128)(2,1)S(1)} %get-tuple-element.14.ahead, ...), custom_call_target="tpu_custom_call" | custom-call | flops 2000000000 | bytes 3145728 | tf_op jit(solution)/shard_map/modes_part/pallas_call | solution.py:295
  48.5 5.3 %collective-permute-start.3 = (bf16[17,16,384]{2,1,0:T(8,128)(2,1)S(1)}, bf16[17,16,384]{2,1,0:T(8,128)(2,1)S(1)}, u32[]{:S(2)}, u32[]{:S(2)}) collective-permute-start(bf16[17,16,384]{2,1,0:T(8,128)(2,1)S(1)} %modes_part.5.after), channel_id=1, source_target_pairs={{0,112},{16,96},{32,80},{48,64},{64,48},{80,32},{96,16},{112,0},{1... | collective-permute-start | bytes 626696 | tf_op jit(solution)/shard_map/ppermute | solution.py:522
  53.7 0.0 copy-done
  53.7 8.9 %modes_all.1 = (bf16[16,16,3072]{2,1,0:T(8,128)(2,1)}, f32[8,16]{1,0:T(8,128)}, bf16[16,16,1536]{2,1,0:T(8,128)(2,1)S(1)}, bf16[16,16,1536]{2,1,0:T(8,128)(2,1)S(1)}) custom-call(bf16[16,8,384]{2,1,0:T(8,128)(2,1)S(1)} %all_to_all.16.messages, f32[1,3072]{1,0:T(1,128)S(1)} %bitcast.5, bf16[8,3072,256]{2,1,0:T(8,128)(2,1)S(1)} %get-tuple-element.18.theirs, ...), custom_call_target="tpu_custom_call" | custom-call | flops 7000000000 | bytes 25165824 | tf_op jit(solution)/shard_map/modes_all/pallas_call | solution.py:360
  62.7 0.0 collective-permute-done.1.rest_0_
  62.7 0.0 collective-permute-done.2.rest_1_
  62.7 0.5 early_products.1.early
  63.2 2.2 %collective-permute-done.3.share = bf16[17,16,384]{2,1,0:T(8,128)(2,1)S(1)} collective-permute-done((bf16[17,16,384]{2,1,0:T(8,128)(2,1)S(1)}, bf16[17,16,384]{2,1,0:T(8,128)(2,1)S(1)}, u32[]{:S(2)}, u32[]{:S(2)}) %collective-permute-start.3) | collective-permute-done | bytes 208928 | tf_op jit(solution)/shard_map/ppermute | solution.py:522
  65.5 0.6 cross_sums.1
  66.1 16.1 %all_to_all.17.parts = bf16[32,8,256]{2,1,0:T(8,128)(2,1)S(1)} all-to-all(bf16[32,8,256]{2,1,0:T(8,128)(2,1)S(1)} %cross_sums.1), channel_id=1, replica_groups={{0,1,2,3,4,5,6,7,8,9,10,11,12,13,14,15,112,113,114,115,116,117,118,119,..., dimensions={0} | all-to-all | bytes 262144 | tf_op jit(solution)/shard_map/all_to_all | solution.py:530
  82.2 0.7 finish.1
Async XLA Ops:
  7.4 6.1 %collective-permute-start = (f32[8,128,128]{2,1,0:T(8,128)S(1)}, f32[8,128,128]{2,1,0:T(8,128)S(1)}, u32[]{:S(2)}, u32[]{:S(2)}) collective-permute-start(f32[8,128,128]{2,1,0:T(8,128)S(1)} %get-tuple-element.16), channel_id=1, source_target_pairs={{0,1},{1,0},{2,3},{3,2},{4,5},{5,4},{6,7},{7,6},{8,9},{9,8},{10,11... | collective-permute-start | bytes 1572872 | tf_op jit(solution)/shard_map/ppermute | solution.py:499
  40.2 22.5 %collective-permute-start.1 = (bf16[16,16,384]{2,1,0:T(8,128)(2,1)S(1)}, bf16[16,16,384]{2,1,0:T(8,128)(2,1)S(1)}, u32[]{:S(2)}, u32[]{:S(2)}) collective-permute-start(bf16[16,16,384]{2,1,0:T(8,128)(2,1)S(1)} %modes_part.3.more_0_), channel_id=1, source_target_pairs={{0,112},{16,96},{32,80},{48,64},{64,48},{80,32},{96,16},{112,0},{1... | collective-permute-start | bytes 589832 | tf_op jit(solution)/shard_map/ppermute | solution.py:522
  47.5 6.3 %copy-start = (f32[3072]{0:T(1024)S(1)}, f32[3072]{0:T(1024)}, u32[]{:S(2)}) copy-start(f32[3072]{0:T(1024)} %param.5) | copy-start | bytes 36868
  47.5 15.2 %collective-permute-start.2 = (bf16[16,16,768]{2,1,0:T(8,128)(2,1)S(1)}, bf16[16,16,768]{2,1,0:T(8,128)(2,1)S(1)}, u32[]{:S(2)}, u32[]{:S(2)}) collective-permute-start(bf16[16,16,768]{2,1,0:T(8,128)(2,1)S(1)} %modes_part.4.more_0_), channel_id=1, source_target_pairs={{0,112},{16,96},{32,80},{48,64},{64,48},{80,32},{96,16},{112,0},{1... | collective-permute-start | bytes 1179656 | tf_op jit(solution)/shard_map/ppermute | solution.py:522
  48.5 17.0 %collective-permute-start.3 = (bf16[17,16,384]{2,1,0:T(8,128)(2,1)S(1)}, bf16[17,16,384]{2,1,0:T(8,128)(2,1)S(1)}, u32[]{:S(2)}, u32[]{:S(2)}) collective-permute-start(bf16[17,16,384]{2,1,0:T(8,128)(2,1)S(1)} %modes_part.5.after), channel_id=1, source_target_pairs={{0,112},{16,96},{32,80},{48,64},{64,48},{80,32},{96,16},{112,0},{1... | collective-permute-start | bytes 626696 | tf_op jit(solution)/shard_map/ppermute | solution.py:522

commit v6 on v5

--- a/solution.py
+++ b/solution.py
@@ -160,7 +160,7 @@
     return (re, im)
 
 
-def solve_kernel(total, parts, counts, partner, out, table, kept_all, partners, sems):
+def solve_kernel(total, orders, parts, counts, partner, out, table, kept_all, partners, sems):
     count, half, _ = parts.shape
     small = (
         pltpu.make_async_copy(counts, kept_all, sems.at[0]),
@@ -204,7 +204,12 @@
     for copy in small:
         copy.wait()
     place = lax.axis_index("space")
-    kept = kept_all[lax.rem(place, 2) * (kept_all.shape[0] // 2) + place // 2]
+    z_high = lax.rem(lax.axis_index("freq"), 2)
+    slot = jnp.int32(0)
+    for side, order in enumerate(orders):
+        for index, chip in enumerate(order):
+            slot = jnp.where((z_high == side) & (place // 2 == chip), index, slot)
+    kept = kept_all[lax.rem(place, 2) * (kept_all.shape[0] // 2) + slot]
     ranks, lanes = iotas((KMAX, half))
     scale = jnp.where(ranks[:, :1] < kept, 1.0 / jnp.sqrt(energy + EPS), 0.0)
     first = energy.astype(BF16)
@@ -226,11 +231,11 @@
     table[...] = value.astype(F32).astype(BF16)
 
 
-def solve(parts, counts, partner, total, lanes):
+def solve(parts, counts, partner, total, orders, lanes):
     _, half, _ = parts.shape
     groups = counts.shape[0]
     return pl.pallas_call(
-        functools.partial(solve_kernel, total),
+        functools.partial(solve_kernel, total, orders),
         in_specs=[VMEM, HBM, HBM],
         out_specs=(VMEM, VMEM),
         out_shape=(
@@ -249,7 +254,7 @@
 
 
 def place_of(index, groups):
-    return 2 * (index % (groups // 2)) + index // (groups // 2)
+    return 2 * (index % (groups // 2)) + 1 - index // (groups // 2)
 
 
 def held_parts(theirs, ahead, rest):
@@ -282,7 +287,7 @@
     start = pl.multiple_of((1 - kept_half()) * (points // 2) + begin, 128)
     for held, side, first in held_parts(theirs, ahead, rest):
         for index in range(held.shape[0]):
-            rows = coefficient_rows(messages[2 * (first + index) + side], width // 2)
+            rows = coefficient_rows(messages[2 * (first + index) + 1 - side], width // 2)
             target = side * (groups // 2) + first + index
             out[target] = project(rows, held[index, pl.ds(start, size)])
     if out.shape[0] > groups:
@@ -335,7 +340,7 @@
                     store(slot, target).wait()
 
             for index, slot, target in zip(local, places, targets):
-                rows = coefficient_rows(messages[2 * (first + index) + side], width // 2)
+                rows = coefficient_rows(messages[2 * (first + index) + 1 - side], width // 2)
                 value = project(rows, held[index])
                 made[slot] = value
                 own = jnp.where(upper, value[:, part:], value[:, :part]).astype(F32) * scale
@@ -427,7 +432,7 @@
     )(high, low, *arrived)
 
 
-def cross_kernel(begin, early, table, high, low, share, out):
+def cross_kernel(begin, sides, early, table, high, low, share, out):
     groups, rank, part = high.shape
     rows = groups * rank
     cross = early[...] + products(high, low, share, begin)
@@ -439,19 +444,27 @@
     source, target = iotas((rows, rows))
     moved = target == (source % rank) * groups + source // rank
     ordered = jnp.dot(both, moved.astype(F32).astype(BF16), preferred_element_type=F32)
-    first = kept_half() == 0
-    lower = jnp.where(first, ordered[:KMAX], ordered[KMAX:]).astype(BF16)
-    upper = jnp.where(first, ordered[KMAX:], ordered[:KMAX]).astype(BF16)
-    half = out.shape[0] // 2
-    for index in range(half):
-        out[index] = lower
-        out[half + index] = upper
-
-
-def cross_sums(early, table, high, low, share, begin, members):
+    own_copy = ordered[:KMAX].astype(BF16)
+    other_copy = ordered[KMAX:].astype(BF16)
+    place = lax.axis_index("freq")
+    upper = kept_half()
+    pair = jnp.where(upper == 0, place, lax.axis_size("freq") - 1 - place)
+    step = 16
+    for begin in range(0, out.shape[0], step):
+        bits = jnp.int32(0)
+        for index, side in enumerate(sides):
+            mask = sum(bit << k for k, bit in enumerate(side[begin : begin + step]))
+            bits = jnp.where(pair == index, mask, bits)
+        for k in range(step):
+            same = ((bits >> k) & 1) == upper
+            out[begin + k] = jnp.where(same, own_copy, other_copy)
+
+
+def cross_sums(early, table, high, low, share, begin, sides):
     groups, rank, part = high.shape
-    return pl.pallas_call(
-        functools.partial(cross_kernel, begin),
+    members = len(sides[0])
+    return pl.pallas_call(
+        functools.partial(cross_kernel, begin, sides),
         in_specs=[VMEM] * 5,
         out_specs=VMEM,
         out_shape=jax.ShapeDtypeStruct((members, KMAX, groups * rank), BF16),
@@ -486,6 +499,13 @@
     )(parts)
 
 
+def hops_from_corner(device, n_space):
+    freq, space = divmod(device, n_space)
+    x, z_high = divmod(freq, 2)
+    z_low, rest = divmod(space, 8)
+    return sum(min(a, 4 - a) for a in (x, rest // 2, 2 * z_high + z_low))
+
+
 def on_device(spectra, weight, partner, counts):
     groups, points, width = spectra.shape
     n_freq, n_space = (lax.axis_size("freq"), lax.axis_size("space"))
@@ -504,16 +524,31 @@
         ahead,
         pltpu.with_memory_space_constraint(rest, pltpu.VMEM),
     ]
-    chips = [[index for index in range(core, n_space, 2)] for core in range(2)]
+    orders = [
+        sorted(range(n_space // 2), key=lambda chip: -hops_from_corner(side * n_space + 2 * chip, n_space))
+        for side in range(2)
+    ]
+    both_axes = ("freq", "space")
+    chips = [
+        [group * n_space + 2 * chip + core for chip in orders[group % 2]]
+        for group in range(n_freq)
+        for core in range(2)
+    ]
+    devices = [
+        [group * n_space + 2 * chip + core for chip in orders[group % 2] for core in (1, 0)]
+        for group in range(n_freq)
+    ]
     parts = lax.all_to_all(
-        (mine + swapped).astype(BF16), "space", 0, 0, tiled=True, axis_index_groups=chips
+        (mine + swapped).astype(BF16), both_axes, 0, 0, tiled=True, axis_index_groups=chips
     )
     part = points // 2
     sizes = (part // 4, part // 2, part // 4)
     begins = (0, part // 4, 3 * part // 4)
     in_hbm = [pltpu.with_memory_space_constraint(array, pltpu.HBM) for array in (counts, partner)]
-    message, table = solve(parts, *in_hbm, total, sizes[-1])
-    messages = lax.all_to_all(message, "space", 0, 0, tiled=True)
+    message, table = solve(parts, *in_hbm, total, orders, sizes[-1])
+    messages = lax.all_to_all(
+        message, both_axes, 0, 0, tiled=True, axis_index_groups=devices
+    )
 
     shares = []
     for begin, size in zip(begins, sizes):
@@ -524,14 +559,18 @@
     early = early_products(high, low, arrived[:-1], begins[:-1])
 
     members = [
-        [group * n_space + index for group in (low_group, n_freq - 1 - low_group) for index in range(n_space)]
+        sorted(
+            (group * n_space + index for group in (low_group, n_freq - 1 - low_group) for index in range(n_space)),
+            key=lambda device: -hops_from_corner(device, n_space),
+        )
         for low_group in range(n_freq // 2)
     ]
+    sides = [[2 * device // (n_freq * n_space) for device in order] for order in members]
     gathered = lax.all_to_all(
         cross_sums(
-            early, table, high, low, arrived[-1], begins[-1], 2 * n_space
+            early, table, high, low, arrived[-1], begins[-1], sides
         ),
-        ("freq", "space"),
+        both_axes,
         0,
         0,
         tiled=True,

time: 83.3 us -> 79.4 us (0.953)
  blocking collectives: 38.2 us -> 33.6 us
    all_to_all x2, blocking collectives: 22.1 us -> 19.6 us  [the longest x1 10.9 us: on_device(): lax.all_to_all((mine + swapped).astype(BF16), both_axes, 0, 0, tiled=True...]
    all_to_all x1, blocking collectives: 16.1 us -> 13.9 us  [on_device(): lax.all_to_all(cross_sums(early, table, high, low, arrived[-1], begins[-1...]
  transfers between devices with their start and end apart: 4 -> 4, of which waited for: 1 -> 1; matrix products, arithmetic and copies ran while one was open for 0% -> 0% of each run, Pallas kernels for 20% -> 21%
where the time goes in v6:
time: 79.4 us; the launch traced here: 79.1 us
  blocking collectives  33.6 us (42%)
  Pallas kernels  29.5 us (37%)
  starting transfers between devices  13.1 us (16%)
  waiting for transfers between devices  2.19 us (3%)
    all_to_all x1, blocking collectives, on_device(): lax.all_to_all(cross_sums(early, table, high, low, arrived[-1], begins[-1...  13.9 us
    ppermute x3, starting transfers between devices, on_device(): arrived = [lax.ppermute(share, 'freq', mirror) for share in shares]  11.6 us
    all_to_all x1, blocking collectives, on_device(): lax.all_to_all((mine + swapped).astype(BF16), both_axes, 0, 0, tiled=True...  10.9 us
    pallas_call x1, Pallas kernels, modes_all(): pl.pallas_call(functools.partial(modes_kernel, slots), in_specs=[VMEM] *...  8.95 us
    all_to_all x1, blocking collectives, on_device(): lax.all_to_all(message, both_axes, 0, 0, tiled=True, axis_index_groups=de...  8.67 us
    pallas_call x1, Pallas kernels, gram_other(): pl.pallas_call(gram_other_kernel, in_specs=[HBM, HBM], out_specs=(VMEM, V...  6.81 us
    pallas_call x1, Pallas kernels, gram_mine(): pl.pallas_call(gram_mine_kernel, in_specs=[VMEM, HBM, HBM], out_specs=(VM...  4.65 us
    pallas_call x1, Pallas kernels, solve(): pl.pallas_call(functools.partial(solve_kernel, total, orders), in_specs=[...  3.6 us
  transfers between devices with their start and end apart: 4, of which 1 were waited for; matrix products, arithmetic and copies ran while one was open for 0% of the time, Pallas kernels for 21%

profile of v6, /device:TPU:1, one launch (start us, length us, event | category | flops | bytes accessed | tf_op | source)
XLA Modules:
  0.0 79.1 jit_solution(13660462200701740597)
XLA Ops:
  0.6 6.8 %gram_other.1 = (f32[8,128,128]{2,1,0:T(8,128)S(1)}, bf16[8,3072,256]{2,1,0:T(8,128)(2,1)S(1)}, bf16[4,3072,256]{2,1,0:T(8,128)(2,1)S(1)}) custom-call(bf16[16,3072,256]{2,1,0:T(8,128)(2,1)} %spectra.3, f32[1,3072]{1,0:T(1,128)} %bitcast.3), custom_call_target="tpu_custom_call" | custom-call | flops 3221225472 | bytes 12582912 | tf_op jit(solution)/shard_map/gram_other/pallas_call | solution.py:101
  7.4 1.5 %collective-permute-start = (f32[8,128,128]{2,1,0:T(8,128)S(1)}, f32[8,128,128]{2,1,0:T(8,128)S(1)}, u32[]{:S(2)}, u32[]{:S(2)}) collective-permute-start(f32[8,128,128]{2,1,0:T(8,128)S(1)} %get-tuple-element.16), channel_id=1, source_target_pairs={{0,1},{1,0},{2,3},{3,2},{4,5},{5,4},{6,7},{7,6},{8,9},{9,8},{10,11... | collective-permute-start | bytes 1572872 | tf_op jit(solution)/shard_map/ppermute | solution.py:519
  8.9 4.7 %gram_mine.1 = (f32[8,128,128]{2,1,0:T(8,128)S(1)}, bf16[4,3072,256]{2,1,0:T(8,128)(2,1)S(1)}) custom-call(bf16[4,3072,256]{2,1,0:T(8,128)(2,1)S(1)} %get-tuple-element.14.ahead, bf16[16,3072,256]{2,1,0:T(8,128)(2,1)} %spectra.3, f32[1,3072]{1,0:T(1,128)} %bitcast.4), custom_call_target="tpu_custom_call" | custom-call | flops 3221225472 | bytes 12582912 | tf_op jit(solution)/shard_map/gram_mine/pallas_call | solution.py:125
  13.6 0.0 collective-permute-done
  13.6 0.1 add_convert_fusion
  13.6 10.9 %all_to_all.15.parts = bf16[8,128,128]{2,1,0:T(8,128)(2,1)S(1)} all-to-all(bf16[8,128,128]{2,1,0:T(8,128)(2,1)S(1)} %add_convert_fusion), channel_id=1, replica_groups={{12,4,10,14,2,6,8,0},{13,5,11,15,3,7,9,1},{20,18,22,28,16,26,30,24},{21..., dimensions={0} | all-to-all | bytes 524288 | tf_op jit(solution)/shard_map/all_to_all | solution.py:541
  24.6 3.6 %solve.1 = (bf16[16,8,384]{2,1,0:T(8,128)(2,1)S(1)}, bf16[16,384]{1,0:T(8,128)(2,1)S(1)}) custom-call(bf16[8,128,128]{2,1,0:T(8,128)(2,1)S(1)} %all_to_all.15.parts, s32[16]{0:T(128)} %counts.1, s32[16]{0:T(128)} %partner.1), custom_call_target="tpu_custom_call" | custom-call | flops 8000000000 | bytes 262144 | tf_op jit(solution)/shard_map/solve/pallas_call | solution.py:237
  28.2 8.7 %all_to_all.16.messages = bf16[16,8,384]{2,1,0:T(8,128)(2,1)S(1)} all-to-all(bf16[16,8,384]{2,1,0:T(8,128)(2,1)S(1)} %get-tuple-element.17), channel_id=1, replica_groups={{13,12,5,4,11,10,15,14,3,2,7,6,9,8,1,0},{21,20,19,18,23,22,29,28,17,16,..., dimensions={0} | all-to-all | bytes 196608 | tf_op jit(solution)/shard_map/all_to_all | solution.py:549
  36.9 0.9 %modes_part.3.more_0_ = bf16[16,16,384]{2,1,0:T(8,128)(2,1)S(1)} custom-call(bf16[16,8,384]{2,1,0:T(8,128)(2,1)S(1)} %all_to_all.16.messages, bf16[16,384]{1,0:T(8,128)(2,1)S(1)} %get-tuple-element.20.table, bf16[8,3072,256]{2,1,0:T(8,128)(2,1)S(1)} %get-tuple-element.18.theirs, bf16[4,3072,256]{2,1,0:T(8,128)(2,1)S(1)} %get-tuple-element.14.ahead, ...), custom_call_target="tpu_custom_call" | custom-call | flops 2000000000 | bytes 3145728 | tf_op jit(solution)/shard_map/modes_part/pallas_call | solution.py:300
  37.8 6.3 %collective-permute-start.1 = (bf16[16,16,384]{2,1,0:T(8,128)(2,1)S(1)}, bf16[16,16,384]{2,1,0:T(8,128)(2,1)S(1)}, u32[]{:S(2)}, u32[]{:S(2)}) collective-permute-start(bf16[16,16,384]{2,1,0:T(8,128)(2,1)S(1)} %modes_part.3.more_0_), channel_id=1, source_target_pairs={{0,112},{16,96},{32,80},{48,64},{64,48},{80,32},{96,16},{112,0},{1... | collective-permute-start | bytes 589832 | tf_op jit(solution)/shard_map/ppermute | solution.py:557
  44.1 1.7 %modes_part.4.more_0_ = bf16[16,16,768]{2,1,0:T(8,128)(2,1)S(1)} custom-call(bf16[16,8,384]{2,1,0:T(8,128)(2,1)S(1)} %all_to_all.16.messages, bf16[16,384]{1,0:T(8,128)(2,1)S(1)} %get-tuple-element.20.table, bf16[8,3072,256]{2,1,0:T(8,128)(2,1)S(1)} %get-tuple-element.18.theirs, bf16[4,3072,256]{2,1,0:T(8,128)(2,1)S(1)} %get-tuple-element.14.ahead, ...), custom_call_target="tpu_custom_call" | custom-call | flops 2000000000 | bytes 6291456 | tf_op jit(solution)/shard_map/modes_part/pallas_call | solution.py:300
  45.8 0.0 copy-start
  45.8 0.1 collective-permute-start.2
  45.9 0.9 %modes_part.5.after = bf16[17,16,384]{2,1,0:T(8,128)(2,1)S(1)} custom-call(bf16[16,8,384]{2,1,0:T(8,128)(2,1)S(1)} %all_to_all.16.messages, bf16[16,384]{1,0:T(8,128)(2,1)S(1)} %get-tuple-element.20.table, bf16[8,3072,256]{2,1,0:T(8,128)(2,1)S(1)} %get-tuple-element.18.theirs, bf16[4,3072,256]{2,1,0:T(8,128)(2,1)S(1)} %get-tuple-element.14.ahead, ...), custom_call_target="tpu_custom_call" | custom-call | flops 2000000000 | bytes 3145728 | tf_op jit(solution)/shard_map/modes_part/pallas_call | solution.py:300
  46.8 5.3 %collective-permute-start.3 = (bf16[17,16,384]{2,1,0:T(8,128)(2,1)S(1)}, bf16[17,16,384]{2,1,0:T(8,128)(2,1)S(1)}, u32[]{:S(2)}, u32[]{:S(2)}) collective-permute-start(bf16[17,16,384]{2,1,0:T(8,128)(2,1)S(1)} %modes_part.5.after), channel_id=1, source_target_pairs={{0,112},{16,96},{32,80},{48,64},{64,48},{80,32},{96,16},{112,0},{1... | collective-permute-start | bytes 626696 | tf_op jit(solution)/shard_map/ppermute | solution.py:557
  52.1 0.0 copy-done
  52.1 8.9 %modes_all.1 = (bf16[16,16,3072]{2,1,0:T(8,128)(2,1)}, f32[8,16]{1,0:T(8,128)}, bf16[16,16,1536]{2,1,0:T(8,128)(2,1)S(1)}, bf16[16,16,1536]{2,1,0:T(8,128)(2,1)S(1)}) custom-call(bf16[16,8,384]{2,1,0:T(8,128)(2,1)S(1)} %all_to_all.16.messages, f32[1,3072]{1,0:T(1,128)S(1)} %bitcast.5, bf16[8,3072,256]{2,1,0:T(8,128)(2,1)S(1)} %get-tuple-element.18.theirs, ...), custom_call_target="tpu_custom_call" | custom-call | flops 7000000000 | bytes 25165824 | tf_op jit(solution)/shard_map/modes_all/pallas_call | solution.py:365
  61.0 0.0 collective-permute-done.1.rest_0_
  61.0 0.0 collective-permute-done.2.rest_1_
  61.0 0.5 early_products.1.early
  61.6 2.2 %collective-permute-done.3.share = bf16[17,16,384]{2,1,0:T(8,128)(2,1)S(1)} collective-permute-done((bf16[17,16,384]{2,1,0:T(8,128)(2,1)S(1)}, bf16[17,16,384]{2,1,0:T(8,128)(2,1)S(1)}, u32[]{:S(2)}, u32[]{:S(2)}) %collective-permute-start.3) | collective-permute-done | bytes 208928 | tf_op jit(solution)/shard_map/ppermute | solution.py:557
  63.7 0.6 cross_sums.1
  64.4 13.9 %all_to_all.17.parts = bf16[32,8,256]{2,1,0:T(8,128)(2,1)S(1)} all-to-all(bf16[32,8,256]{2,1,0:T(8,128)(2,1)S(1)} %cross_sums.1), channel_id=1, replica_groups={{116,117,114,115,118,119,124,125,12,13,112,113,122,123,126,127,4,5,10,1..., dimensions={0} | all-to-all | bytes 262144 | tf_op jit(solution)/shard_map/all_to_all | solution.py:569
  78.3 0.7 finish.1
Async XLA Ops:
  7.4 6.1 %collective-permute-start = (f32[8,128,128]{2,1,0:T(8,128)S(1)}, f32[8,128,128]{2,1,0:T(8,128)S(1)}, u32[]{:S(2)}, u32[]{:S(2)}) collective-permute-start(f32[8,128,128]{2,1,0:T(8,128)S(1)} %get-tuple-element.16), channel_id=1, source_target_pairs={{0,1},{1,0},{2,3},{3,2},{4,5},{5,4},{6,7},{7,6},{8,9},{9,8},{10,11... | collective-permute-start | bytes 1572872 | tf_op jit(solution)/shard_map/ppermute | solution.py:519
  37.8 23.2 %collective-permute-start.1 = (bf16[16,16,384]{2,1,0:T(8,128)(2,1)S(1)}, bf16[16,16,384]{2,1,0:T(8,128)(2,1)S(1)}, u32[]{:S(2)}, u32[]{:S(2)}) collective-permute-start(bf16[16,16,384]{2,1,0:T(8,128)(2,1)S(1)} %modes_part.3.more_0_), channel_id=1, source_target_pairs={{0,112},{16,96},{32,80},{48,64},{64,48},{80,32},{96,16},{112,0},{1... | collective-permute-start | bytes 589832 | tf_op jit(solution)/shard_map/ppermute | solution.py:557
  45.8 6.3 %copy-start = (f32[3072]{0:T(1024)S(1)}, f32[3072]{0:T(1024)}, u32[]{:S(2)}) copy-start(f32[3072]{0:T(1024)} %param.5) | copy-start | bytes 36868
  45.8 15.2 %collective-permute-start.2 = (bf16[16,16,768]{2,1,0:T(8,128)(2,1)S(1)}, bf16[16,16,768]{2,1,0:T(8,128)(2,1)S(1)}, u32[]{:S(2)}, u32[]{:S(2)}) collective-permute-start(bf16[16,16,768]{2,1,0:T(8,128)(2,1)S(1)} %modes_part.4.more_0_), channel_id=1, source_target_pairs={{0,112},{16,96},{32,80},{48,64},{64,48},{80,32},{96,16},{112,0},{1... | collective-permute-start | bytes 1179656 | tf_op jit(solution)/shard_map/ppermute | solution.py:557
  46.8 17.0 %collective-permute-start.3 = (bf16[17,16,384]{2,1,0:T(8,128)(2,1)S(1)}, bf16[17,16,384]{2,1,0:T(8,128)(2,1)S(1)}, u32[]{:S(2)}, u32[]{:S(2)}) collective-permute-start(bf16[17,16,384]{2,1,0:T(8,128)(2,1)S(1)} %modes_part.5.after), channel_id=1, source_target_pairs={{0,112},{16,96},{32,80},{48,64},{64,48},{80,32},{96,16},{112,0},{1... | collective-permute-start | bytes 626696 | tf_op jit(solution)/shard_map/ppermute | solution.py:557

commit v7 on v6

--- a/solution.py
+++ b/solution.py
@@ -542,8 +542,8 @@
         (mine + swapped).astype(BF16), both_axes, 0, 0, tiled=True, axis_index_groups=chips
     )
     part = points // 2
-    sizes = (part // 4, part // 2, part // 4)
-    begins = (0, part // 4, 3 * part // 4)
+    sizes = (part // 3, part // 12 * 5, part // 4)
+    begins = (0, part // 3, 3 * part // 4)
     in_hbm = [pltpu.with_memory_space_constraint(array, pltpu.HBM) for array in (counts, partner)]
     message, table = solve(parts, *in_hbm, total, orders, sizes[-1])
     messages = lax.all_to_all(
@@ -561,7 +561,7 @@
     members = [
         sorted(
             (group * n_space + index for group in (low_group, n_freq - 1 - low_group) for index in range(n_space)),
-            key=lambda device: -hops_from_corner(device, n_space),
+            key=lambda device: (-hops_from_corner(device, n_space), -(device % 2)),
         )
         for low_group in range(n_freq // 2)
     ]

time: 79.4 us -> 77.8 us (0.980)
  waiting for transfers between devices: 2.19 us -> 0.75 us
    ppermute x3, waiting for transfers between devices: 2.19 us -> 0.75 us  [on_device(): arrived = [lax.ppermute(share, 'freq', mirror) for share in shares]]
where the time goes in v7:
time: 77.8 us; the launch traced here: 77.4 us
  blocking collectives  33.3 us (43%)
  Pallas kernels  29.5 us (38%)
  starting transfers between devices  13.1 us (17%)
    all_to_all x1, blocking collectives, on_device(): lax.all_to_all(cross_sums(early, table, high, low, arrived[-1], begins[-1...  13.7 us
    ppermute x3, starting transfers between devices, on_device(): arrived = [lax.ppermute(share, 'freq', mirror) for share in shares]  11.6 us
    all_to_all x1, blocking collectives, on_device(): lax.all_to_all((mine + swapped).astype(BF16), both_axes, 0, 0, tiled=True...  10.9 us
    pallas_call x1, Pallas kernels, modes_all(): pl.pallas_call(functools.partial(modes_kernel, slots), in_specs=[VMEM] *...  8.95 us
    all_to_all x1, blocking collectives, on_device(): lax.all_to_all(message, both_axes, 0, 0, tiled=True, axis_index_groups=de...  8.67 us
    pallas_call x1, Pallas kernels, gram_other(): pl.pallas_call(gram_other_kernel, in_specs=[HBM, HBM], out_specs=(VMEM, V...  6.81 us
    pallas_call x1, Pallas kernels, gram_mine(): pl.pallas_call(gram_mine_kernel, in_specs=[VMEM, HBM, HBM], out_specs=(VM...  4.65 us
    pallas_call x1, Pallas kernels, solve(): pl.pallas_call(functools.partial(solve_kernel, total, orders), in_specs=[...  3.6 us
  transfers between devices with their start and end apart: 4, of which 1 were waited for; matrix products, arithmetic and copies ran while one was open for 0% of the time, Pallas kernels for 21%

profile of v7, /device:TPU:1, one launch (start us, length us, event | category | flops | bytes accessed | tf_op | source)
XLA Modules:
  0.0 77.4 jit_solution(7126028212915923396)
XLA Ops:
  0.6 6.8 %gram_other.1 = (f32[8,128,128]{2,1,0:T(8,128)S(1)}, bf16[8,3072,256]{2,1,0:T(8,128)(2,1)S(1)}, bf16[4,3072,256]{2,1,0:T(8,128)(2,1)S(1)}) custom-call(bf16[16,3072,256]{2,1,0:T(8,128)(2,1)} %spectra.3, f32[1,3072]{1,0:T(1,128)} %bitcast.3), custom_call_target="tpu_custom_call" | custom-call | flops 3221225472 | bytes 12582912 | tf_op jit(solution)/shard_map/gram_other/pallas_call | solution.py:101
  7.4 1.5 %collective-permute-start = (f32[8,128,128]{2,1,0:T(8,128)S(1)}, f32[8,128,128]{2,1,0:T(8,128)S(1)}, u32[]{:S(2)}, u32[]{:S(2)}) collective-permute-start(f32[8,128,128]{2,1,0:T(8,128)S(1)} %get-tuple-element.16), channel_id=1, source_target_pairs={{0,1},{1,0},{2,3},{3,2},{4,5},{5,4},{6,7},{7,6},{8,9},{9,8},{10,11... | collective-permute-start | bytes 1572872 | tf_op jit(solution)/shard_map/ppermute | solution.py:519
  8.9 4.7 %gram_mine.1 = (f32[8,128,128]{2,1,0:T(8,128)S(1)}, bf16[4,3072,256]{2,1,0:T(8,128)(2,1)S(1)}) custom-call(bf16[4,3072,256]{2,1,0:T(8,128)(2,1)S(1)} %get-tuple-element.14.ahead, bf16[16,3072,256]{2,1,0:T(8,128)(2,1)} %spectra.3, f32[1,3072]{1,0:T(1,128)} %bitcast.4), custom_call_target="tpu_custom_call" | custom-call | flops 3221225472 | bytes 12582912 | tf_op jit(solution)/shard_map/gram_mine/pallas_call | solution.py:125
  13.6 0.0 collective-permute-done
  13.6 0.1 add_convert_fusion
  13.6 10.9 %all_to_all.15.parts = bf16[8,128,128]{2,1,0:T(8,128)(2,1)S(1)} all-to-all(bf16[8,128,128]{2,1,0:T(8,128)(2,1)S(1)} %add_convert_fusion), channel_id=1, replica_groups={{12,4,10,14,2,6,8,0},{13,5,11,15,3,7,9,1},{20,18,22,28,16,26,30,24},{21..., dimensions={0} | all-to-all | bytes 524288 | tf_op jit(solution)/shard_map/all_to_all | solution.py:541
  24.6 3.6 %solve.1 = (bf16[16,8,384]{2,1,0:T(8,128)(2,1)S(1)}, bf16[16,384]{1,0:T(8,128)(2,1)S(1)}) custom-call(bf16[8,128,128]{2,1,0:T(8,128)(2,1)S(1)} %all_to_all.15.parts, s32[16]{0:T(128)} %counts.1, s32[16]{0:T(128)} %partner.1), custom_call_target="tpu_custom_call" | custom-call | flops 8000000000 | bytes 262144 | tf_op jit(solution)/shard_map/solve/pallas_call | solution.py:237
  28.2 8.7 %all_to_all.16.messages = bf16[16,8,384]{2,1,0:T(8,128)(2,1)S(1)} all-to-all(bf16[16,8,384]{2,1,0:T(8,128)(2,1)S(1)} %get-tuple-element.17), channel_id=1, replica_groups={{13,12,5,4,11,10,15,14,3,2,7,6,9,8,1,0},{21,20,19,18,23,22,29,28,17,16,..., dimensions={0} | all-to-all | bytes 196608 | tf_op jit(solution)/shard_map/all_to_all | solution.py:549
  36.9 1.2 %modes_part.3.more_0_ = bf16[16,16,512]{2,1,0:T(8,128)(2,1)S(1)} custom-call(bf16[16,8,384]{2,1,0:T(8,128)(2,1)S(1)} %all_to_all.16.messages, bf16[16,384]{1,0:T(8,128)(2,1)S(1)} %get-tuple-element.20.table, bf16[8,3072,256]{2,1,0:T(8,128)(2,1)S(1)} %get-tuple-element.18.theirs, bf16[4,3072,256]{2,1,0:T(8,128)(2,1)S(1)} %get-tuple-element.14.ahead, ...), custom_call_target="tpu_custom_call" | custom-call | flops 2000000000 | bytes 4194304 | tf_op jit(solution)/shard_map/modes_part/pallas_call | solution.py:300
  38.1 6.3 %collective-permute-start.1 = (bf16[16,16,512]{2,1,0:T(8,128)(2,1)S(1)}, bf16[16,16,512]{2,1,0:T(8,128)(2,1)S(1)}, u32[]{:S(2)}, u32[]{:S(2)}) collective-permute-start(bf16[16,16,512]{2,1,0:T(8,128)(2,1)S(1)} %modes_part.3.more_0_), channel_id=1, source_target_pairs={{0,112},{16,96},{32,80},{48,64},{64,48},{80,32},{96,16},{112,0},{1... | collective-permute-start | bytes 786440 | tf_op jit(solution)/shard_map/ppermute | solution.py:557
  44.3 1.5 %modes_part.4.more_0_ = bf16[16,16,640]{2,1,0:T(8,128)(2,1)S(1)} custom-call(bf16[16,8,384]{2,1,0:T(8,128)(2,1)S(1)} %all_to_all.16.messages, bf16[16,384]{1,0:T(8,128)(2,1)S(1)} %get-tuple-element.20.table, bf16[8,3072,256]{2,1,0:T(8,128)(2,1)S(1)} %get-tuple-element.18.theirs, bf16[4,3072,256]{2,1,0:T(8,128)(2,1)S(1)} %get-tuple-element.14.ahead, ...), custom_call_target="tpu_custom_call" | custom-call | flops 2000000000 | bytes 5242880 | tf_op jit(solution)/shard_map/modes_part/pallas_call | solution.py:300
  45.8 0.0 copy-start
  45.8 0.1 collective-permute-start.2
  45.9 0.9 %modes_part.5.after = bf16[17,16,384]{2,1,0:T(8,128)(2,1)S(1)} custom-call(bf16[16,8,384]{2,1,0:T(8,128)(2,1)S(1)} %all_to_all.16.messages, bf16[16,384]{1,0:T(8,128)(2,1)S(1)} %get-tuple-element.20.table, bf16[8,3072,256]{2,1,0:T(8,128)(2,1)S(1)} %get-tuple-element.18.theirs, bf16[4,3072,256]{2,1,0:T(8,128)(2,1)S(1)} %get-tuple-element.14.ahead, ...), custom_call_target="tpu_custom_call" | custom-call | flops 2000000000 | bytes 3145728 | tf_op jit(solution)/shard_map/modes_part/pallas_call | solution.py:300
  46.8 5.3 %collective-permute-start.3 = (bf16[17,16,384]{2,1,0:T(8,128)(2,1)S(1)}, bf16[17,16,384]{2,1,0:T(8,128)(2,1)S(1)}, u32[]{:S(2)}, u32[]{:S(2)}) collective-permute-start(bf16[17,16,384]{2,1,0:T(8,128)(2,1)S(1)} %modes_part.5.after), channel_id=1, source_target_pairs={{0,112},{16,96},{32,80},{48,64},{64,48},{80,32},{96,16},{112,0},{1... | collective-permute-start | bytes 626696 | tf_op jit(solution)/shard_map/ppermute | solution.py:557
  52.1 0.0 copy-done
  52.1 8.9 %modes_all.1 = (bf16[16,16,3072]{2,1,0:T(8,128)(2,1)}, f32[8,16]{1,0:T(8,128)}, bf16[16,16,1536]{2,1,0:T(8,128)(2,1)S(1)}, bf16[16,16,1536]{2,1,0:T(8,128)(2,1)S(1)}) custom-call(bf16[16,8,384]{2,1,0:T(8,128)(2,1)S(1)} %all_to_all.16.messages, f32[1,3072]{1,0:T(1,128)S(1)} %bitcast.5, bf16[8,3072,256]{2,1,0:T(8,128)(2,1)S(1)} %get-tuple-element.18.theirs, ...), custom_call_target="tpu_custom_call" | custom-call | flops 7000000000 | bytes 25165824 | tf_op jit(solution)/shard_map/modes_all/pallas_call | solution.py:365
  61.0 0.0 collective-permute-done.1.rest_0_
  61.0 0.0 collective-permute-done.2.rest_1_
  61.0 0.5 early_products.1.early
  61.6 0.7 collective-permute-done.3.share
  62.3 0.6 cross_sums.1
  63.0 13.7 %all_to_all.17.parts = bf16[32,8,256]{2,1,0:T(8,128)(2,1)S(1)} all-to-all(bf16[32,8,256]{2,1,0:T(8,128)(2,1)S(1)} %cross_sums.1), channel_id=1, replica_groups={{117,116,115,119,125,114,118,124,13,113,123,127,12,112,122,126,5,11,15,..., dimensions={0} | all-to-all | bytes 262144 | tf_op jit(solution)/shard_map/all_to_all | solution.py:569
  76.7 0.7 finish.1
Async XLA Ops:
  7.4 6.1 %collective-permute-start = (f32[8,128,128]{2,1,0:T(8,128)S(1)}, f32[8,128,128]{2,1,0:T(8,128)S(1)}, u32[]{:S(2)}, u32[]{:S(2)}) collective-permute-start(f32[8,128,128]{2,1,0:T(8,128)S(1)} %get-tuple-element.16), channel_id=1, source_target_pairs={{0,1},{1,0},{2,3},{3,2},{4,5},{5,4},{6,7},{7,6},{8,9},{9,8},{10,11... | collective-permute-start | bytes 1572872 | tf_op jit(solution)/shard_map/ppermute | solution.py:519
  38.1 23.0 %collective-permute-start.1 = (bf16[16,16,512]{2,1,0:T(8,128)(2,1)S(1)}, bf16[16,16,512]{2,1,0:T(8,128)(2,1)S(1)}, u32[]{:S(2)}, u32[]{:S(2)}) collective-permute-start(bf16[16,16,512]{2,1,0:T(8,128)(2,1)S(1)} %modes_part.3.more_0_), channel_id=1, source_target_pairs={{0,112},{16,96},{32,80},{48,64},{64,48},{80,32},{96,16},{112,0},{1... | collective-permute-start | bytes 786440 | tf_op jit(solution)/shard_map/ppermute | solution.py:557
  45.8 6.3 %copy-start = (f32[3072]{0:T(1024)S(1)}, f32[3072]{0:T(1024)}, u32[]{:S(2)}) copy-start(f32[3072]{0:T(1024)} %param.5) | copy-start | bytes 36868
  45.8 15.2 %collective-permute-start.2 = (bf16[16,16,640]{2,1,0:T(8,128)(2,1)S(1)}, bf16[16,16,640]{2,1,0:T(8,128)(2,1)S(1)}, u32[]{:S(2)}, u32[]{:S(2)}) collective-permute-start(bf16[16,16,640]{2,1,0:T(8,128)(2,1)S(1)} %modes_part.4.more_0_), channel_id=1, source_target_pairs={{0,112},{16,96},{32,80},{48,64},{64,48},{80,32},{96,16},{112,0},{1... | collective-permute-start | bytes 983048 | tf_op jit(solution)/shard_map/ppermute | solution.py:557
  46.8 15.5 %collective-permute-start.3 = (bf16[17,16,384]{2,1,0:T(8,128)(2,1)S(1)}, bf16[17,16,384]{2,1,0:T(8,128)(2,1)S(1)}, u32[]{:S(2)}, u32[]{:S(2)}) collective-permute-start(bf16[17,16,384]{2,1,0:T(8,128)(2,1)S(1)} %modes_part.5.after), channel_id=1, source_target_pairs={{0,112},{16,96},{32,80},{48,64},{64,48},{80,32},{96,16},{112,0},{1... | collective-permute-start | bytes 626696 | tf_op jit(solution)/shard_map/ppermute | solution.py:557
